TPU v7x, 8 devices: a whole 2x2x1 slice. The times are simulated.
8 devices in a mesh: task: 1 (over z), row: 8 (over y, x, core).
Axes of the slice: x: 2, y: 2, z: 1, core: 2. Of those that a mesh axis runs over, the one named last changes fastest.
Arguments:
- points: bfloat16 [24576, 768], P(('task', 'row'))
- vectors: bfloat16 [24576, 32], P(('task', 'row'))
- length_scale: float32 [1], P('task')
- out_scale: float32 [1], P('task')
Outputs:
- output: float32 [24576, 32], P(('task', 'row'))
All inputs are finite; a program needn't handle non-finite values.
Results may differ from a plain program's by a relative error of at most 0.001.
Values are sent between devices in bfloat16 or wider.
A program may use at most 1 GiB of HBM per device.

v0:
```python
import jax
import jax.numpy as jnp
from jax import lax
from jax.sharding import PartitionSpec as P


def solution(mesh):
    n_row = mesh.shape["row"]
    shift_pairs = [(source_idx, (source_idx + 1) % n_row) for source_idx in range(n_row)]

    def kernel_product(x_rows, norm_rows, x_cols, norm_cols, v_cols, length_scale, out_scale):
        gram_mat = jnp.einsum("if,jf->ij", x_rows, x_cols, preferred_element_type=jnp.float32)
        sq_dist = jnp.maximum(norm_rows[:, None] + norm_cols[None, :] - 2.0 * gram_mat, 0.0)
        kern_tile = (out_scale * jnp.exp(-sq_dist / (2.0 * length_scale * length_scale))).astype(jnp.bfloat16)
        return jnp.dot(kern_tile, v_cols, preferred_element_type=jnp.float32)

    def kernel_pass(x_loc, norm_loc, v_loc, length_scale, out_scale):
        own_part = kernel_product(x_loc, norm_loc, x_loc, norm_loc, v_loc, length_scale, out_scale)

        def visit_step(step_idx, loop_state):
            x_vis, v_vis, running = loop_state
            x_vis = lax.ppermute(x_vis, "row", shift_pairs)
            v_vis = lax.ppermute(v_vis, "row", shift_pairs)
            norm_vis = jnp.sum(jnp.square(x_vis.astype(jnp.float32)), axis=1)
            running = running + kernel_product(x_loc, norm_loc, x_vis, norm_vis, v_vis, length_scale, out_scale)
            return x_vis, v_vis, running

        final_state = lax.fori_loop(1, n_row, visit_step, (x_loc, v_loc, own_part))
        return final_state[2]

    def local_program(x_loc, v_loc, length_scale, out_scale):
        norm_loc = jnp.sum(jnp.square(x_loc.astype(jnp.float32)), axis=1)
        first_pass = kernel_pass(x_loc, norm_loc, v_loc, length_scale, out_scale).astype(jnp.bfloat16)
        return kernel_pass(x_loc, norm_loc, first_pass, length_scale, out_scale)

    row_spec = P(("task", "row"), None)
    return jax.shard_map(local_program, mesh=mesh, in_specs=(row_spec, row_spec, P("task"), P("task")), out_specs=row_spec, check_vma=False)
```

profile of v0, /device:TPU:0, one launch (start us, length us, event | category | flops | bytes accessed | tf_op | source)
XLA Modules:
  0.0 1354.0 jit_solution(5190728025163439460)
XLA Ops:
  5.6 25.7 %multiply_convert_fusion.2 = bf16[3072,3072]{1,0:T(8,128)(2,1)} fusion(bf16[3072,768]{1,0:T(8,128)(2,1)} %param.8, f32[]{:T(128)} %bitcast.5, f32[3072]{0:T(1024)S(1)} %multiply_reduce_fusion.2, f32[]{:T(128)} %bitcast.38), kind=kOutput, calls=%fused_computation.12 | convolution fusion | flops 14571012096 | bytes 23605256 | tf_op jit(solution)/shard_map/if,jf->ij/dot_general | solution.py:12
  31.3 9.4 fusion.8
  40.7 4.9 copy.7
  45.6 648.5 %while.32 = (s32[]{:T(128)}, bf16[3072,768]{1,0:T(8,128)(2,1)}, bf16[3072,32]{0,1:T(8,128)(2,1)S(1)}, f32[3072,32]{0,1:T(8,128)S(1)}, f32[1]{0:T(128)}, /*index=...) while((s32[]{:T(128)}, bf16[3072,768]{1,0:T(8,128)(2,1)}, ...), condition=%wide.region_3.0_spmd, body=%wide.region_1.0_spmd.sunk | while | flops 15182164992 | bytes 44667060 | solution.py:28
  49.1 54.2 %collective-permute-done.1 = bf16[3072,32]{0,1:T(8,128)(2,1)S(1)} collective-permute-done((bf16[3072,32]{0,1:T(8,128)(2,1)S(1)}, bf16[3072,32]{0,1:T(8,128)(2,1)S(1)}, u32[]{:S(2)}, u32[]{:S(2)}) %collective-permute-start.1) | collective-permute-done | bytes 196640 | tf_op jit(solution)/shard_map/while/body/eval_jaxpr/ppermute | solution.py:23
  106.6 4.9 copy.15
  111.5 27.6 %fusion.33 = f32[3072,32]{0,1:T(8,128)S(1)} fusion(f32[3072,32]{0,1:T(8,128)S(1)} %get-tuple-element.339, bf16[3072,32]{0,1:T(8,128)(2,1)S(1)} %collective-permute-done.1, bf16[3072,768]{1,0:T(8,128)(2,1)} %get-tuple-element.351, bf16[3072,768]{1,0:T(8,128)(2,1)} %collective-permute-done, f32[]{:T(128)} %bitcast.31, ...), kind=kOutput, calls=%fused_computation.3.clone.1 | convolution fusion | flops 15175090176 | bytes 10444808 | tf_op jit(solution)/shard_map/while/body/eval_jaxpr/dot_general | solution.py:15
  140.7 55.1 %collective-permute-done.1 = bf16[3072,32]{0,1:T(8,128)(2,1)S(1)} collective-permute-done((bf16[3072,32]{0,1:T(8,128)(2,1)S(1)}, bf16[3072,32]{0,1:T(8,128)(2,1)S(1)}, u32[]{:S(2)}, u32[]{:S(2)}) %collective-permute-start.1) | collective-permute-done | bytes 196640 | tf_op jit(solution)/shard_map/while/body/eval_jaxpr/ppermute | solution.py:23
  199.1 4.9 copy.15
  204.0 27.6 %fusion.33 = f32[3072,32]{0,1:T(8,128)S(1)} fusion(f32[3072,32]{0,1:T(8,128)S(1)} %get-tuple-element.339, bf16[3072,32]{0,1:T(8,128)(2,1)S(1)} %collective-permute-done.1, bf16[3072,768]{1,0:T(8,128)(2,1)} %get-tuple-element.351, bf16[3072,768]{1,0:T(8,128)(2,1)} %collective-permute-done, f32[]{:T(128)} %bitcast.31, ...), kind=kOutput, calls=%fused_computation.3.clone.1 | convolution fusion | flops 15175090176 | bytes 10444808 | tf_op jit(solution)/shard_map/while/body/eval_jaxpr/dot_general | solution.py:15
  232.3 56.0 %collective-permute-done.1 = bf16[3072,32]{0,1:T(8,128)(2,1)S(1)} collective-permute-done((bf16[3072,32]{0,1:T(8,128)(2,1)S(1)}, bf16[3072,32]{0,1:T(8,128)(2,1)S(1)}, u32[]{:S(2)}, u32[]{:S(2)}) %collective-permute-start.1) | collective-permute-done | bytes 196640 | tf_op jit(solution)/shard_map/while/body/eval_jaxpr/ppermute | solution.py:23
  291.6 4.9 copy.15
  296.5 27.6 %fusion.33 = f32[3072,32]{0,1:T(8,128)S(1)} fusion(f32[3072,32]{0,1:T(8,128)S(1)} %get-tuple-element.339, bf16[3072,32]{0,1:T(8,128)(2,1)S(1)} %collective-permute-done.1, bf16[3072,768]{1,0:T(8,128)(2,1)} %get-tuple-element.351, bf16[3072,768]{1,0:T(8,128)(2,1)} %collective-permute-done, f32[]{:T(128)} %bitcast.31, ...), kind=kOutput, calls=%fused_computation.3.clone.1 | convolution fusion | flops 15175090176 | bytes 10444808 | tf_op jit(solution)/shard_map/while/body/eval_jaxpr/dot_general | solution.py:15
  324.3 56.5 %collective-permute-done.1 = bf16[3072,32]{0,1:T(8,128)(2,1)S(1)} collective-permute-done((bf16[3072,32]{0,1:T(8,128)(2,1)S(1)}, bf16[3072,32]{0,1:T(8,128)(2,1)S(1)}, u32[]{:S(2)}, u32[]{:S(2)}) %collective-permute-start.1) | collective-permute-done | bytes 196640 | tf_op jit(solution)/shard_map/while/body/eval_jaxpr/ppermute | solution.py:23
  384.1 4.9 copy.15
  389.0 27.6 %fusion.33 = f32[3072,32]{0,1:T(8,128)S(1)} fusion(f32[3072,32]{0,1:T(8,128)S(1)} %get-tuple-element.339, bf16[3072,32]{0,1:T(8,128)(2,1)S(1)} %collective-permute-done.1, bf16[3072,768]{1,0:T(8,128)(2,1)} %get-tuple-element.351, bf16[3072,768]{1,0:T(8,128)(2,1)} %collective-permute-done, f32[]{:T(128)} %bitcast.31, ...), kind=kOutput, calls=%fused_computation.3.clone.1 | convolution fusion | flops 15175090176 | bytes 10444808 | tf_op jit(solution)/shard_map/while/body/eval_jaxpr/dot_general | solution.py:15
  416.8 56.5 %collective-permute-done.1 = bf16[3072,32]{0,1:T(8,128)(2,1)S(1)} collective-permute-done((bf16[3072,32]{0,1:T(8,128)(2,1)S(1)}, bf16[3072,32]{0,1:T(8,128)(2,1)S(1)}, u32[]{:S(2)}, u32[]{:S(2)}) %collective-permute-start.1) | collective-permute-done | bytes 196640 | tf_op jit(solution)/shard_map/while/body/eval_jaxpr/ppermute | solution.py:23
  476.6 4.9 copy.15
  481.5 27.6 %fusion.33 = f32[3072,32]{0,1:T(8,128)S(1)} fusion(f32[3072,32]{0,1:T(8,128)S(1)} %get-tuple-element.339, bf16[3072,32]{0,1:T(8,128)(2,1)S(1)} %collective-permute-done.1, bf16[3072,768]{1,0:T(8,128)(2,1)} %get-tuple-element.351, bf16[3072,768]{1,0:T(8,128)(2,1)} %collective-permute-done, f32[]{:T(128)} %bitcast.31, ...), kind=kOutput, calls=%fused_computation.3.clone.1 | convolution fusion | flops 15175090176 | bytes 10444808 | tf_op jit(solution)/shard_map/while/body/eval_jaxpr/dot_general | solution.py:15
  509.3 56.5 %collective-permute-done.1 = bf16[3072,32]{0,1:T(8,128)(2,1)S(1)} collective-permute-done((bf16[3072,32]{0,1:T(8,128)(2,1)S(1)}, bf16[3072,32]{0,1:T(8,128)(2,1)S(1)}, u32[]{:S(2)}, u32[]{:S(2)}) %collective-permute-start.1) | collective-permute-done | bytes 196640 | tf_op jit(solution)/shard_map/while/body/eval_jaxpr/ppermute | solution.py:23
  569.1 4.9 copy.15
  574.0 27.6 %fusion.33 = f32[3072,32]{0,1:T(8,128)S(1)} fusion(f32[3072,32]{0,1:T(8,128)S(1)} %get-tuple-element.339, bf16[3072,32]{0,1:T(8,128)(2,1)S(1)} %collective-permute-done.1, bf16[3072,768]{1,0:T(8,128)(2,1)} %get-tuple-element.351, bf16[3072,768]{1,0:T(8,128)(2,1)} %collective-permute-done, f32[]{:T(128)} %bitcast.31, ...), kind=kOutput, calls=%fused_computation.3.clone.1 | convolution fusion | flops 15175090176 | bytes 10444808 | tf_op jit(solution)/shard_map/while/body/eval_jaxpr/dot_general | solution.py:15
  601.8 56.5 %collective-permute-done.1 = bf16[3072,32]{0,1:T(8,128)(2,1)S(1)} collective-permute-done((bf16[3072,32]{0,1:T(8,128)(2,1)S(1)}, bf16[3072,32]{0,1:T(8,128)(2,1)S(1)}, u32[]{:S(2)}, u32[]{:S(2)}) %collective-permute-start.1) | collective-permute-done | bytes 196640 | tf_op jit(solution)/shard_map/while/body/eval_jaxpr/ppermute | solution.py:23
  661.6 4.9 copy.15
  666.5 27.6 %fusion.33 = f32[3072,32]{0,1:T(8,128)S(1)} fusion(f32[3072,32]{0,1:T(8,128)S(1)} %get-tuple-element.339, bf16[3072,32]{0,1:T(8,128)(2,1)S(1)} %collective-permute-done.1, bf16[3072,768]{1,0:T(8,128)(2,1)} %get-tuple-element.351, bf16[3072,768]{1,0:T(8,128)(2,1)} %collective-permute-done, f32[]{:T(128)} %bitcast.31, ...), kind=kOutput, calls=%fused_computation.3.clone.1 | convolution fusion | flops 15175090176 | bytes 10444808 | tf_op jit(solution)/shard_map/while/body/eval_jaxpr/dot_general | solution.py:15
  694.2 9.8 fusion.9
  706.3 647.0 %while.33 = (s32[]{:T(128)}, bf16[3072,768]{1,0:T(8,128)(2,1)}, bf16[3072,32]{0,1:T(8,128)(2,1)S(1)}, f32[3072,32]{0,1:T(8,128)S(1)}, f32[1]{0:T(128)}, /*index=...) while((s32[]{:T(128)}, bf16[3072,768]{1,0:T(8,128)(2,1)}, ...), condition=%wide.region_6.0_spmd, body=%wide.region_4.0_spmd.sunk | while | flops 15182164992 | bytes 44667060 | solution.py:28
  706.3 56.5 %collective-permute-done.3 = bf16[3072,32]{0,1:T(8,128)(2,1)S(1)} collective-permute-done((bf16[3072,32]{0,1:T(8,128)(2,1)S(1)}, bf16[3072,32]{0,1:T(8,128)(2,1)S(1)}, u32[]{:S(2)}, u32[]{:S(2)}) %collective-permute-start.3) | collective-permute-done | bytes 196640 | tf_op jit(solution)/shard_map/while/body/eval_jaxpr/ppermute | solution.py:23
  766.2 4.8 copy.27
  771.0 27.7 %fusion.37 = f32[3072,32]{0,1:T(8,128)S(1)} fusion(f32[3072,32]{0,1:T(8,128)S(1)} %get-tuple-element.366, bf16[3072,32]{0,1:T(8,128)(2,1)S(1)} %collective-permute-done.3, bf16[3072,768]{1,0:T(8,128)(2,1)} %get-tuple-element.378, bf16[3072,768]{1,0:T(8,128)(2,1)} %collective-permute-done.2, f32[]{:T(128)} %bitcast.36, ...), kind=kOutput, calls=%fused_computation.9.clone.1 | convolution fusion | flops 15175090176 | bytes 10444808 | tf_op jit(solution)/shard_map/while/body/eval_jaxpr/dot_general | solution.py:15
  798.8 56.5 %collective-permute-done.3 = bf16[3072,32]{0,1:T(8,128)(2,1)S(1)} collective-permute-done((bf16[3072,32]{0,1:T(8,128)(2,1)S(1)}, bf16[3072,32]{0,1:T(8,128)(2,1)S(1)}, u32[]{:S(2)}, u32[]{:S(2)}) %collective-permute-start.3) | collective-permute-done | bytes 196640 | tf_op jit(solution)/shard_map/while/body/eval_jaxpr/ppermute | solution.py:23
  858.6 4.8 copy.27
  863.4 27.7 %fusion.37 = f32[3072,32]{0,1:T(8,128)S(1)} fusion(f32[3072,32]{0,1:T(8,128)S(1)} %get-tuple-element.366, bf16[3072,32]{0,1:T(8,128)(2,1)S(1)} %collective-permute-done.3, bf16[3072,768]{1,0:T(8,128)(2,1)} %get-tuple-element.378, bf16[3072,768]{1,0:T(8,128)(2,1)} %collective-permute-done.2, f32[]{:T(128)} %bitcast.36, ...), kind=kOutput, calls=%fused_computation.9.clone.1 | convolution fusion | flops 15175090176 | bytes 10444808 | tf_op jit(solution)/shard_map/while/body/eval_jaxpr/dot_general | solution.py:15
  891.2 56.5 %collective-permute-done.3 = bf16[3072,32]{0,1:T(8,128)(2,1)S(1)} collective-permute-done((bf16[3072,32]{0,1:T(8,128)(2,1)S(1)}, bf16[3072,32]{0,1:T(8,128)(2,1)S(1)}, u32[]{:S(2)}, u32[]{:S(2)}) %collective-permute-start.3) | collective-permute-done | bytes 196640 | tf_op jit(solution)/shard_map/while/body/eval_jaxpr/ppermute | solution.py:23
  951.0 4.8 copy.27
  955.9 27.7 %fusion.37 = f32[3072,32]{0,1:T(8,128)S(1)} fusion(f32[3072,32]{0,1:T(8,128)S(1)} %get-tuple-element.366, bf16[3072,32]{0,1:T(8,128)(2,1)S(1)} %collective-permute-done.3, bf16[3072,768]{1,0:T(8,128)(2,1)} %get-tuple-element.378, bf16[3072,768]{1,0:T(8,128)(2,1)} %collective-permute-done.2, f32[]{:T(128)} %bitcast.36, ...), kind=kOutput, calls=%fused_computation.9.clone.1 | convolution fusion | flops 15175090176 | bytes 10444808 | tf_op jit(solution)/shard_map/while/body/eval_jaxpr/dot_general | solution.py:15
  983.6 56.5 %collective-permute-done.3 = bf16[3072,32]{0,1:T(8,128)(2,1)S(1)} collective-permute-done((bf16[3072,32]{0,1:T(8,128)(2,1)S(1)}, bf16[3072,32]{0,1:T(8,128)(2,1)S(1)}, u32[]{:S(2)}, u32[]{:S(2)}) %collective-permute-start.3) | collective-permute-done | bytes 196640 | tf_op jit(solution)/shard_map/while/body/eval_jaxpr/ppermute | solution.py:23
  1043.5 4.8 copy.27
  1048.3 27.7 %fusion.37 = f32[3072,32]{0,1:T(8,128)S(1)} fusion(f32[3072,32]{0,1:T(8,128)S(1)} %get-tuple-element.366, bf16[3072,32]{0,1:T(8,128)(2,1)S(1)} %collective-permute-done.3, bf16[3072,768]{1,0:T(8,128)(2,1)} %get-tuple-element.378, bf16[3072,768]{1,0:T(8,128)(2,1)} %collective-permute-done.2, f32[]{:T(128)} %bitcast.36, ...), kind=kOutput, calls=%fused_computation.9.clone.1 | convolution fusion | flops 15175090176 | bytes 10444808 | tf_op jit(solution)/shard_map/while/body/eval_jaxpr/dot_general | solution.py:15
  1076.0 56.5 %collective-permute-done.3 = bf16[3072,32]{0,1:T(8,128)(2,1)S(1)} collective-permute-done((bf16[3072,32]{0,1:T(8,128)(2,1)S(1)}, bf16[3072,32]{0,1:T(8,128)(2,1)S(1)}, u32[]{:S(2)}, u32[]{:S(2)}) %collective-permute-start.3) | collective-permute-done | bytes 196640 | tf_op jit(solution)/shard_map/while/body/eval_jaxpr/ppermute | solution.py:23
  1135.9 4.8 copy.27
  1140.7 27.7 %fusion.37 = f32[3072,32]{0,1:T(8,128)S(1)} fusion(f32[3072,32]{0,1:T(8,128)S(1)} %get-tuple-element.366, bf16[3072,32]{0,1:T(8,128)(2,1)S(1)} %collective-permute-done.3, bf16[3072,768]{1,0:T(8,128)(2,1)} %get-tuple-element.378, bf16[3072,768]{1,0:T(8,128)(2,1)} %collective-permute-done.2, f32[]{:T(128)} %bitcast.36, ...), kind=kOutput, calls=%fused_computation.9.clone.1 | convolution fusion | flops 15175090176 | bytes 10444808 | tf_op jit(solution)/shard_map/while/body/eval_jaxpr/dot_general | solution.py:15
  1168.5 56.5 %collective-permute-done.3 = bf16[3072,32]{0,1:T(8,128)(2,1)S(1)} collective-permute-done((bf16[3072,32]{0,1:T(8,128)(2,1)S(1)}, bf16[3072,32]{0,1:T(8,128)(2,1)S(1)}, u32[]{:S(2)}, u32[]{:S(2)}) %collective-permute-start.3) | collective-permute-done | bytes 196640 | tf_op jit(solution)/shard_map/while/body/eval_jaxpr/ppermute | solution.py:23
  1228.3 4.8 copy.27
  1233.2 27.7 %fusion.37 = f32[3072,32]{0,1:T(8,128)S(1)} fusion(f32[3072,32]{0,1:T(8,128)S(1)} %get-tuple-element.366, bf16[3072,32]{0,1:T(8,128)(2,1)S(1)} %collective-permute-done.3, bf16[3072,768]{1,0:T(8,128)(2,1)} %get-tuple-element.378, bf16[3072,768]{1,0:T(8,128)(2,1)} %collective-permute-done.2, f32[]{:T(128)} %bitcast.36, ...), kind=kOutput, calls=%fused_computation.9.clone.1 | convolution fusion | flops 15175090176 | bytes 10444808 | tf_op jit(solution)/shard_map/while/body/eval_jaxpr/dot_general | solution.py:15
  1260.9 56.5 %collective-permute-done.3 = bf16[3072,32]{0,1:T(8,128)(2,1)S(1)} collective-permute-done((bf16[3072,32]{0,1:T(8,128)(2,1)S(1)}, bf16[3072,32]{0,1:T(8,128)(2,1)S(1)}, u32[]{:S(2)}, u32[]{:S(2)}) %collective-permute-start.3) | collective-permute-done | bytes 196640 | tf_op jit(solution)/shard_map/while/body/eval_jaxpr/ppermute | solution.py:23
  1320.8 4.8 copy.27
  1325.6 27.7 %fusion.37 = f32[3072,32]{0,1:T(8,128)S(1)} fusion(f32[3072,32]{0,1:T(8,128)S(1)} %get-tuple-element.366, bf16[3072,32]{0,1:T(8,128)(2,1)S(1)} %collective-permute-done.3, bf16[3072,768]{1,0:T(8,128)(2,1)} %get-tuple-element.378, bf16[3072,768]{1,0:T(8,128)(2,1)} %collective-permute-done.2, f32[]{:T(128)} %bitcast.36, ...), kind=kOutput, calls=%fused_computation.9.clone.1 | convolution fusion | flops 15175090176 | bytes 10444808 | tf_op jit(solution)/shard_map/while/body/eval_jaxpr/dot_general | solution.py:15
  (81 shorter events, 60.2 us)
Async XLA Ops:
  45.6 57.7 %collective-permute-start = (bf16[3072,768]{1,0:T(8,128)(2,1)}, bf16[3072,768]{1,0:T(8,128)(2,1)}, u32[]{:S(2)}, u32[]{:S(2)}) collective-permute-start(bf16[3072,768]{1,0:T(8,128)(2,1)} %get-tuple-element.337), channel_id=1, source_target_pairs={{0,1},{1,2},{2,3},{3,4},{4,5},{5,6},{6,7},{7,0}} | collective-permute-start | bytes 14155784 | tf_op jit(solution)/shard_map/while/body/eval_jaxpr/ppermute | solution.py:22
  46.5 56.8 %collective-permute-start.1 = (bf16[3072,32]{0,1:T(8,128)(2,1)S(1)}, bf16[3072,32]{0,1:T(8,128)(2,1)S(1)}, u32[]{:S(2)}, u32[]{:S(2)}) collective-permute-start(bf16[3072,32]{0,1:T(8,128)(2,1)S(1)} %get-tuple-element.338), channel_id=1, source_target_pairs={{0,1},{1,2},{2,3},{3,4},{4,5},{5,6},{6,7},{7,0}} | collective-permute-start | bytes 589832 | tf_op jit(solution)/shard_map/while/body/eval_jaxpr/ppermute | solution.py:23
  139.2 56.6 %collective-permute-start = (bf16[3072,768]{1,0:T(8,128)(2,1)}, bf16[3072,768]{1,0:T(8,128)(2,1)}, u32[]{:S(2)}, u32[]{:S(2)}) collective-permute-start(bf16[3072,768]{1,0:T(8,128)(2,1)} %get-tuple-element.337), channel_id=1, source_target_pairs={{0,1},{1,2},{2,3},{3,4},{4,5},{5,6},{6,7},{7,0}} | collective-permute-start | bytes 14155784 | tf_op jit(solution)/shard_map/while/body/eval_jaxpr/ppermute | solution.py:22
  139.2 56.5 %collective-permute-start.1 = (bf16[3072,32]{0,1:T(8,128)(2,1)S(1)}, bf16[3072,32]{0,1:T(8,128)(2,1)S(1)}, u32[]{:S(2)}, u32[]{:S(2)}) collective-permute-start(bf16[3072,32]{0,1:T(8,128)(2,1)S(1)} %get-tuple-element.338), channel_id=1, source_target_pairs={{0,1},{1,2},{2,3},{3,4},{4,5},{5,6},{6,7},{7,0}} | collective-permute-start | bytes 589832 | tf_op jit(solution)/shard_map/while/body/eval_jaxpr/ppermute | solution.py:23
  231.7 56.6 %collective-permute-start = (bf16[3072,768]{1,0:T(8,128)(2,1)}, bf16[3072,768]{1,0:T(8,128)(2,1)}, u32[]{:S(2)}, u32[]{:S(2)}) collective-permute-start(bf16[3072,768]{1,0:T(8,128)(2,1)} %get-tuple-element.337), channel_id=1, source_target_pairs={{0,1},{1,2},{2,3},{3,4},{4,5},{5,6},{6,7},{7,0}} | collective-permute-start | bytes 14155784 | tf_op jit(solution)/shard_map/while/body/eval_jaxpr/ppermute | solution.py:22
  231.7 56.5 %collective-permute-start.1 = (bf16[3072,32]{0,1:T(8,128)(2,1)S(1)}, bf16[3072,32]{0,1:T(8,128)(2,1)S(1)}, u32[]{:S(2)}, u32[]{:S(2)}) collective-permute-start(bf16[3072,32]{0,1:T(8,128)(2,1)S(1)} %get-tuple-element.338), channel_id=1, source_target_pairs={{0,1},{1,2},{2,3},{3,4},{4,5},{5,6},{6,7},{7,0}} | collective-permute-start | bytes 589832 | tf_op jit(solution)/shard_map/while/body/eval_jaxpr/ppermute | solution.py:23
  324.2 56.6 %collective-permute-start = (bf16[3072,768]{1,0:T(8,128)(2,1)}, bf16[3072,768]{1,0:T(8,128)(2,1)}, u32[]{:S(2)}, u32[]{:S(2)}) collective-permute-start(bf16[3072,768]{1,0:T(8,128)(2,1)} %get-tuple-element.337), channel_id=1, source_target_pairs={{0,1},{1,2},{2,3},{3,4},{4,5},{5,6},{6,7},{7,0}} | collective-permute-start | bytes 14155784 | tf_op jit(solution)/shard_map/while/body/eval_jaxpr/ppermute | solution.py:22
  324.2 56.5 %collective-permute-start.1 = (bf16[3072,32]{0,1:T(8,128)(2,1)S(1)}, bf16[3072,32]{0,1:T(8,128)(2,1)S(1)}, u32[]{:S(2)}, u32[]{:S(2)}) collective-permute-start(bf16[3072,32]{0,1:T(8,128)(2,1)S(1)} %get-tuple-element.338), channel_id=1, source_target_pairs={{0,1},{1,2},{2,3},{3,4},{4,5},{5,6},{6,7},{7,0}} | collective-permute-start | bytes 589832 | tf_op jit(solution)/shard_map/while/body/eval_jaxpr/ppermute | solution.py:23
  416.7 56.6 %collective-permute-start = (bf16[3072,768]{1,0:T(8,128)(2,1)}, bf16[3072,768]{1,0:T(8,128)(2,1)}, u32[]{:S(2)}, u32[]{:S(2)}) collective-permute-start(bf16[3072,768]{1,0:T(8,128)(2,1)} %get-tuple-element.337), channel_id=1, source_target_pairs={{0,1},{1,2},{2,3},{3,4},{4,5},{5,6},{6,7},{7,0}} | collective-permute-start | bytes 14155784 | tf_op jit(solution)/shard_map/while/body/eval_jaxpr/ppermute | solution.py:22
  416.7 56.5 %collective-permute-start.1 = (bf16[3072,32]{0,1:T(8,128)(2,1)S(1)}, bf16[3072,32]{0,1:T(8,128)(2,1)S(1)}, u32[]{:S(2)}, u32[]{:S(2)}) collective-permute-start(bf16[3072,32]{0,1:T(8,128)(2,1)S(1)} %get-tuple-element.338), channel_id=1, source_target_pairs={{0,1},{1,2},{2,3},{3,4},{4,5},{5,6},{6,7},{7,0}} | collective-permute-start | bytes 589832 | tf_op jit(solution)/shard_map/while/body/eval_jaxpr/ppermute | solution.py:23
  509.2 56.6 %collective-permute-start = (bf16[3072,768]{1,0:T(8,128)(2,1)}, bf16[3072,768]{1,0:T(8,128)(2,1)}, u32[]{:S(2)}, u32[]{:S(2)}) collective-permute-start(bf16[3072,768]{1,0:T(8,128)(2,1)} %get-tuple-element.337), channel_id=1, source_target_pairs={{0,1},{1,2},{2,3},{3,4},{4,5},{5,6},{6,7},{7,0}} | collective-permute-start | bytes 14155784 | tf_op jit(solution)/shard_map/while/body/eval_jaxpr/ppermute | solution.py:22
  509.2 56.5 %collective-permute-start.1 = (bf16[3072,32]{0,1:T(8,128)(2,1)S(1)}, bf16[3072,32]{0,1:T(8,128)(2,1)S(1)}, u32[]{:S(2)}, u32[]{:S(2)}) collective-permute-start(bf16[3072,32]{0,1:T(8,128)(2,1)S(1)} %get-tuple-element.338), channel_id=1, source_target_pairs={{0,1},{1,2},{2,3},{3,4},{4,5},{5,6},{6,7},{7,0}} | collective-permute-start | bytes 589832 | tf_op jit(solution)/shard_map/while/body/eval_jaxpr/ppermute | solution.py:23
  601.7 56.6 %collective-permute-start = (bf16[3072,768]{1,0:T(8,128)(2,1)}, bf16[3072,768]{1,0:T(8,128)(2,1)}, u32[]{:S(2)}, u32[]{:S(2)}) collective-permute-start(bf16[3072,768]{1,0:T(8,128)(2,1)} %get-tuple-element.337), channel_id=1, source_target_pairs={{0,1},{1,2},{2,3},{3,4},{4,5},{5,6},{6,7},{7,0}} | collective-permute-start | bytes 14155784 | tf_op jit(solution)/shard_map/while/body/eval_jaxpr/ppermute | solution.py:22
  601.7 56.5 %collective-permute-start.1 = (bf16[3072,32]{0,1:T(8,128)(2,1)S(1)}, bf16[3072,32]{0,1:T(8,128)(2,1)S(1)}, u32[]{:S(2)}, u32[]{:S(2)}) collective-permute-start(bf16[3072,32]{0,1:T(8,128)(2,1)S(1)} %get-tuple-element.338), channel_id=1, source_target_pairs={{0,1},{1,2},{2,3},{3,4},{4,5},{5,6},{6,7},{7,0}} | collective-permute-start | bytes 589832 | tf_op jit(solution)/shard_map/while/body/eval_jaxpr/ppermute | solution.py:23
  694.2 9.9 slice-start
  694.2 9.8 slice-start.1
  706.3 56.6 %collective-permute-start.2 = (bf16[3072,768]{1,0:T(8,128)(2,1)}, bf16[3072,768]{1,0:T(8,128)(2,1)}, u32[]{:S(2)}, u32[]{:S(2)}) collective-permute-start(bf16[3072,768]{1,0:T(8,128)(2,1)} %get-tuple-element.364), channel_id=1, source_target_pairs={{0,1},{1,2},{2,3},{3,4},{4,5},{5,6},{6,7},{7,0}} | collective-permute-start | bytes 14155784 | tf_op jit(solution)/shard_map/while/body/eval_jaxpr/ppermute | solution.py:22
  706.3 56.6 %collective-permute-start.3 = (bf16[3072,32]{0,1:T(8,128)(2,1)S(1)}, bf16[3072,32]{0,1:T(8,128)(2,1)S(1)}, u32[]{:S(2)}, u32[]{:S(2)}) collective-permute-start(bf16[3072,32]{0,1:T(8,128)(2,1)S(1)} %get-tuple-element.365), channel_id=1, source_target_pairs={{0,1},{1,2},{2,3},{3,4},{4,5},{5,6},{6,7},{7,0}} | collective-permute-start | bytes 589832 | tf_op jit(solution)/shard_map/while/body/eval_jaxpr/ppermute | solution.py:23
  798.7 56.6 %collective-permute-start.2 = (bf16[3072,768]{1,0:T(8,128)(2,1)}, bf16[3072,768]{1,0:T(8,128)(2,1)}, u32[]{:S(2)}, u32[]{:S(2)}) collective-permute-start(bf16[3072,768]{1,0:T(8,128)(2,1)} %get-tuple-element.364), channel_id=1, source_target_pairs={{0,1},{1,2},{2,3},{3,4},{4,5},{5,6},{6,7},{7,0}} | collective-permute-start | bytes 14155784 | tf_op jit(solution)/shard_map/while/body/eval_jaxpr/ppermute | solution.py:22
  798.7 56.5 %collective-permute-start.3 = (bf16[3072,32]{0,1:T(8,128)(2,1)S(1)}, bf16[3072,32]{0,1:T(8,128)(2,1)S(1)}, u32[]{:S(2)}, u32[]{:S(2)}) collective-permute-start(bf16[3072,32]{0,1:T(8,128)(2,1)S(1)} %get-tuple-element.365), channel_id=1, source_target_pairs={{0,1},{1,2},{2,3},{3,4},{4,5},{5,6},{6,7},{7,0}} | collective-permute-start | bytes 589832 | tf_op jit(solution)/shard_map/while/body/eval_jaxpr/ppermute | solution.py:23
  891.1 56.6 %collective-permute-start.2 = (bf16[3072,768]{1,0:T(8,128)(2,1)}, bf16[3072,768]{1,0:T(8,128)(2,1)}, u32[]{:S(2)}, u32[]{:S(2)}) collective-permute-start(bf16[3072,768]{1,0:T(8,128)(2,1)} %get-tuple-element.364), channel_id=1, source_target_pairs={{0,1},{1,2},{2,3},{3,4},{4,5},{5,6},{6,7},{7,0}} | collective-permute-start | bytes 14155784 | tf_op jit(solution)/shard_map/while/body/eval_jaxpr/ppermute | solution.py:22
  891.1 56.5 %collective-permute-start.3 = (bf16[3072,32]{0,1:T(8,128)(2,1)S(1)}, bf16[3072,32]{0,1:T(8,128)(2,1)S(1)}, u32[]{:S(2)}, u32[]{:S(2)}) collective-permute-start(bf16[3072,32]{0,1:T(8,128)(2,1)S(1)} %get-tuple-element.365), channel_id=1, source_target_pairs={{0,1},{1,2},{2,3},{3,4},{4,5},{5,6},{6,7},{7,0}} | collective-permute-start | bytes 589832 | tf_op jit(solution)/shard_map/while/body/eval_jaxpr/ppermute | solution.py:23
  983.5 56.6 %collective-permute-start.2 = (bf16[3072,768]{1,0:T(8,128)(2,1)}, bf16[3072,768]{1,0:T(8,128)(2,1)}, u32[]{:S(2)}, u32[]{:S(2)}) collective-permute-start(bf16[3072,768]{1,0:T(8,128)(2,1)} %get-tuple-element.364), channel_id=1, source_target_pairs={{0,1},{1,2},{2,3},{3,4},{4,5},{5,6},{6,7},{7,0}} | collective-permute-start | bytes 14155784 | tf_op jit(solution)/shard_map/while/body/eval_jaxpr/ppermute | solution.py:22
  983.6 56.5 %collective-permute-start.3 = (bf16[3072,32]{0,1:T(8,128)(2,1)S(1)}, bf16[3072,32]{0,1:T(8,128)(2,1)S(1)}, u32[]{:S(2)}, u32[]{:S(2)}) collective-permute-start(bf16[3072,32]{0,1:T(8,128)(2,1)S(1)} %get-tuple-element.365), channel_id=1, source_target_pairs={{0,1},{1,2},{2,3},{3,4},{4,5},{5,6},{6,7},{7,0}} | collective-permute-start | bytes 589832 | tf_op jit(solution)/shard_map/while/body/eval_jaxpr/ppermute | solution.py:23
  1076.0 56.6 %collective-permute-start.2 = (bf16[3072,768]{1,0:T(8,128)(2,1)}, bf16[3072,768]{1,0:T(8,128)(2,1)}, u32[]{:S(2)}, u32[]{:S(2)}) collective-permute-start(bf16[3072,768]{1,0:T(8,128)(2,1)} %get-tuple-element.364), channel_id=1, source_target_pairs={{0,1},{1,2},{2,3},{3,4},{4,5},{5,6},{6,7},{7,0}} | collective-permute-start | bytes 14155784 | tf_op jit(solution)/shard_map/while/body/eval_jaxpr/ppermute | solution.py:22
  1076.0 56.5 %collective-permute-start.3 = (bf16[3072,32]{0,1:T(8,128)(2,1)S(1)}, bf16[3072,32]{0,1:T(8,128)(2,1)S(1)}, u32[]{:S(2)}, u32[]{:S(2)}) collective-permute-start(bf16[3072,32]{0,1:T(8,128)(2,1)S(1)} %get-tuple-element.365), channel_id=1, source_target_pairs={{0,1},{1,2},{2,3},{3,4},{4,5},{5,6},{6,7},{7,0}} | collective-permute-start | bytes 589832 | tf_op jit(solution)/shard_map/while/body/eval_jaxpr/ppermute | solution.py:23
  1168.4 56.6 %collective-permute-start.2 = (bf16[3072,768]{1,0:T(8,128)(2,1)}, bf16[3072,768]{1,0:T(8,128)(2,1)}, u32[]{:S(2)}, u32[]{:S(2)}) collective-permute-start(bf16[3072,768]{1,0:T(8,128)(2,1)} %get-tuple-element.364), channel_id=1, source_target_pairs={{0,1},{1,2},{2,3},{3,4},{4,5},{5,6},{6,7},{7,0}} | collective-permute-start | bytes 14155784 | tf_op jit(solution)/shard_map/while/body/eval_jaxpr/ppermute | solution.py:22
  1168.4 56.5 %collective-permute-start.3 = (bf16[3072,32]{0,1:T(8,128)(2,1)S(1)}, bf16[3072,32]{0,1:T(8,128)(2,1)S(1)}, u32[]{:S(2)}, u32[]{:S(2)}) collective-permute-start(bf16[3072,32]{0,1:T(8,128)(2,1)S(1)} %get-tuple-element.365), channel_id=1, source_target_pairs={{0,1},{1,2},{2,3},{3,4},{4,5},{5,6},{6,7},{7,0}} | collective-permute-start | bytes 589832 | tf_op jit(solution)/shard_map/while/body/eval_jaxpr/ppermute | solution.py:23
  1260.8 56.6 %collective-permute-start.2 = (bf16[3072,768]{1,0:T(8,128)(2,1)}, bf16[3072,768]{1,0:T(8,128)(2,1)}, u32[]{:S(2)}, u32[]{:S(2)}) collective-permute-start(bf16[3072,768]{1,0:T(8,128)(2,1)} %get-tuple-element.364), channel_id=1, source_target_pairs={{0,1},{1,2},{2,3},{3,4},{4,5},{5,6},{6,7},{7,0}} | collective-permute-start | bytes 14155784 | tf_op jit(solution)/shard_map/while/body/eval_jaxpr/ppermute | solution.py:22
  1260.9 56.5 %collective-permute-start.3 = (bf16[3072,32]{0,1:T(8,128)(2,1)S(1)}, bf16[3072,32]{0,1:T(8,128)(2,1)S(1)}, u32[]{:S(2)}, u32[]{:S(2)}) collective-permute-start(bf16[3072,32]{0,1:T(8,128)(2,1)S(1)} %get-tuple-element.365), channel_id=1, source_target_pairs={{0,1},{1,2},{2,3},{3,4},{4,5},{5,6},{6,7},{7,0}} | collective-permute-start | bytes 589832 | tf_op jit(solution)/shard_map/while/body/eval_jaxpr/ppermute | solution.py:23
  1353.3 0.7 copy-start
where the time goes:
time: 1360 us; the launch traced here: 1350 us
  waiting for transfers between devices  787 us (58%)
  matrix products  432 us (32%)
  local copies, waits for them, and re-layouts  76.8 us (6%)
  other arithmetic  50 us (4%)
    ppermute x14, waiting for transfers between devices, visit_step(): v_vis = lax.ppermute(v_vis, 'row', shift_pairs)  787 us
    dot_general x16, matrix products, kernel_product(): return jnp.dot(kern_tile, v_cols, preferred_element_type=jnp.float32)  406 us
    while x28, local copies, waits for them, and re-layouts  68.1 us
    reduce_sum x14, other arithmetic, visit_step(): norm_vis = jnp.sum(jnp.square(x_vis.astype(jnp.float32)), axis=1)  46.6 us
  transfers between devices with their start and end apart: 28, of which 14 were waited for; matrix products, arithmetic and copies ran while one was open for 0% of the time, Pallas kernels for 0%

commit v1 on v0

v1 whole, which is shorter than its diff:
```python
import functools

import jax
import jax.numpy as jnp
from jax import lax
from jax.experimental import pallas as pl
from jax.experimental.pallas import tpu as pltpu
from jax.sharding import PartitionSpec as P

MESH = pl.DeviceIdType.MESH
F32, BF16 = jnp.float32, jnp.bfloat16
LOG2E = 1.4426950408889634

ROWS = 3072
STRIP = 256
CHUNK = 512
N_STRIP = ROWS // STRIP
N_CHUNK = ROWS // CHUNK
UNITS = 3
OWN, XNB, YNB, PAR, TRASH = 0, 1, 2, 3, 4

PRE = 7
FILL = (0, 4, 4, 2, 2, 0, 0, 4, 4, 2, 2, 0)
TILES = tuple(12 + 2 * (n // 2) + 2 * (n % 2) for n in range(N_STRIP))
STEPS = tuple((TILES[n] + FILL[n]) // 6 for n in range(N_STRIP))
N_STEP = PRE + sum(STEPS) + 2
TAIL0 = PRE + sum(STEPS[:11])
LEFT0 = TAIL0 + STEPS[11]


def table(values, n):
    out = jnp.int32(values[0])
    for i in range(1, len(values)):
        if values[i] != values[i - 1]:
            out = out + (values[i] - values[i - 1]) * (n >= i).astype(jnp.int32)
    return out


def cumulative(values):
    out = [0]
    for v in values:
        out.append(out[-1] + v)
    return tuple(out[:-1])


FILL_BASE = tuple(PRE * 6 + c for c in cumulative(FILL))
STEP_BASE = tuple(PRE + c for c in cumulative(STEPS))


def pick(cond, a, b):
    return tuple(jnp.where(cond, x, y) for x, y in zip(a, b))


def i32(*xs):
    return tuple(jnp.int32(x) for x in xs)


def own_tile(w, core):
    e = w - 24
    a = e // 3
    par = (jnp.int32(OWN), a, jnp.int32(PAR), 2 * (e % 3) + (a // 2 + core) % 2, jnp.int32(PAR))
    v = jnp.where(w < 24, w, w - 36)
    d, rem = v // 12, v % 12
    i = rem // 2
    own = (jnp.int32(OWN), 2 * i + rem % 2, jnp.int32(OWN), (i + d) % N_CHUNK, jnp.where(d == 0, TRASH, OWN))
    return pick(jnp.logical_and(w >= 24, w < 60), par, own)


def strip_tile(n, idx, core):
    m = n // 2
    t = (jnp.int32(XNB), n, jnp.int32(OWN), idx, jnp.int32(OWN))
    t = pick(idx < 6, t, (jnp.int32(YNB), n, jnp.int32(OWN), idx - 6, jnp.int32(OWN)))
    t = pick(idx < 12, t, (jnp.int32(XNB), n, jnp.int32(YNB), idx - 12, jnp.int32(YNB)))
    t = pick(idx < 12 + m, t, (jnp.int32(YNB), n, jnp.int32(XNB), idx - 12 - m, jnp.int32(XNB)))
    t = pick(idx < 12 + 2 * m, t, (jnp.int32(XNB), n - 1 + (idx - 12 - 2 * m), jnp.int32(YNB), m, jnp.int32(YNB)))
    end = 12 + 2 * m + 2 * (n % 2)
    w = table(FILL_BASE, n) + idx - end
    return pick(idx < end, t, own_tile(w, core))


def last_tile(idx):
    c = idx // 2
    n = jnp.int32(N_STRIP - 1)
    odd = idx % 2 == 1
    t = pick(odd, (jnp.int32(XNB), n, jnp.int32(YNB), c, jnp.int32(YNB)), (jnp.int32(YNB), n, jnp.int32(XNB), c, jnp.int32(XNB)))
    t = pick(idx < 10, t, (jnp.int32(XNB), idx, jnp.int32(YNB), jnp.int32(5), jnp.int32(YNB)))
    j = idx - 12
    return pick(idx < 12, t, (jnp.where(j < 6, XNB, YNB), n, jnp.int32(OWN), j % 6, jnp.int32(OWN)))


def step_tile(step, j, core):
    n = jnp.int32(0)
    for i in range(1, N_STRIP):
        n = n + (step >= STEP_BASE[i]).astype(jnp.int32)
    idx = (step - table(STEP_BASE, n)) * 6 + j
    t = pick(n < N_STRIP - 1, strip_tile(n, idx, core), last_tile(idx))
    w = jnp.where(step < PRE, step * 6, 66 + (step - LEFT0) * 6) + j
    return pick(jnp.logical_or(step < PRE, step >= LEFT0), own_tile(w, core), t)


def rows_of(a):
    return pl.ds(pl.multiple_of(a * STRIP, STRIP), STRIP)


def sums_of(c):
    return pl.ds(pl.multiple_of(STRIP + c * CHUNK, STRIP), CHUNK)


def cols_of(b):
    return pl.ds(pl.multiple_of(b * CHUNK, CHUNK), CHUNK)


def body(
    x_hbm, v_hbm, ell_ref, amp_ref, out_ref, k_hbm,
    X, V0, VT, YV, NA, NB, CR, YR, YT, SB, RB, SB2, RB2, kr0, kr1, KB,
    sx_sem, rx_sem, sv_sem, rv_sem, sn_sem, rn_sem, sp_sem, rp_sem, loc_sem, ko_sem, ki_sem,
    s1_sem, r1_sem, sy_sem, ry_sem, s2_sem, r2_sem,
):
    me = lax.axis_index("row")
    core, cx, cy = me % 2, (me // 2) % 2, me // 4

    def dev(px, py, pc):
        return {"row": (py * 2 + px) * 2 + pc}

    tx = dev(1 - cx, cy, (core + 1 + cx) % 2)
    ty = dev(cx, 1 - cy, (core + 1 + cx + cy) % 2)
    sx = dev(1 - cx, cy, (core + cx) % 2)
    sy = dev(cx, 1 - cy, (core + cx + cy) % 2)
    pt = dev(cx, cy, 1 - core)

    def remote(src, dst, ss, rs, to):
        return pltpu.make_async_remote_copy(src_ref=src, dst_ref=dst, send_sem=ss, recv_sem=rs, device_id=to, device_id_type=MESH)

    def x_copy(j, n):
        return remote(x_hbm.at[rows_of(n)], X.at[1 + j, rows_of(n)], sx_sem.at[j, n], rx_sem.at[j, n], (tx, ty)[j])

    p_copy = remote(x_hbm, X.at[PAR], sp_sem, rp_sem, pt)
    v_copies = [remote(VT.at[OWN], VT.at[1 + j], sv_sem.at[j], rv_sem.at[j], d) for j, d in enumerate((tx, ty, pt))]
    n_copies = [remote(NB.at[OWN], NB.at[1 + j], sn_sem.at[j], rn_sem.at[j], d) for j, d in enumerate((tx, ty, pt))]

    x_loc = pltpu.make_async_copy(x_hbm, X.at[OWN], loc_sem.at[0])
    v_loc = pltpu.make_async_copy(v_hbm, V0, loc_sem.at[1])
    v_loc.start()
    x_loc.start()

    barrier = pltpu.get_barrier_semaphore()
    for d in (tx, ty, sx, sy, pt):
        pl.semaphore_signal(barrier, inc=1, device_id=d, device_id_type=MESH)
    pl.semaphore_wait(barrier, 5)

    for j in range(2):
        x_copy(j, 0).start()
    p_copy.start()

    ell = jnp.full((1, CHUNK), ell_ref[0], F32)
    half = LOG2E / (2.0 * ell * ell)
    top = jnp.log2(jnp.full((1, CHUNK), amp_ref[0], F32))
    CR[0:1, :] = 2.0 * half
    CR[1:2, :] = top
    h1, l1 = half[:, 0:128], top[:, 0:128]

    for s in range(3):
        YR[s] = jnp.zeros((STRIP + ROWS, 32), F32)
    for t in range(5):
        YT[t] = jnp.zeros((32, ROWS), F32)
    kr0[...] = jnp.zeros_like(kr0)
    kr1[...] = jnp.zeros_like(kr1)

    eye = (lax.broadcasted_iota(jnp.int32, (32, 32), 0) == lax.broadcasted_iota(jnp.int32, (32, 32), 1)).astype(F32).astype(BF16)
    v_loc.wait()

    def turn(c, _):
        v = V0[pl.ds(pl.multiple_of(c * CHUNK, CHUNK), CHUNK), :]
        VT[OWN, :, cols_of(c)] = lax.dot_general(eye, v, (((1,), (1,)), ((), ())), preferred_element_type=F32).astype(BF16)
        return 0

    lax.fori_loop(0, N_CHUNK, turn, 0)
    x_loc.wait()

    def own_norm(c, _):
        r = pl.ds(pl.multiple_of(c * CHUNK, CHUNK), CHUNK)
        x = X[OWN, r, :].astype(F32)
        n = jnp.broadcast_to(jnp.sum(x * x, axis=1, keepdims=True), (CHUNK, 128)) * h1
        NA[OWN, r, :] = l1 - n
        NB[OWN, :, cols_of(c)] = -jnp.transpose(n)[0:1, :]
        return 0

    lax.fori_loop(0, N_CHUNK, own_norm, 0)
    for c in v_copies + n_copies:
        c.start()

    def send_strip(n, _):
        for j in range(2):
            x_copy(j, n).start()
        return 0

    lax.fori_loop(1, N_STRIP, send_strip, 0)

    def left_norm(s):
        def one(c, _):
            r = pl.ds(pl.multiple_of(c * CHUNK, CHUNK), CHUNK)
            NA[s, r, :] = l1 + jnp.transpose(jnp.broadcast_to(NB[s, :, cols_of(c)], (128, CHUNK)))
            return 0

        lax.fori_loop(0, N_CHUNK, one, 0)

    def gram(tile):
        s, a, t, b, _ = tile
        return lax.dot_general(X[s, rows_of(a), :], X[t, cols_of(b), :], (((1,), (1,)), ((), ())), preferred_element_type=F32)

    def kern(tile, g):
        s, a, t, b, _ = tile
        na = NA[s, rows_of(a), :]
        e = (g * CR[0:1, :] + NB[t, :, cols_of(b)]) + jnp.concatenate([na] * (CHUNK // 128), axis=1)
        return jnp.exp2(jnp.minimum(e, CR[1:2, :])).astype(BF16)

    def apply(tile, k, vec):
        s, a, t, b, to = tile
        YR[s, rows_of(a + 1), :] += lax.dot_general(k, vec[t, :, cols_of(b)], (((1,), (1,)), ((), ())), preferred_element_type=F32)
        YT[to, :, cols_of(b)] += jnp.dot(vec[s, :, rows_of(jnp.maximum(a, 0))], k, preferred_element_type=F32)

    def k_out(step, half):
        kr = (kr0, kr1)[half]
        return pltpu.make_async_copy(kr.at[step % 2], k_hbm.at[step, half], ko_sem.at[step % 2, half])

    def half_step(prev, cur, kr_new, d_new, kr_old, d_old):
        gs = [gram(t) for t in cur]
        for u in range(UNITS):
            apply(prev[u], kr_old[d_old, u], VT)
        for u in range(UNITS):
            kr_new[d_new, u] = kern(cur[u], gs[u])

    def flat(tiles):
        return tuple(x for t in tiles for x in t)

    def unflat(xs):
        return [tuple(xs[5 * u : 5 * u + 5]) for u in range(UNITS)]

    def step_of(step, prev):
        d = step % 2

        @pl.when(step >= 2)
        def _():
            for h in range(2):
                k_out(step - 2, h).wait()

        @pl.when(step >= 1)
        def _():
            for h in range(2):
                k_out(step - 1, h).start()

        first = [step_tile(step, u, core) for u in range(UNITS)]
        second = [step_tile(step, UNITS + u, core) for u in range(UNITS)]
        half_step(unflat(prev), first, kr0, d, kr1, 1 - d)
        half_step(first, second, kr1, d, kr0, d)
        return flat(second)

    none = flat([i32(OWN, -1, OWN, 0, TRASH)] * UNITS)

    def steps(lo, hi, prev):
        return lax.fori_loop(lo, hi, step_of, prev)

    def pre_step(step, prev):
        @pl.when(step == 4)
        def _():
            p_copy.wait_recv()
            v_copies[2].wait_recv()
            n_copies[2].wait_recv()

        return step_of(step, prev)

    prev = lax.fori_loop(0, PRE, pre_step, none)

    for j in range(2):
        v_copies[j].wait_recv()
        n_copies[j].wait_recv()
        left_norm(1 + j)

    def strip(n, prev):
        for j in range(2):
            x_copy(j, n).wait_recv()
        lo = table(STEP_BASE, n)
        return steps(lo, lo + table(STEPS, n), prev)

    prev = lax.fori_loop(0, N_STRIP - 1, strip, prev)

    for j in range(2):
        x_copy(j, N_STRIP - 1).wait_recv()

    def flush(step, prev):
        for u, t in enumerate(unflat(prev)):
            apply(t, kr1[step % 2, u], VT)

    homes = ((XNB, sx), (YNB, sy), (PAR, pt))

    def part_copy(j, c, send, recv, ss, rs):
        return remote(send.at[j, :, cols_of(c)], recv.at[j, :, cols_of(c)], ss.at[j, c], rs.at[j, c], homes[j][1])

    def finish(j, c, send):
        s = homes[j][0]
        part = YT[s, :, cols_of(c)]
        if j < 2:
            part = part + jnp.transpose(YR[s, sums_of(c), :])
            YR[s, sums_of(c), :] = jnp.zeros((CHUNK, 32), F32)
        send[j, :, cols_of(c)] = part
        YT[s, :, cols_of(c)] = jnp.zeros((32, CHUNK), F32)

    def finish_range(lo, hi, send, recv, ss, rs, js=(0, 1)):
        def one(c, _):
            for j in js:
                finish(j, c, send)
            return 0

        def go(c, _):
            for j in js:
                part_copy(j, c, send, recv, ss, rs).start()
            return 0

        lax.fori_loop(lo, hi, one, 0)
        lax.fori_loop(lo, hi, go, 0)

    def last_step(step, prev):
        prev = step_of(step, prev)
        flush(step, prev)
        i = step - TAIL0
        lo = table((0, 3, 5, 5), i)
        hi = table((3, 5, 5, 6), i)
        finish_range(lo, hi, SB, RB, s1_sem, r1_sem)
        return none

    prev = lax.fori_loop(TAIL0, LEFT0, last_step, prev)
    prev = steps(LEFT0, N_STEP, prev)
    flush(N_STEP - 1, prev)
    finish_range(0, N_CHUNK, SB, RB, s1_sem, r1_sem, (2,))
    for h in range(2):
        k_out(N_STEP - 2, h).wait()
        k_out(N_STEP - 1, h).start()
    for h in range(2):
        k_out(N_STEP - 1, h).wait()

    def order(i):
        return jnp.where(i < PRE, i, jnp.where(i < PRE + 2, LEFT0 + i - PRE, N_STEP - 1 + PRE - i))

    DEPTH = KB.shape[0]

    def k_in(i):
        return pltpu.make_async_copy(k_hbm.at[order(i)], KB.at[i % DEPTH], ki_sem.at[i % DEPTH])

    for i in range(DEPTH - 1):
        k_in(jnp.int32(i)).start()

    def y_copy(j, c):
        return remote(YV.at[OWN, :, cols_of(c)], YV.at[1 + j, :, cols_of(c)], sy_sem.at[j, c], ry_sem.at[j, c], (tx, ty, pt)[j])

    def middle(c, _):
        for j in range(3):
            part_copy(j, c, SB, RB, s1_sem, r1_sem).wait_recv()
        y = YT[OWN, :, cols_of(c)] + jnp.transpose(YR[OWN, sums_of(c), :])
        y = y + RB[0, :, cols_of(c)] + RB[1, :, cols_of(c)] + RB[2, :, cols_of(c)]
        YV[OWN, :, cols_of(c)] = y.astype(BF16)
        YT[OWN, :, cols_of(c)] = jnp.zeros((32, CHUNK), F32)
        YR[OWN, sums_of(c), :] = jnp.zeros((CHUNK, 32), F32)
        return 0

    def middle_go(c, _):
        for j in range(3):
            y_copy(j, c).start()
        return 0

    lax.fori_loop(0, N_CHUNK, middle, 0)
    lax.fori_loop(0, N_CHUNK, middle_go, 0)

    def second(i, _):
        step = order(i)
        k_in(i).wait()

        @pl.when(i + DEPTH - 1 < N_STEP)
        def _():
            k_in(i + DEPTH - 1).start()

        for j in range(6):
            apply(step_tile(step, j, core), KB[i % DEPTH, j // 3, j % 3], YV)
        return 0

    def wait_y(j):
        def one(c, _):
            y_copy(j, c).wait_recv()
            return 0

        lax.fori_loop(0, N_CHUNK, one, 0)

    lax.fori_loop(0, 4, second, 0)
    wait_y(2)
    lax.fori_loop(4, PRE + 2, second, 0)
    wait_y(0)
    wait_y(1)

    bounds = tuple(N_STEP + PRE - STEP_BASE[2 * c] for c in range(N_CHUNK))

    def second_chunk(k, lo):
        c = N_CHUNK - 1 - k
        hi = table(bounds, c)
        lax.fori_loop(lo, hi, second, 0)
        finish_range(c, c + 1, SB2, RB2, s2_sem, r2_sem, (0, 1))
        return hi

    lo = lax.fori_loop(0, N_CHUNK, second_chunk, jnp.int32(PRE + 2))
    finish_range(0, N_CHUNK, SB2, RB2, s2_sem, r2_sem, (2,))

    def final(k, _):
        c = N_CHUNK - 1 - k
        for j in range(3):
            part_copy(j, c, SB2, RB2, s2_sem, r2_sem).wait_recv()
        r = pl.ds(pl.multiple_of(c * CHUNK, CHUNK), CHUNK)
        w = YT[OWN, :, cols_of(c)] + RB2[0, :, cols_of(c)] + RB2[1, :, cols_of(c)] + RB2[2, :, cols_of(c)]
        out_ref[r, :] = YR[OWN, sums_of(c), :] + jnp.transpose(w)
        return 0

    lax.fori_loop(0, N_CHUNK, final, 0)

    p_copy.wait_send()
    for c in v_copies + n_copies:
        c.wait_send()

    def sent_x(n, _):
        for j in range(2):
            x_copy(j, n).wait_send()
        return 0

    lax.fori_loop(0, N_STRIP, sent_x, 0)

    def sent(c, _):
        for j in range(3):
            part_copy(j, c, SB, RB, s1_sem, r1_sem).wait_send()
            y_copy(j, c).wait_send()
            part_copy(j, c, SB2, RB2, s2_sem, r2_sem).wait_send()
        return 0

    lax.fori_loop(0, N_CHUNK, sent, 0)


def solution(mesh):
    def local_program(x_loc, v_loc, length_scale, out_scale):
        dma = pltpu.SemaphoreType.DMA
        hbm = pl.BlockSpec(memory_space=pltpu.HBM)
        smem = pl.BlockSpec(memory_space=pltpu.SMEM)
        w, _ = pl.pallas_call(
            body,
            out_shape=(
                jax.ShapeDtypeStruct((ROWS, 32), F32),
                jax.ShapeDtypeStruct((N_STEP, 2, UNITS, STRIP, CHUNK), BF16),
            ),
            in_specs=[hbm, hbm, smem, smem],
            out_specs=(pl.BlockSpec(memory_space=pltpu.VMEM), hbm),
            scratch_shapes=[
                pltpu.VMEM((4, ROWS, 768), BF16),
                pltpu.VMEM((ROWS, 32), BF16),
                pltpu.VMEM((4, 32, ROWS), BF16),
                pltpu.VMEM((4, 32, ROWS), BF16),
                pltpu.VMEM((3, ROWS, 128), F32),
                pltpu.VMEM((4, 1, ROWS), F32),
                pltpu.VMEM((8, CHUNK), F32),
                pltpu.VMEM((3, STRIP + ROWS, 32), F32),
                pltpu.VMEM((5, 32, ROWS), F32),
                pltpu.VMEM((3, 32, ROWS), F32),
                pltpu.VMEM((3, 32, ROWS), F32),
                pltpu.VMEM((3, 32, ROWS), F32),
                pltpu.VMEM((3, 32, ROWS), F32),
                pltpu.VMEM((2, UNITS, STRIP, CHUNK), BF16),
                pltpu.VMEM((2, UNITS, STRIP, CHUNK), BF16),
                pltpu.VMEM((4, 2, UNITS, STRIP, CHUNK), BF16),
                dma((2, N_STRIP)), dma((2, N_STRIP)),
                dma((3,)), dma((3,)), dma((3,)), dma((3,)), dma, dma, dma((2,)),
                dma((2, 2)), dma((4,)),
                dma((3, N_CHUNK)), dma((3, N_CHUNK)), dma((3, N_CHUNK)), dma((3, N_CHUNK)), dma((3, N_CHUNK)), dma((3, N_CHUNK)),
            ],
            compiler_params=pltpu.CompilerParams(collective_id=0, has_side_effects=True, vmem_limit_bytes=62 * 2**20),
            name="products",
        )(x_loc, v_loc, length_scale, out_scale)
        return w

    row_spec = P(("task", "row"), None)
    return jax.shard_map(local_program, mesh=mesh, in_specs=(row_spec, row_spec, P("task"), P("task")), out_specs=row_spec, check_vma=False)
```

time: 1360 us -> 198 us (0.15)
  waiting for transfers between devices: 787 us -> 0 us
  matrix products: 432 us -> 0 us
  Pallas kernels: 0 us -> 192 us
  local copies, waits for them, and re-layouts: 76.8 us -> 4.71 us
  other arithmetic: 50 us -> 0 us
    ppermute x28 -> x0, waiting for transfers between devices: 787 us -> none  [the longest x14 787 us: visit_step(): v_vis = lax.ppermute(v_vis, 'row', shift_pairs)]
    dot_general x17 -> x0, matrix products: 432 us -> none  [the longest x16 406 us: kernel_product(): return jnp.dot(kern_tile, v_cols, preferred_element_type=jnp.float32)]
    pallas_call x0 -> x1, Pallas kernels: none -> 192 us  [local_program(): pl.pallas_call(body, out_shape=(jax.ShapeDtypeStruct((ROWS, 32), F32), ja...]
    while x28 -> x0, local copies, waits for them, and re-layouts: 68.1 us -> none
    reduce_sum x15 -> x0, other arithmetic: 49.9 us -> none  [the longest x14 46.6 us: visit_step(): norm_vis = jnp.sum(jnp.square(x_vis.astype(jnp.float32)), axis=1)]
  transfers between devices with their start and end apart: 28 -> 0, of which waited for: 14 -> 0; matrix products, arithmetic and copies ran while one was open for 0% -> 0% of each run, Pallas kernels for 0% -> 0%
where the time goes in v1:
time: 198 us
  Pallas kernels  192 us (97%)
  local copies, waits for them, and re-layouts  4.71 us (2%)
    pallas_call x1, Pallas kernels, local_program(): pl.pallas_call(body, out_shape=(jax.ShapeDtypeStruct((ROWS, 32), F32), ja...  192 us

profile of v1, /device:TPU:0, one launch (start us, length us, event | category | flops | bytes accessed | tf_op | source)
XLA Modules:
  0.0 198.1 jit_solution(15483063148375156481)
XLA Ops:
  1.3 2.1 %copy.5.v_hbm = bf16[3072,32]{1,0:T(8,128)(2,1)} copy(bf16[3072,32]{0,1:T(8,128)(2,1)} %param.5) | data formatting | bytes 393216 | tf_op args[1]
  3.4 192.0 %products.1 = (f32[3072,32]{1,0:T(8,128)}, bf16[49,2,3,256,512]{4,3,2,1,0:T(8,128)(2,1)}) custom-call(bf16[3072,768]{1,0:T(8,128)(2,1)} %x_hbm.1, bf16[3072,32]{1,0:T(8,128)(2,1)} %copy.5.v_hbm, f32[1]{0:T(128)S(6)} %copy.7.ell_ref, f32[1]{0:T(128)S(6)} %copy.8.amp_ref), custom_call_target="tpu_custom_call" | custom-call | tf_op jit(solution)/shard_map/products/pallas_call | solution.py:447
  195.5 2.6 %copy.6 = f32[3072,32]{0,1:T(8,128)} copy(f32[3072,32]{1,0:T(8,128)} %get-tuple-element.6) | data formatting | bytes 786432 | tf_op jit(solution)/shard_map/products/pallas_call | solution.py:447

commit v2 on v1

--- a/solution.py
+++ b/solution.py
@@ -55,47 +55,59 @@
     return tuple(jnp.int32(x) for x in xs)
 
 
-def own_tile(w, core):
+def wrap(x):
+    return jnp.where(x >= N_CHUNK, x - N_CHUNK, x)
+
+
+def own_pair(i, d, half):
+    return (jnp.int32(OWN), 2 * i + half, jnp.int32(OWN), wrap(i + d), jnp.where(d == 0, TRASH, OWN))
+
+
+def par_pair(a, k, core):
+    return (jnp.int32(OWN), a, jnp.int32(PAR), 2 * k + (((a >> 1) + core) & 1), jnp.int32(PAR))
+
+
+def pre_tile(step, j, core):
+    near = own_pair(3 * (step & 1) + j // 2, step >> 1, j % 2)
+    return pick(step < 4, near, par_pair(2 * (step - 4) + j // 3, j % 3, core))
+
+
+def fill_tile(w, j, core):
     e = w - 24
-    a = e // 3
-    par = (jnp.int32(OWN), a, jnp.int32(PAR), 2 * (e % 3) + (a // 2 + core) % 2, jnp.int32(PAR))
-    v = jnp.where(w < 24, w, w - 36)
-    d, rem = v // 12, v % 12
-    i = rem // 2
-    own = (jnp.int32(OWN), 2 * i + rem % 2, jnp.int32(OWN), (i + d) % N_CHUNK, jnp.where(d == 0, TRASH, OWN))
-    return pick(jnp.logical_and(w >= 24, w < 60), par, own)
-
-
-def strip_tile(n, idx, core):
-    m = n // 2
-    t = (jnp.int32(XNB), n, jnp.int32(OWN), idx, jnp.int32(OWN))
-    t = pick(idx < 6, t, (jnp.int32(YNB), n, jnp.int32(OWN), idx - 6, jnp.int32(OWN)))
-    t = pick(idx < 12, t, (jnp.int32(XNB), n, jnp.int32(YNB), idx - 12, jnp.int32(YNB)))
-    t = pick(idx < 12 + m, t, (jnp.int32(YNB), n, jnp.int32(XNB), idx - 12 - m, jnp.int32(XNB)))
-    t = pick(idx < 12 + 2 * m, t, (jnp.int32(XNB), n - 1 + (idx - 12 - 2 * m), jnp.int32(YNB), m, jnp.int32(YNB)))
-    end = 12 + 2 * m + 2 * (n % 2)
-    w = table(FILL_BASE, n) + idx - end
-    return pick(idx < end, t, own_tile(w, core))
-
-
-def last_tile(idx):
-    c = idx // 2
+    a = (e * 171) >> 9
+    return pick(w < 60, par_pair(a, e - 3 * a, core), own_pair((w - 60) >> 1, jnp.int32(2), j % 2))
+
+
+def left_tile(step, j, core):
+    u = step - LEFT0
+    return own_pair(3 * (1 - u) + j // 2, 2 + u, j % 2)
+
+
+def strip_tile(n, i, j, core):
+    m, odd = n >> 1, n & 1
+    r = 6 * (i - 2) + j
+    t = (jnp.int32(1) + i, n, jnp.int32(OWN), jnp.int32(j), jnp.int32(OWN))
+    t = pick(i < 2, t, (jnp.int32(XNB), n, jnp.int32(YNB), r, jnp.int32(YNB)))
+    t = pick(r < m, t, (jnp.int32(YNB), n, jnp.int32(XNB), r - m, jnp.int32(XNB)))
+    t = pick(r < 2 * m, t, (jnp.int32(XNB), n - 1 + (r - 2 * m), jnp.int32(YNB), m, jnp.int32(YNB)))
+    end = 2 * (m + odd)
+    return pick(r < end, t, fill_tile(table(FILL_BASE, n) + r - end, j, core))
+
+
+def last_tile(i, j):
     n = jnp.int32(N_STRIP - 1)
-    odd = idx % 2 == 1
-    t = pick(odd, (jnp.int32(XNB), n, jnp.int32(YNB), c, jnp.int32(YNB)), (jnp.int32(YNB), n, jnp.int32(XNB), c, jnp.int32(XNB)))
-    t = pick(idx < 10, t, (jnp.int32(XNB), idx, jnp.int32(YNB), jnp.int32(5), jnp.int32(YNB)))
-    j = idx - 12
-    return pick(idx < 12, t, (jnp.where(j < 6, XNB, YNB), n, jnp.int32(OWN), j % 6, jnp.int32(OWN)))
-
-
-def step_tile(step, j, core):
+    s, t = (XNB, YNB) if j % 2 else (YNB, XNB)
+    cross = (jnp.int32(s), n, jnp.int32(t), 3 * i + j // 2, jnp.int32(t))
+    if j >= 4:
+        cross = pick(i < 1, cross, (jnp.int32(XNB), jnp.int32(N_STRIP - 2 + j % 2), jnp.int32(YNB), jnp.int32(5), jnp.int32(YNB)))
+    return pick(i < 2, cross, (i - 1, n, jnp.int32(OWN), jnp.int32(j), jnp.int32(OWN)))
+
+
+def strip_of(step):
     n = jnp.int32(0)
     for i in range(1, N_STRIP):
         n = n + (step >= STEP_BASE[i]).astype(jnp.int32)
-    idx = (step - table(STEP_BASE, n)) * 6 + j
-    t = pick(n < N_STRIP - 1, strip_tile(n, idx, core), last_tile(idx))
-    w = jnp.where(step < PRE, step * 6, 66 + (step - LEFT0) * 6) + j
-    return pick(jnp.logical_or(step < PRE, step >= LEFT0), own_tile(w, core), t)
+    return n
 
 
 def rows_of(a):
@@ -112,7 +124,7 @@
 
 def body(
     x_hbm, v_hbm, ell_ref, amp_ref, out_ref, k_hbm,
-    X, V0, VT, YV, NA, NB, CR, YR, YT, SB, RB, SB2, RB2, kr0, kr1, KB,
+    X, VT, YV, NA, NB, CR, YR, YT, SB, RB, SB2, RB2, kr0, kr1, KB,
     sx_sem, rx_sem, sv_sem, rv_sem, sn_sem, rn_sem, sp_sem, rp_sem, loc_sem, ko_sem, ki_sem,
     s1_sem, r1_sem, sy_sem, ry_sem, s2_sem, r2_sem,
 ):
@@ -135,19 +147,22 @@
         return remote(x_hbm.at[rows_of(n)], X.at[1 + j, rows_of(n)], sx_sem.at[j, n], rx_sem.at[j, n], (tx, ty)[j])
 
     p_copy = remote(x_hbm, X.at[PAR], sp_sem, rp_sem, pt)
-    v_copies = [remote(VT.at[OWN], VT.at[1 + j], sv_sem.at[j], rv_sem.at[j], d) for j, d in enumerate((tx, ty, pt))]
+    v_copies = [remote(v_hbm, VT.at[1 + j], sv_sem.at[j], rv_sem.at[j], d) for j, d in enumerate((tx, ty, pt))]
     n_copies = [remote(NB.at[OWN], NB.at[1 + j], sn_sem.at[j], rn_sem.at[j], d) for j, d in enumerate((tx, ty, pt))]
 
     x_loc = pltpu.make_async_copy(x_hbm, X.at[OWN], loc_sem.at[0])
-    v_loc = pltpu.make_async_copy(v_hbm, V0, loc_sem.at[1])
+    v_loc = pltpu.make_async_copy(v_hbm, VT.at[OWN], loc_sem.at[1])
     v_loc.start()
     x_loc.start()
 
     barrier = pltpu.get_barrier_semaphore()
     for d in (tx, ty, sx, sy, pt):
         pl.semaphore_signal(barrier, inc=1, device_id=d, device_id_type=MESH)
-    pl.semaphore_wait(barrier, 5)
-
+    with jax.named_scope("barrier"):
+        pl.semaphore_wait(barrier, 5)
+
+    for c in v_copies:
+        c.start()
     for j in range(2):
         x_copy(j, 0).start()
     p_copy.start()
@@ -166,16 +181,9 @@
     kr0[...] = jnp.zeros_like(kr0)
     kr1[...] = jnp.zeros_like(kr1)
 
-    eye = (lax.broadcasted_iota(jnp.int32, (32, 32), 0) == lax.broadcasted_iota(jnp.int32, (32, 32), 1)).astype(F32).astype(BF16)
     v_loc.wait()
-
-    def turn(c, _):
-        v = V0[pl.ds(pl.multiple_of(c * CHUNK, CHUNK), CHUNK), :]
-        VT[OWN, :, cols_of(c)] = lax.dot_general(eye, v, (((1,), (1,)), ((), ())), preferred_element_type=F32).astype(BF16)
-        return 0
-
-    lax.fori_loop(0, N_CHUNK, turn, 0)
-    x_loc.wait()
+    with jax.named_scope("x_local"):
+        x_loc.wait()
 
     def own_norm(c, _):
         r = pl.ds(pl.multiple_of(c * CHUNK, CHUNK), CHUNK)
@@ -185,8 +193,9 @@
         NB[OWN, :, cols_of(c)] = -jnp.transpose(n)[0:1, :]
         return 0
 
-    lax.fori_loop(0, N_CHUNK, own_norm, 0)
-    for c in v_copies + n_copies:
+    with jax.named_scope("own_norm"):
+        lax.fori_loop(0, N_CHUNK, own_norm, 0)
+    for c in n_copies:
         c.start()
 
     def send_strip(n, _):
@@ -221,7 +230,7 @@
 
     def k_out(step, half):
         kr = (kr0, kr1)[half]
-        return pltpu.make_async_copy(kr.at[step % 2], k_hbm.at[step, half], ko_sem.at[step % 2, half])
+        return pltpu.make_async_copy(kr.at[step & 1], k_hbm.at[step, half], ko_sem.at[step & 1, half])
 
     def half_step(prev, cur, kr_new, d_new, kr_old, d_old):
         gs = [gram(t) for t in cur]
@@ -236,8 +245,8 @@
     def unflat(xs):
         return [tuple(xs[5 * u : 5 * u + 5]) for u in range(UNITS)]
 
-    def step_of(step, prev):
-        d = step % 2
+    def step_of(step, prev, tile):
+        d = step & 1
 
         @pl.when(step >= 2)
         def _():
@@ -249,16 +258,13 @@
             for h in range(2):
                 k_out(step - 1, h).start()
 
-        first = [step_tile(step, u, core) for u in range(UNITS)]
-        second = [step_tile(step, UNITS + u, core) for u in range(UNITS)]
+        first = [tile(u) for u in range(UNITS)]
+        second = [tile(UNITS + u) for u in range(UNITS)]
         half_step(unflat(prev), first, kr0, d, kr1, 1 - d)
         half_step(first, second, kr1, d, kr0, d)
         return flat(second)
 
     none = flat([i32(OWN, -1, OWN, 0, TRASH)] * UNITS)
-
-    def steps(lo, hi, prev):
-        return lax.fori_loop(lo, hi, step_of, prev)
 
     def pre_step(step, prev):
         @pl.when(step == 4)
@@ -267,29 +273,34 @@
             v_copies[2].wait_recv()
             n_copies[2].wait_recv()
 
-        return step_of(step, prev)
-
-    prev = lax.fori_loop(0, PRE, pre_step, none)
-
-    for j in range(2):
-        v_copies[j].wait_recv()
-        n_copies[j].wait_recv()
-        left_norm(1 + j)
+        return step_of(step, prev, lambda j: pre_tile(step, j, core))
+
+    with jax.named_scope("pre"):
+        prev = lax.fori_loop(0, PRE, pre_step, none)
+
+    with jax.named_scope("left_norm"):
+        for j in range(2):
+            v_copies[j].wait_recv()
+            n_copies[j].wait_recv()
+            left_norm(1 + j)
 
     def strip(n, prev):
+        with jax.named_scope("wait_strip"):
+            for j in range(2):
+                x_copy(j, n).wait_recv()
+            lo = table(STEP_BASE, n)
+        with jax.named_scope("strip"):
+            return lax.fori_loop(0, table(STEPS, n), lambda i, p: step_of(lo + i, p, lambda j: strip_tile(n, i, j, core)), prev)
+
+    prev = lax.fori_loop(0, N_STRIP - 1, strip, prev)
+
+    with jax.named_scope("wait_last"):
         for j in range(2):
-            x_copy(j, n).wait_recv()
-        lo = table(STEP_BASE, n)
-        return steps(lo, lo + table(STEPS, n), prev)
-
-    prev = lax.fori_loop(0, N_STRIP - 1, strip, prev)
-
-    for j in range(2):
-        x_copy(j, N_STRIP - 1).wait_recv()
+            x_copy(j, N_STRIP - 1).wait_recv()
 
     def flush(step, prev):
         for u, t in enumerate(unflat(prev)):
-            apply(t, kr1[step % 2, u], VT)
+            apply(t, kr1[step & 1, u], VT)
 
     homes = ((XNB, sx), (YNB, sy), (PAR, pt))
 
@@ -320,17 +331,19 @@
         lax.fori_loop(lo, hi, go, 0)
 
     def last_step(step, prev):
-        prev = step_of(step, prev)
+        i = step - TAIL0
+        prev = step_of(step, prev, lambda j: last_tile(i, j))
         flush(step, prev)
-        i = step - TAIL0
         lo = table((0, 3, 5, 5), i)
         hi = table((3, 5, 5, 6), i)
         finish_range(lo, hi, SB, RB, s1_sem, r1_sem)
         return none
 
-    prev = lax.fori_loop(TAIL0, LEFT0, last_step, prev)
-    prev = steps(LEFT0, N_STEP, prev)
-    flush(N_STEP - 1, prev)
+    with jax.named_scope("last"):
+        prev = lax.fori_loop(TAIL0, LEFT0, last_step, prev)
+    with jax.named_scope("left"):
+        prev = lax.fori_loop(LEFT0, N_STEP, lambda step, p: step_of(step, p, lambda j: left_tile(step, j, core)), prev)
+        flush(N_STEP - 1, prev)
     finish_range(0, N_CHUNK, SB, RB, s1_sem, r1_sem, (2,))
     for h in range(2):
         k_out(N_STEP - 2, h).wait()
@@ -344,7 +357,7 @@
     DEPTH = KB.shape[0]
 
     def k_in(i):
-        return pltpu.make_async_copy(k_hbm.at[order(i)], KB.at[i % DEPTH], ki_sem.at[i % DEPTH])
+        return pltpu.make_async_copy(k_hbm.at[order(i)], KB.at[i & (DEPTH - 1)], ki_sem.at[i & (DEPTH - 1)])
 
     for i in range(DEPTH - 1):
         k_in(jnp.int32(i)).start()
@@ -353,8 +366,9 @@
         return remote(YV.at[OWN, :, cols_of(c)], YV.at[1 + j, :, cols_of(c)], sy_sem.at[j, c], ry_sem.at[j, c], (tx, ty, pt)[j])
 
     def middle(c, _):
-        for j in range(3):
-            part_copy(j, c, SB, RB, s1_sem, r1_sem).wait_recv()
+        with jax.named_scope("wait_part"):
+            for j in range(3):
+                part_copy(j, c, SB, RB, s1_sem, r1_sem).wait_recv()
         y = YT[OWN, :, cols_of(c)] + jnp.transpose(YR[OWN, sums_of(c), :])
         y = y + RB[0, :, cols_of(c)] + RB[1, :, cols_of(c)] + RB[2, :, cols_of(c)]
         YV[OWN, :, cols_of(c)] = y.astype(BF16)
@@ -367,11 +381,11 @@
             y_copy(j, c).start()
         return 0
 
-    lax.fori_loop(0, N_CHUNK, middle, 0)
+    with jax.named_scope("middle"):
+        lax.fori_loop(0, N_CHUNK, middle, 0)
     lax.fori_loop(0, N_CHUNK, middle_go, 0)
 
-    def second(i, _):
-        step = order(i)
+    def second(i, tile):
         k_in(i).wait()
 
         @pl.when(i + DEPTH - 1 < N_STEP)
@@ -379,8 +393,20 @@
             k_in(i + DEPTH - 1).start()
 
         for j in range(6):
-            apply(step_tile(step, j, core), KB[i % DEPTH, j // 3, j % 3], YV)
-        return 0
+            apply(tile(j), KB[i & (DEPTH - 1), j // 3, j % 3], YV)
+        return 0
+
+    def second_own(i, _):
+        return second(i, lambda j: pick(i < PRE, pre_tile(i, j, core), left_tile(order(i), j, core)))
+
+    def second_last(i, _):
+        return second(i, lambda j: last_tile(order(i) - TAIL0, j))
+
+    def second_strip(i, _):
+        step = order(i)
+        n = strip_of(step)
+        k = step - table(STEP_BASE, n)
+        return second(i, lambda j: strip_tile(n, k, j, core))
 
     def wait_y(j):
         def one(c, _):
@@ -389,36 +415,42 @@
 
         lax.fori_loop(0, N_CHUNK, one, 0)
 
-    lax.fori_loop(0, 4, second, 0)
-    wait_y(2)
-    lax.fori_loop(4, PRE + 2, second, 0)
-    wait_y(0)
-    wait_y(1)
+    with jax.named_scope("second_own"):
+        lax.fori_loop(0, 4, second_own, 0)
+        wait_y(2)
+        lax.fori_loop(4, PRE + 2, second_own, 0)
+    with jax.named_scope("wait_y"):
+        wait_y(0)
+        wait_y(1)
 
     bounds = tuple(N_STEP + PRE - STEP_BASE[2 * c] for c in range(N_CHUNK))
 
     def second_chunk(k, lo):
         c = N_CHUNK - 1 - k
         hi = table(bounds, c)
-        lax.fori_loop(lo, hi, second, 0)
+        with jax.named_scope("second_chunk"):
+            lax.fori_loop(lo, hi, second_strip, 0)
         finish_range(c, c + 1, SB2, RB2, s2_sem, r2_sem, (0, 1))
         return hi
 
-    lo = lax.fori_loop(0, N_CHUNK, second_chunk, jnp.int32(PRE + 2))
+    with jax.named_scope("second_last"):
+        lax.fori_loop(PRE + 2, PRE + 2 + STEPS[11], second_last, 0)
+    lo = lax.fori_loop(0, N_CHUNK, second_chunk, jnp.int32(PRE + 2 + STEPS[11]))
     finish_range(0, N_CHUNK, SB2, RB2, s2_sem, r2_sem, (2,))
 
     def final(k, _):
         c = N_CHUNK - 1 - k
         for j in range(3):
             part_copy(j, c, SB2, RB2, s2_sem, r2_sem).wait_recv()
-        r = pl.ds(pl.multiple_of(c * CHUNK, CHUNK), CHUNK)
-        w = YT[OWN, :, cols_of(c)] + RB2[0, :, cols_of(c)] + RB2[1, :, cols_of(c)] + RB2[2, :, cols_of(c)]
-        out_ref[r, :] = YR[OWN, sums_of(c), :] + jnp.transpose(w)
-        return 0
-
-    lax.fori_loop(0, N_CHUNK, final, 0)
-
-    p_copy.wait_send()
+        w = YT[OWN, :, cols_of(c)] + jnp.transpose(YR[OWN, sums_of(c), :]) + RB2[0, :, cols_of(c)] + RB2[1, :, cols_of(c)] + RB2[2, :, cols_of(c)]
+        out_ref[:, cols_of(c)] = w
+        return 0
+
+    with jax.named_scope("final"):
+        lax.fori_loop(0, N_CHUNK, final, 0)
+
+    with jax.named_scope("drain"):
+        p_copy.wait_send()
     for c in v_copies + n_copies:
         c.wait_send()
 
@@ -447,14 +479,13 @@
         w, _ = pl.pallas_call(
             body,
             out_shape=(
-                jax.ShapeDtypeStruct((ROWS, 32), F32),
+                jax.ShapeDtypeStruct((32, ROWS), F32),
                 jax.ShapeDtypeStruct((N_STEP, 2, UNITS, STRIP, CHUNK), BF16),
             ),
             in_specs=[hbm, hbm, smem, smem],
             out_specs=(pl.BlockSpec(memory_space=pltpu.VMEM), hbm),
             scratch_shapes=[
                 pltpu.VMEM((4, ROWS, 768), BF16),
-                pltpu.VMEM((ROWS, 32), BF16),
                 pltpu.VMEM((4, 32, ROWS), BF16),
                 pltpu.VMEM((4, 32, ROWS), BF16),
                 pltpu.VMEM((3, ROWS, 128), F32),
@@ -476,8 +507,8 @@
             ],
             compiler_params=pltpu.CompilerParams(collective_id=0, has_side_effects=True, vmem_limit_bytes=62 * 2**20),
             name="products",
-        )(x_loc, v_loc, length_scale, out_scale)
-        return w
+        )(x_loc, v_loc.T, length_scale, out_scale)
+        return w.T
 
     row_spec = P(("task", "row"), None)
     return jax.shard_map(local_program, mesh=mesh, in_specs=(row_spec, row_spec, P("task"), P("task")), out_specs=row_spec, check_vma=False)

time: 198 us -> 171 us (0.86)
  Pallas kernels: 192 us -> 167 us
  local copies, waits for them, and re-layouts: 4.71 us -> 1.77 us
    pallas_call x1, Pallas kernels: 192 us -> 167 us  [local_program(): pl.pallas_call(body, out_shape=(jax.ShapeDtypeStruct((32, ROWS), F32), ja...]
    pallas_call x1 -> x0, local copies, waits for them, and re-layouts: 2.6 us -> none  [local_program(): pl.pallas_call(body, out_shape=(jax.ShapeDtypeStruct((ROWS, 32), F32), ja...]
where the time goes in v2:
time: 171 us; the launch traced here: 170 us
  Pallas kernels  167 us (98%)
  local copies, waits for them, and re-layouts  1.77 us (1%)
    pallas_call x1, Pallas kernels, local_program(): pl.pallas_call(body, out_shape=(jax.ShapeDtypeStruct((32, ROWS), F32), ja...  167 us

profile of v2, /device:TPU:0, one launch (start us, length us, event | category | flops | bytes accessed | tf_op | source)
XLA Modules:
  0.0 170.5 jit_solution(13693507817345195890)
XLA Ops:
  1.3 167.4 %products.1 = (f32[32,3072]{1,0:T(8,128)}, bf16[49,2,3,256,512]{4,3,2,1,0:T(8,128)(2,1)}) custom-call(bf16[3072,768]{1,0:T(8,128)(2,1)} %x_hbm.1, bf16[32,3072]{1,0:T(8,128)(2,1)} %bitcast.3, f32[1]{0:T(128)S(6)} %copy.6.ell_ref, f32[1]{0:T(128)S(6)} %copy.7.amp_ref), custom_call_target="tpu_custom_call" | custom-call | tf_op jit(solution)/shard_map/products/pallas_call | solution.py:479
  168.7 1.8 %copy.8 = f32[3072,32]{0,1:T(8,128)} copy(f32[3072,32]{0,1:T(8,128)} %bitcast.2) | data formatting | bytes 786432

commit v3 on v2

--- a/solution.py
+++ b/solution.py
@@ -19,13 +19,16 @@
 UNITS = 3
 OWN, XNB, YNB, PAR, TRASH = 0, 1, 2, 3, 4
 
-PRE = 7
-FILL = (0, 4, 4, 2, 2, 0, 0, 4, 4, 2, 2, 0)
-TILES = tuple(12 + 2 * (n // 2) + 2 * (n % 2) for n in range(N_STRIP))
-STEPS = tuple((TILES[n] + FILL[n]) // 6 for n in range(N_STRIP))
-N_STEP = PRE + sum(STEPS) + 2
-TAIL0 = PRE + sum(STEPS[:11])
-LEFT0 = TAIL0 + STEPS[11]
+N_OWN, N_PAIR, N_CROSS = 7, 13, 12
+PRE = 5
+OWN_AT = (5, 7, 9, 11, 12, 13, 13, 13, 13, 13, 13, 13)
+CROSS_AT = (0, 0, 0, 0, 1, 2, 3, 4, 5, 6, 8, 10)
+CROSS_TILE = (0, 0, 2, 4, 8, 12, 18, 24, 32, 40, 50, 60)
+OWN_PLACE = 1
+CROSS_PLACE = OWN_PLACE + N_PAIR
+STRIP_PLACE = CROSS_PLACE + N_CROSS
+N_PLACE = STRIP_PLACE + 2 * N_STRIP
+N_DOUBLE = N_PLACE // 2
 
 
 def table(values, n):
@@ -36,15 +39,11 @@
     return out
 
 
-def cumulative(values):
-    out = [0]
-    for v in values:
-        out.append(out[-1] + v)
-    return tuple(out[:-1])
-
-
-FILL_BASE = tuple(PRE * 6 + c for c in cumulative(FILL))
-STEP_BASE = tuple(PRE + c for c in cumulative(STEPS))
+def rank(bounds, x):
+    out = jnp.int32(0)
+    for b in bounds:
+        out = out + (x >= b).astype(jnp.int32)
+    return out
 
 
 def pick(cond, a, b):
@@ -55,43 +54,27 @@
     return tuple(jnp.int32(x) for x in xs)
 
 
-def wrap(x):
-    return jnp.where(x >= N_CHUNK, x - N_CHUNK, x)
-
-
-def own_pair(i, d, half):
-    return (jnp.int32(OWN), 2 * i + half, jnp.int32(OWN), wrap(i + d), jnp.where(d == 0, TRASH, OWN))
-
-
-def par_pair(a, k, core):
-    return (jnp.int32(OWN), a, jnp.int32(PAR), 2 * k + (((a >> 1) + core) & 1), jnp.int32(PAR))
-
-
-def pre_tile(step, j, core):
-    near = own_pair(3 * (step & 1) + j // 2, step >> 1, j % 2)
-    return pick(step < 4, near, par_pair(2 * (step - 4) + j // 3, j % 3, core))
-
-
-def fill_tile(w, j, core):
-    e = w - 24
-    a = (e * 171) >> 9
-    return pick(w < 60, par_pair(a, e - 3 * a, core), own_pair((w - 60) >> 1, jnp.int32(2), j % 2))
-
-
-def left_tile(step, j, core):
-    u = step - LEFT0
-    return own_pair(3 * (1 - u) + j // 2, 2 + u, j % 2)
-
-
-def strip_tile(n, i, j, core):
-    m, odd = n >> 1, n & 1
-    r = 6 * (i - 2) + j
-    t = (jnp.int32(1) + i, n, jnp.int32(OWN), jnp.int32(j), jnp.int32(OWN))
-    t = pick(i < 2, t, (jnp.int32(XNB), n, jnp.int32(YNB), r, jnp.int32(YNB)))
-    t = pick(r < m, t, (jnp.int32(YNB), n, jnp.int32(XNB), r - m, jnp.int32(XNB)))
-    t = pick(r < 2 * m, t, (jnp.int32(XNB), n - 1 + (r - 2 * m), jnp.int32(YNB), m, jnp.int32(YNB)))
-    end = 2 * (m + odd)
-    return pick(r < end, t, fill_tile(table(FILL_BASE, n) + r - end, j, core))
+def own_tile(o, j, core):
+    p = 3 * o + j // 2
+    c = rank((1, 3, 6, 10, 15), p)
+    i = p - ((c * (c + 1)) >> 1)
+    own = (jnp.int32(OWN), 2 * i + j % 2, jnp.int32(OWN), c, jnp.where(i == c, TRASH, OWN))
+    a = 2 * (o - N_OWN) + j // 3
+    par = (jnp.int32(OWN), a, jnp.int32(PAR), 2 * (j % 3) + (((a >> 1) + core) & 1), jnp.int32(PAR))
+    return pick(o < N_OWN, own, par)
+
+
+def strip_tile(n, side, j):
+    return (1 + side, n, jnp.int32(OWN), jnp.int32(j), jnp.int32(OWN))
+
+
+def cross_tile(q, j):
+    g = 6 * q + j
+    n = 1 + rank(CROSS_TILE[2:11], g)
+    r = g - table(CROSS_TILE, n)
+    m = n >> 1
+    t = pick(r < m, (jnp.int32(XNB), n, jnp.int32(YNB), r, jnp.int32(YNB)), (jnp.int32(YNB), n, jnp.int32(XNB), r - m, jnp.int32(XNB)))
+    return pick(r < 2 * m, t, (jnp.int32(XNB), n - 1 + (r - 2 * m), jnp.int32(YNB), m, jnp.int32(YNB)))
 
 
 def last_tile(i, j):
@@ -100,14 +83,7 @@
     cross = (jnp.int32(s), n, jnp.int32(t), 3 * i + j // 2, jnp.int32(t))
     if j >= 4:
         cross = pick(i < 1, cross, (jnp.int32(XNB), jnp.int32(N_STRIP - 2 + j % 2), jnp.int32(YNB), jnp.int32(5), jnp.int32(YNB)))
-    return pick(i < 2, cross, (i - 1, n, jnp.int32(OWN), jnp.int32(j), jnp.int32(OWN)))
-
-
-def strip_of(step):
-    n = jnp.int32(0)
-    for i in range(1, N_STRIP):
-        n = n + (step >= STEP_BASE[i]).astype(jnp.int32)
-    return n
+    return cross
 
 
 def rows_of(a):
@@ -228,9 +204,9 @@
         YR[s, rows_of(a + 1), :] += lax.dot_general(k, vec[t, :, cols_of(b)], (((1,), (1,)), ((), ())), preferred_element_type=F32)
         YT[to, :, cols_of(b)] += jnp.dot(vec[s, :, rows_of(jnp.maximum(a, 0))], k, preferred_element_type=F32)
 
-    def k_out(step, half):
+    def k_out(seq, place, half):
         kr = (kr0, kr1)[half]
-        return pltpu.make_async_copy(kr.at[step & 1], k_hbm.at[step, half], ko_sem.at[step & 1, half])
+        return pltpu.make_async_copy(kr.at[seq & 1], k_hbm.at[place, half], ko_sem.at[seq & 1, half])
 
     def half_step(prev, cur, kr_new, d_new, kr_old, d_old):
         gs = [gram(t) for t in cur]
@@ -245,62 +221,64 @@
     def unflat(xs):
         return [tuple(xs[5 * u : 5 * u + 5]) for u in range(UNITS)]
 
-    def step_of(step, prev, tile):
-        d = step & 1
-
-        @pl.when(step >= 2)
+    def step_of(state, place, tile):
+        seq, before, prev = state[0], state[1], state[2:]
+        d = seq & 1
+
+        @pl.when(seq >= 2)
         def _():
             for h in range(2):
-                k_out(step - 2, h).wait()
-
-        @pl.when(step >= 1)
+                k_out(seq, place, h).wait()
+
+        @pl.when(seq >= 1)
         def _():
             for h in range(2):
-                k_out(step - 1, h).start()
+                k_out(seq - 1, before, h).start()
 
         first = [tile(u) for u in range(UNITS)]
         second = [tile(UNITS + u) for u in range(UNITS)]
         half_step(unflat(prev), first, kr0, d, kr1, 1 - d)
         half_step(first, second, kr1, d, kr0, d)
-        return flat(second)
+        return (seq + 1, place) + flat(second)
 
     none = flat([i32(OWN, -1, OWN, 0, TRASH)] * UNITS)
 
-    def pre_step(step, prev):
-        @pl.when(step == 4)
-        def _():
-            p_copy.wait_recv()
-            v_copies[2].wait_recv()
-            n_copies[2].wait_recv()
-
-        return step_of(step, prev, lambda j: pre_tile(step, j, core))
+    def flush(state):
+        for u, t in enumerate(unflat(state[2:])):
+            apply(t, kr1[(state[0] - 1) & 1, u], VT)
+        return state[:2] + none
+
+    def own_step(o, state):
+        return step_of(state, OWN_PLACE + o, lambda j: own_tile(o, j, core))
+
+    def cross_step(q, state):
+        return step_of(state, CROSS_PLACE + q, lambda j: cross_tile(q, j))
+
+    def strip_step(n, side, state):
+        return step_of(state, STRIP_PLACE + 2 * (N_STRIP - 1 - n) + side, lambda j: strip_tile(n, side, j))
 
     with jax.named_scope("pre"):
-        prev = lax.fori_loop(0, PRE, pre_step, none)
+        state = lax.fori_loop(0, PRE, own_step, i32(0, 0) + none)
 
     with jax.named_scope("left_norm"):
         for j in range(2):
             v_copies[j].wait_recv()
             n_copies[j].wait_recv()
             left_norm(1 + j)
-
-    def strip(n, prev):
+        p_copy.wait_recv()
+        v_copies[2].wait_recv()
+        n_copies[2].wait_recv()
+
+    def strip(n, state):
         with jax.named_scope("wait_strip"):
             for j in range(2):
                 x_copy(j, n).wait_recv()
-            lo = table(STEP_BASE, n)
         with jax.named_scope("strip"):
-            return lax.fori_loop(0, table(STEPS, n), lambda i, p: step_of(lo + i, p, lambda j: strip_tile(n, i, j, core)), prev)
-
-    prev = lax.fori_loop(0, N_STRIP - 1, strip, prev)
-
-    with jax.named_scope("wait_last"):
-        for j in range(2):
-            x_copy(j, N_STRIP - 1).wait_recv()
-
-    def flush(step, prev):
-        for u, t in enumerate(unflat(prev)):
-            apply(t, kr1[step & 1, u], VT)
+            state = lax.fori_loop(0, 2, lambda side, st: strip_step(n, side, st), state)
+            state = lax.fori_loop(table(CROSS_AT, n), table(CROSS_AT, n + 1), cross_step, state)
+            return lax.fori_loop(table(OWN_AT, n), table(OWN_AT, n + 1), own_step, state)
+
+    state = lax.fori_loop(0, N_STRIP - 1, strip, state)
 
     homes = ((XNB, sx), (YNB, sy), (PAR, pt))
 
@@ -330,83 +308,87 @@
         lax.fori_loop(lo, hi, one, 0)
         lax.fori_loop(lo, hi, go, 0)
 
-    def last_step(step, prev):
-        i = step - TAIL0
-        prev = step_of(step, prev, lambda j: last_tile(i, j))
-        flush(step, prev)
-        lo = table((0, 3, 5, 5), i)
-        hi = table((3, 5, 5, 6), i)
+    def k_in(i):
+        return pltpu.make_async_copy(k_hbm.at[pl.ds(2 * i, 2)], KB.at[i & 3], ki_sem.at[i & 3])
+
+    first_in = pltpu.make_async_copy(k_hbm.at[1], KB.at[0, 1], ki_sem.at[0])
+    first_in.start()
+    for i in range(1, 4):
+        k_in(jnp.int32(i)).start()
+
+    finish_range(0, N_CHUNK, SB, RB, s1_sem, r1_sem, (2,))
+    with jax.named_scope("wait_last"):
+        for j in range(2):
+            x_copy(j, N_STRIP - 1).wait_recv()
+
+    def last_step(i, state):
+        state = step_of(state, CROSS_PLACE + 10 + i, lambda j: last_tile(i, j))
+        state = flush(state)
+        lo, hi = 3 * i, 3 + 2 * i
         finish_range(lo, hi, SB, RB, s1_sem, r1_sem)
-        return none
+        return state
 
     with jax.named_scope("last"):
-        prev = lax.fori_loop(TAIL0, LEFT0, last_step, prev)
-    with jax.named_scope("left"):
-        prev = lax.fori_loop(LEFT0, N_STEP, lambda step, p: step_of(step, p, lambda j: left_tile(step, j, core)), prev)
-        flush(N_STEP - 1, prev)
-    finish_range(0, N_CHUNK, SB, RB, s1_sem, r1_sem, (2,))
+        state = lax.fori_loop(0, 2, last_step, state)
+        state = lax.fori_loop(0, 2, lambda side, st: strip_step(jnp.int32(N_STRIP - 1), side, st), state)
+        state = flush(state)
+        finish_range(5, 6, SB, RB, s1_sem, r1_sem)
+
     for h in range(2):
-        k_out(N_STEP - 2, h).wait()
-        k_out(N_STEP - 1, h).start()
-    for h in range(2):
-        k_out(N_STEP - 1, h).wait()
-
-    def order(i):
-        return jnp.where(i < PRE, i, jnp.where(i < PRE + 2, LEFT0 + i - PRE, N_STEP - 1 + PRE - i))
-
-    DEPTH = KB.shape[0]
-
-    def k_in(i):
-        return pltpu.make_async_copy(k_hbm.at[order(i)], KB.at[i & (DEPTH - 1)], ki_sem.at[i & (DEPTH - 1)])
-
-    for i in range(DEPTH - 1):
-        k_in(jnp.int32(i)).start()
+        k_out(state[0], 0, h).wait()
+        k_out(state[0] - 1, state[1], h).start()
 
     def y_copy(j, c):
         return remote(YV.at[OWN, :, cols_of(c)], YV.at[1 + j, :, cols_of(c)], sy_sem.at[j, c], ry_sem.at[j, c], (tx, ty, pt)[j])
 
-    def middle(c, _):
-        with jax.named_scope("wait_part"):
+    def middle(lo, hi):
+        def one(c, _):
+            with jax.named_scope("wait_part"):
+                for j in range(3):
+                    part_copy(j, c, SB, RB, s1_sem, r1_sem).wait_recv()
+            y = YT[OWN, :, cols_of(c)] + jnp.transpose(YR[OWN, sums_of(c), :])
+            y = y + RB[0, :, cols_of(c)] + RB[1, :, cols_of(c)] + RB[2, :, cols_of(c)]
+            YV[OWN, :, cols_of(c)] = y.astype(BF16)
+            YT[OWN, :, cols_of(c)] = jnp.zeros((32, CHUNK), F32)
+            YR[OWN, sums_of(c), :] = jnp.zeros((CHUNK, 32), F32)
+            return 0
+
+        def go(c, _):
             for j in range(3):
-                part_copy(j, c, SB, RB, s1_sem, r1_sem).wait_recv()
-        y = YT[OWN, :, cols_of(c)] + jnp.transpose(YR[OWN, sums_of(c), :])
-        y = y + RB[0, :, cols_of(c)] + RB[1, :, cols_of(c)] + RB[2, :, cols_of(c)]
-        YV[OWN, :, cols_of(c)] = y.astype(BF16)
-        YT[OWN, :, cols_of(c)] = jnp.zeros((32, CHUNK), F32)
-        YR[OWN, sums_of(c), :] = jnp.zeros((CHUNK, 32), F32)
-        return 0
-
-    def middle_go(c, _):
-        for j in range(3):
-            y_copy(j, c).start()
-        return 0
-
-    with jax.named_scope("middle"):
-        lax.fori_loop(0, N_CHUNK, middle, 0)
-    lax.fori_loop(0, N_CHUNK, middle_go, 0)
-
-    def second(i, tile):
+                y_copy(j, c).start()
+            return 0
+
+        lax.fori_loop(lo, hi, one, 0)
+        lax.fori_loop(lo, hi, go, 0)
+
+    def second(i, tile, count=2):
+        @pl.when(i + 3 < N_DOUBLE)
+        def _():
+            k_in(i + 3).start()
+
+        for h in range(2 - count, 2):
+            for j in range(6):
+                apply(tile(h, j), KB[i & 3, h, j // 3, j % 3], YV)
+
+    def second_own(i, _):
         k_in(i).wait()
-
-        @pl.when(i + DEPTH - 1 < N_STEP)
-        def _():
-            k_in(i + DEPTH - 1).start()
-
-        for j in range(6):
-            apply(tile(j), KB[i & (DEPTH - 1), j // 3, j % 3], YV)
-        return 0
-
-    def second_own(i, _):
-        return second(i, lambda j: pick(i < PRE, pre_tile(i, j, core), left_tile(order(i), j, core)))
-
-    def second_last(i, _):
-        return second(i, lambda j: last_tile(order(i) - TAIL0, j))
+        second(i, lambda h, j: own_tile(2 * i + h - OWN_PLACE, j, core))
+        return 0
+
+    def second_cross(i, _):
+        k_in(i).wait()
+
+        def tile(h, j):
+            q = 2 * i + h - CROSS_PLACE
+            return pick(q < 10, cross_tile(q, j), last_tile(q - 10, j))
+
+        second(i, tile)
+        return 0
 
     def second_strip(i, _):
-        step = order(i)
-        n = strip_of(step)
-        k = step - table(STEP_BASE, n)
-        return second(i, lambda j: strip_tile(n, k, j, core))
+        k_in(i).wait()
+        second(i, lambda h, j: strip_tile(N_STRIP - 1 + STRIP_PLACE // 2 - i, jnp.int32(h), j))
+        return 0
 
     def wait_y(j):
         def one(c, _):
@@ -415,28 +397,39 @@
 
         lax.fori_loop(0, N_CHUNK, one, 0)
 
+    with jax.named_scope("middle"):
+        middle(0, 4)
     with jax.named_scope("second_own"):
-        lax.fori_loop(0, 4, second_own, 0)
+        first_in.wait()
+        for j in range(6):
+            apply(own_tile(jnp.int32(0), j, core), KB[0, 1, j // 3, j % 3], YV)
+
+        def own_and_middle(i, _):
+            second_own(i, _)
+            middle(i + 3, jnp.minimum(i + 4, N_CHUNK))
+            return 0
+
+        lax.fori_loop(1, 4, own_and_middle, 0)
+        for h in range(2):
+            k_out(state[0] - 1, 0, h).wait()
         wait_y(2)
-        lax.fori_loop(4, PRE + 2, second_own, 0)
+        lax.fori_loop(4, 7, second_own, 0)
+    finish_range(0, N_CHUNK, SB2, RB2, s2_sem, r2_sem, (2,))
     with jax.named_scope("wait_y"):
         wait_y(0)
         wait_y(1)
-
-    bounds = tuple(N_STEP + PRE - STEP_BASE[2 * c] for c in range(N_CHUNK))
-
-    def second_chunk(k, lo):
+    with jax.named_scope("second_cross"):
+        lax.fori_loop(CROSS_PLACE // 2, STRIP_PLACE // 2, second_cross, 0)
+
+    def second_chunk(k, _):
         c = N_CHUNK - 1 - k
-        hi = table(bounds, c)
+        lo = STRIP_PLACE // 2 + 2 * k
         with jax.named_scope("second_chunk"):
-            lax.fori_loop(lo, hi, second_strip, 0)
-        finish_range(c, c + 1, SB2, RB2, s2_sem, r2_sem, (0, 1))
-        return hi
-
-    with jax.named_scope("second_last"):
-        lax.fori_loop(PRE + 2, PRE + 2 + STEPS[11], second_last, 0)
-    lo = lax.fori_loop(0, N_CHUNK, second_chunk, jnp.int32(PRE + 2 + STEPS[11]))
-    finish_range(0, N_CHUNK, SB2, RB2, s2_sem, r2_sem, (2,))
+            lax.fori_loop(lo, lo + 2, second_strip, 0)
+        finish_range(c, c + 1, SB2, RB2, s2_sem, r2_sem)
+        return 0
+
+    lax.fori_loop(0, N_CHUNK, second_chunk, 0)
 
     def final(k, _):
         c = N_CHUNK - 1 - k
@@ -480,7 +473,7 @@
             body,
             out_shape=(
                 jax.ShapeDtypeStruct((32, ROWS), F32),
-                jax.ShapeDtypeStruct((N_STEP, 2, UNITS, STRIP, CHUNK), BF16),
+                jax.ShapeDtypeStruct((N_PLACE, 2, UNITS, STRIP, CHUNK), BF16),
             ),
             in_specs=[hbm, hbm, smem, smem],
             out_specs=(pl.BlockSpec(memory_space=pltpu.VMEM), hbm),
@@ -499,7 +492,7 @@
                 pltpu.VMEM((3, 32, ROWS), F32),
                 pltpu.VMEM((2, UNITS, STRIP, CHUNK), BF16),
                 pltpu.VMEM((2, UNITS, STRIP, CHUNK), BF16),
-                pltpu.VMEM((4, 2, UNITS, STRIP, CHUNK), BF16),
+                pltpu.VMEM((4, 2, 2, UNITS, STRIP, CHUNK), BF16),
                 dma((2, N_STRIP)), dma((2, N_STRIP)),
                 dma((3,)), dma((3,)), dma((3,)), dma((3,)), dma, dma, dma((2,)),
                 dma((2, 2)), dma((4,)),

time: 171 us -> 160 us (0.936)
  Pallas kernels: 167 us -> 157 us
    pallas_call x1, Pallas kernels: 167 us -> 157 us  [local_program(): pl.pallas_call(body, out_shape=(jax.ShapeDtypeStruct((32, ROWS), F32), ja...]
where the time goes in v3:
time: 160 us
  Pallas kernels  157 us (98%)
  local copies, waits for them, and re-layouts  1.77 us (1%)
    pallas_call x1, Pallas kernels, local_program(): pl.pallas_call(body, out_shape=(jax.ShapeDtypeStruct((32, ROWS), F32), ja...  157 us

profile of v3, /device:TPU:0, one launch (start us, length us, event | category | flops | bytes accessed | tf_op | source)
XLA Modules:
  0.0 160.2 jit_solution(13873892428692578363)
XLA Ops:
  1.3 157.1 %products.1 = (f32[32,3072]{1,0:T(8,128)}, bf16[50,2,3,256,512]{4,3,2,1,0:T(8,128)(2,1)}) custom-call(bf16[3072,768]{1,0:T(8,128)(2,1)} %x_hbm.1, bf16[32,3072]{1,0:T(8,128)(2,1)} %bitcast.3, f32[1]{0:T(128)S(6)} %copy.6.ell_ref, f32[1]{0:T(128)S(6)} %copy.7.amp_ref), custom_call_target="tpu_custom_call" | custom-call | tf_op jit(solution)/shard_map/products/pallas_call | solution.py:472
  158.4 1.8 %copy.8 = f32[3072,32]{0,1:T(8,128)} copy(f32[3072,32]{0,1:T(8,128)} %bitcast.2) | data formatting | bytes 786432

commit v4 on v3

v4 whole, which is shorter than its diff:
```python
import functools

import jax
import jax.numpy as jnp
from jax import lax
from jax.experimental import pallas as pl
from jax.experimental.pallas import tpu as pltpu
from jax.sharding import PartitionSpec as P

MESH = pl.DeviceIdType.MESH
F32, BF16 = jnp.float32, jnp.bfloat16
LOG2E = 1.4426950408889634

ROWS = 3072
STRIP = 256
CHUNK = 512
N_STRIP = ROWS // STRIP
N_CHUNK = ROWS // CHUNK
UNITS = 3
OWN, XNB, YNB, PAR, TRASH = 0, 1, 2, 3, 4

N_OWN, N_PAIR, N_CROSS = 7, 13, 12
PRE = 5
OWN_AT = (5, 7, 9, 11, 12, 13, 13, 13, 13, 13, 13, 13)
CROSS_AT = (0, 0, 0, 0, 1, 2, 3, 4, 5, 6, 8, 10)
CROSS_TILE = (0, 0, 2, 4, 8, 12, 18, 24, 32, 40, 50, 60)
OWN_PLACE = (1, 2, 3, 4, 5, 48, 49, 6, 7, 44, 45, 46, 47)
CROSS_PLACE = 8
STRIP_PLACE = CROSS_PLACE + N_CROSS
N_PLACE = STRIP_PLACE + 2 * N_STRIP + 6
STEP_ROWS = 6 * STRIP
HALF_ROWS = UNITS * STRIP
Y_NEED = (4, 5, 6)


def table(values, n):
    out = jnp.int32(values[0])
    for i in range(1, len(values)):
        if values[i] != values[i - 1]:
            out = out + (values[i] - values[i - 1]) * (n >= i).astype(jnp.int32)
    return out


def rank(bounds, x):
    out = jnp.int32(0)
    for b in bounds:
        out = out + (x >= b).astype(jnp.int32)
    return out


def pick(cond, a, b):
    return tuple(jnp.where(cond, x, y) for x, y in zip(a, b))


def i32(*xs):
    return tuple(jnp.int32(x) for x in xs)


def own_tile(o, j, core):
    p = 3 * o + j // 2
    c = rank((1, 3, 6, 10, 15), p)
    i = p - ((c * (c + 1)) >> 1)
    own = (jnp.int32(OWN), 2 * i + j % 2, jnp.int32(OWN), c, jnp.where(i == c, TRASH, OWN))
    p = 3 * (o - N_OWN) + j // 2
    c = 1 + rank((1, 3, 6, 10), p)
    i = p - ((c * (c - 1)) >> 1)
    same = core + 2 * (j // 2)
    i, c = pick(p < 15, (i, c), (same, same))
    par = (jnp.int32(OWN), 2 * i + j % 2, jnp.int32(PAR), c, jnp.int32(PAR))
    return pick(o < N_OWN, own, par)


def strip_tile(n, side, j):
    return (1 + side, n, jnp.int32(OWN), jnp.int32(j), jnp.int32(OWN))


def cross_tile(q, j):
    g = 6 * q + j
    n = 1 + rank(CROSS_TILE[2:11], g)
    r = g - table(CROSS_TILE, n)
    m = n >> 1
    t = pick(r < m, (jnp.int32(XNB), n, jnp.int32(YNB), r, jnp.int32(YNB)), (jnp.int32(YNB), n, jnp.int32(XNB), r - m, jnp.int32(XNB)))
    return pick(r < 2 * m, t, (jnp.int32(XNB), n - 1 + (r - 2 * m), jnp.int32(YNB), m, jnp.int32(YNB)))


def last_tile(i, j):
    n = jnp.int32(N_STRIP - 1)
    s, t = (XNB, YNB) if j % 2 else (YNB, XNB)
    cross = (jnp.int32(s), n, jnp.int32(t), 3 * i + j // 2, jnp.int32(t))
    if j >= 4:
        cross = pick(i < 1, cross, (jnp.int32(XNB), jnp.int32(N_STRIP - 2 + j % 2), jnp.int32(YNB), jnp.int32(5), jnp.int32(YNB)))
    return cross


def rows_of(a):
    return pl.ds(pl.multiple_of(a * STRIP, STRIP), STRIP)


def sums_of(c):
    return pl.ds(pl.multiple_of(STRIP + c * CHUNK, STRIP), CHUNK)


def cols_of(b):
    return pl.ds(pl.multiple_of(b * CHUNK, CHUNK), CHUNK)


def body(
    x_hbm, v_hbm, ell_hbm, amp_hbm, out_ref, RB2, k_hbm,
    X, VT, YV, NA, NB, CR, YR, YT, SB, RB, SB2, kr0, kr1, KB, ell_ref, amp_ref,
    sx_sem, rx_sem, sv_sem, rv_sem, sn_sem, rn_sem, sp_sem, rp_sem, loc_sem, ko_sem, kb_sem, kx_sem,
    s1_sem, r1_sem, sy_sem, ry_sem, ryp_sem, s2_sem, r2_sem,
):
    me = lax.axis_index("row")
    core, cx, cy = me % 2, (me // 2) % 2, me // 4

    def dev(px, py, pc):
        return {"row": (py * 2 + px) * 2 + pc}

    tx = dev(1 - cx, cy, (core + 1 + cx) % 2)
    ty = dev(cx, 1 - cy, (core + 1 + cx + cy) % 2)
    sx = dev(1 - cx, cy, (core + cx) % 2)
    sy = dev(cx, 1 - cy, (core + cx + cy) % 2)
    pt = dev(cx, cy, 1 - core)

    def remote(src, dst, ss, rs, to):
        return pltpu.make_async_remote_copy(src_ref=src, dst_ref=dst, send_sem=ss, recv_sem=rs, device_id=to, device_id_type=MESH)

    def x_copy(j, n):
        return remote(x_hbm.at[rows_of(n)], X.at[1 + j, rows_of(n)], sx_sem.at[j], rx_sem.at[n], (tx, ty)[j])

    def wait_strip(n):
        two = X.at[1:3, rows_of(n)]
        remote(two, two, sx_sem.at[0], rx_sem.at[n], tx).wait_recv()

    p_copy = remote(x_hbm, X.at[PAR], sp_sem, rp_sem, pt)
    v_copies = [remote(v_hbm, VT.at[1 + j], sv_sem, rv_sem.at[j // 2], d) for j, d in enumerate((tx, ty, pt))]
    n_copies = [remote(NB.at[OWN], NB.at[1 + j], sn_sem, rn_sem.at[j // 2], d) for j, d in enumerate((tx, ty, pt))]

    x_loc = pltpu.make_async_copy(x_hbm, X.at[OWN], loc_sem.at[0])
    v_loc = pltpu.make_async_copy(v_hbm, VT.at[OWN], loc_sem.at[1])
    scalars = [pltpu.make_async_copy(src, dst, loc_sem.at[2 + i]) for i, (src, dst) in enumerate(((ell_hbm, ell_ref), (amp_hbm, amp_ref)))]
    for c in scalars + [v_loc, x_loc]:
        c.start()

    barrier = pltpu.get_barrier_semaphore()
    for d in (tx, ty, sx, sy, pt):
        pl.semaphore_signal(barrier, inc=1, device_id=d, device_id_type=MESH)
    with jax.named_scope("barrier"):
        pl.semaphore_wait(barrier, 5)

    for c in v_copies:
        c.start()
    for j in range(2):
        x_copy(j, 0).start()
    p_copy.start()

    for c in scalars:
        c.wait()
    ell = jnp.full((1, CHUNK), ell_ref[0], F32)
    half = LOG2E / (2.0 * ell * ell)
    top = jnp.log2(jnp.full((1, CHUNK), amp_ref[0], F32))
    CR[0:1, :] = 2.0 * half
    CR[1:2, :] = top
    h1, l1 = half[:, 0:128], top[:, 0:128]

    for s in range(3):
        YR[s] = jnp.zeros((STRIP + ROWS, 32), F32)
    for t in range(5):
        YT[t] = jnp.zeros((32, ROWS), F32)
    kr0[...] = jnp.zeros_like(kr0)
    kr1[...] = jnp.zeros_like(kr1)

    v_loc.wait()
    with jax.named_scope("x_local"):
        x_loc.wait()

    def own_norm(c, _):
        r = pl.ds(pl.multiple_of(c * CHUNK, CHUNK), CHUNK)
        x = X[OWN, r, :].astype(F32)
        n = jnp.broadcast_to(jnp.sum(x * x, axis=1, keepdims=True), (CHUNK, 128)) * h1
        NA[OWN, r, :] = l1 - n
        NB[OWN, :, cols_of(c)] = -jnp.transpose(n)[0:1, :]
        return 0

    with jax.named_scope("own_norm"):
        lax.fori_loop(0, N_CHUNK, own_norm, 0)
    for c in n_copies:
        c.start()

    def send_strip(n, _):
        for j in range(2):
            x_copy(j, n).start()
        return 0

    lax.fori_loop(1, N_STRIP, send_strip, 0)

    def left_norm(s):
        def one(c, _):
            r = pl.ds(pl.multiple_of(c * CHUNK, CHUNK), CHUNK)
            NA[s, r, :] = l1 + jnp.transpose(jnp.broadcast_to(NB[s, :, cols_of(c)], (128, CHUNK)))
            return 0

        lax.fori_loop(0, N_CHUNK, one, 0)

    def gram(tile):
        s, a, t, b, _ = tile
        return lax.dot_general(X[s, rows_of(a), :], X[t, cols_of(b), :], (((1,), (1,)), ((), ())), preferred_element_type=F32)

    def kern(tile, g):
        s, a, t, b, _ = tile
        na = NA[s, rows_of(a), :]
        e = (g * CR[0:1, :] + NB[t, :, cols_of(b)]) + jnp.concatenate([na] * (CHUNK // 128), axis=1)
        return jnp.exp2(jnp.minimum(e, CR[1:2, :])).astype(BF16)

    def apply(tile, k, vec):
        s, a, t, b, to = tile
        YR[s, rows_of(a + 1), :] += lax.dot_general(k, vec[t, :, cols_of(b)], (((1,), (1,)), ((), ())), preferred_element_type=F32)
        YT[to, :, cols_of(b)] += jnp.dot(vec[s, :, rows_of(jnp.maximum(a, 0))], k, preferred_element_type=F32)

    def k_out(seq, place, half):
        kr = (kr0, kr1)[half]
        row = pl.multiple_of(place * STEP_ROWS + half * HALF_ROWS, STRIP)
        return pltpu.make_async_copy(kr.at[seq & 1], k_hbm.at[pl.ds(row, HALF_ROWS)], ko_sem.at[seq & 1, half])

    def half_step(prev, cur, kr_new, d_new, kr_old, d_old):
        gs = [gram(t) for t in cur]
        for u in range(UNITS):
            apply(prev[u], kr_old[d_old, u * STRIP : (u + 1) * STRIP, :], VT)
        for u in range(UNITS):
            kr_new[d_new, u * STRIP : (u + 1) * STRIP, :] = kern(cur[u], gs[u])

    def flat(tiles):
        return tuple(x for t in tiles for x in t)

    def unflat(xs):
        return [tuple(xs[5 * u : 5 * u + 5]) for u in range(UNITS)]

    def step_of(state, place, tile):
        seq, before, prev = state[0], state[1], state[2:]
        d = seq & 1

        @pl.when(seq >= 2)
        def _():
            for h in range(2):
                k_out(seq, place, h).wait()

        @pl.when(seq >= 1)
        def _():
            for h in range(2):
                k_out(seq - 1, before, h).start()

        first = [tile(u) for u in range(UNITS)]
        second = [tile(UNITS + u) for u in range(UNITS)]
        half_step(unflat(prev), first, kr0, d, kr1, 1 - d)
        half_step(first, second, kr1, d, kr0, d)
        return (seq + 1, place) + flat(second)

    none = flat([i32(OWN, -1, OWN, 0, TRASH)] * UNITS)

    def flush(state):
        for u, t in enumerate(unflat(state[2:])):
            apply(t, kr1[(state[0] - 1) & 1, u * STRIP : (u + 1) * STRIP, :], VT)
        return state[:2] + none

    def own_step(o, state):
        place = table(OWN_PLACE, o)
        return step_of(state, place, lambda j: own_tile(o, j, core))

    def cross_step(q, state):
        return step_of(state, CROSS_PLACE + q, lambda j: cross_tile(q, j))

    def strip_step(n, side, state):
        return step_of(state, STRIP_PLACE + 2 * (N_STRIP - 1 - n) + side, lambda j: strip_tile(n, side, j))

    with jax.named_scope("pre"):
        state = lax.fori_loop(0, PRE, own_step, i32(0, 0) + none)

    with jax.named_scope("left_norm"):
        remote(VT.at[1:3], VT.at[1:3], sv_sem, rv_sem.at[0], tx).wait_recv()
        remote(NB.at[1:3], NB.at[1:3], sn_sem, rn_sem.at[0], tx).wait_recv()
        for j in range(2):
            left_norm(1 + j)
        p_copy.wait_recv()
        v_copies[2].wait_recv()
        n_copies[2].wait_recv()

    def strip(n, state):
        with jax.named_scope("wait_strip"):
            wait_strip(n)
        with jax.named_scope("strip"):
            state = lax.fori_loop(0, 2, lambda side, st: strip_step(n, side, st), state)
            state = lax.fori_loop(table(CROSS_AT, n), table(CROSS_AT, n + 1), cross_step, state)
            return lax.fori_loop(table(OWN_AT, n), table(OWN_AT, n + 1), own_step, state)

    state = lax.fori_loop(0, N_STRIP - 1, strip, state)

    homes = ((XNB, sx), (YNB, sy), (PAR, pt))

    def part_copy(j, c, send, recv, ss, rs):
        return remote(send.at[j, :, cols_of(c)], recv.at[j, :, cols_of(c)], ss, rs.at[c] if send is SB else rs, homes[j][1])

    def finish(j, c, send):
        s = homes[j][0]
        part = YT[s, :, cols_of(c)]
        if j < 2:
            part = part + jnp.transpose(YR[s, sums_of(c), :])
        send[j, :, cols_of(c)] = part
        if send is SB:
            YT[s, :, cols_of(c)] = jnp.zeros((32, CHUNK), F32)
            if j < 2:
                YR[s, sums_of(c), :] = jnp.zeros((CHUNK, 32), F32)

    def finish_range(lo, hi, send, recv, ss, rs, js=(0, 1)):
        def one(c, _):
            for j in js:
                finish(j, c, send)
            return 0

        lax.fori_loop(lo, hi, one, 0)
        send_range(lo, hi, send, recv, ss, rs, js)

    def send_range(lo, hi, send, recv, ss, rs, js=(0, 1)):
        def go(c, _):
            for j in js:
                part_copy(j, c, send, recv, ss, rs).start()
            return 0

        lax.fori_loop(lo, hi, go, 0)

    def load_kb(d, slot):
        return pltpu.make_async_copy(k_hbm.at[pl.ds(pl.multiple_of(d * 2 * STEP_ROWS, STRIP), 2 * STEP_ROWS)], KB.at[slot], kb_sem.at[slot])

    def load_x(d, slot):
        src = k_hbm.at[pl.ds(pl.multiple_of(d * 2 * STEP_ROWS, STRIP), 2 * STEP_ROWS)]
        return pltpu.make_async_copy(src, X.at[slot, :, 0:CHUNK], kx_sem.at[slot])

    first_in = pltpu.make_async_copy(k_hbm.at[pl.ds(STEP_ROWS, STEP_ROWS)], KB.at[0, pl.ds(STEP_ROWS, STEP_ROWS)], kb_sem.at[0])
    first_in.start()
    for i in range(1, 4):
        load_kb(i, i).start()

    finish_range(0, N_CHUNK, SB, RB, s1_sem, r1_sem, (2,))
    with jax.named_scope("wait_last"):
        wait_strip(N_STRIP - 1)

    last = jnp.int32(N_STRIP - 1)
    with jax.named_scope("last"):
        state = step_of(state, CROSS_PLACE + 10, lambda j: last_tile(jnp.int32(0), j))
        state = flush(state)
        finish_range(0, 3, SB, RB, s1_sem, r1_sem)
        state = step_of(state, CROSS_PLACE + 11, lambda j: last_tile(jnp.int32(1), j))
        finish_range(3, 4, SB, RB, s1_sem, r1_sem)
        state = strip_step(last, jnp.int32(0), state)
        finish_range(4, 5, SB, RB, s1_sem, r1_sem)
        state = strip_step(last, jnp.int32(1), state)
        for i in range(3):
            load_x(4 + 2 * i, i).start()
        state = flush(state)
        finish_range(5, 6, SB, RB, s1_sem, r1_sem)

    for h in range(2):
        k_out(state[0], 0, h).wait()
        k_out(state[0] - 1, state[1], h).start()

    def y_copy(j, c):
        return remote(YV.at[OWN, :, cols_of(c)], YV.at[1 + j, :, cols_of(c)], sy_sem, ryp_sem.at[c >> 2] if j == 2 else ry_sem.at[c], (tx, ty, pt)[j])

    def middle(lo, hi):
        def one(c, _):
            with jax.named_scope("wait_part"):
                three = RB.at[:, :, cols_of(c)]
                remote(three, three, s1_sem, r1_sem.at[c], pt).wait_recv()
            y = YT[OWN, :, cols_of(c)] + jnp.transpose(YR[OWN, sums_of(c), :])
            y = y + RB[0, :, cols_of(c)] + RB[1, :, cols_of(c)] + RB[2, :, cols_of(c)]
            YV[OWN, :, cols_of(c)] = y.astype(BF16)
            YT[OWN, :, cols_of(c)] = jnp.zeros((32, CHUNK), F32)
            YR[OWN, sums_of(c), :] = jnp.zeros((CHUNK, 32), F32)
            for j in range(3):
                y_copy(j, c).start()
            return 0

        lax.fori_loop(lo, hi, one, 0)

    def use(k, slot, tile):
        for h in range(2):
            for j in range(6):
                r = (6 * h + j) * STRIP
                apply(tile(h, j), k[slot, r : r + STRIP, 0:CHUNK], YV)

    def quad(t, tile, beside=None):
        slot = t & 3
        load_x(0, slot).wait()
        load_kb(0, slot).wait()

        @pl.when(jnp.logical_and(t >= 1, t <= 7))
        def _():
            load_x(10 + 2 * t, (t - 1) & 3).start()

        @pl.when(jnp.logical_and(t >= 1, t <= 6))
        def _():
            load_kb(11 + 2 * t, (t - 1) & 3).start()

        if beside is not None:
            beside()
        use(X, slot, lambda h, j: tile(0, h, j))
        use(KB, slot, lambda h, j: tile(1, h, j))

    def wait_y(lo, hi):
        def one(c, _):
            two = YV.at[1:3, :, cols_of(c)]
            remote(two, two, sy_sem, ry_sem.at[c], tx).wait_recv()
            return 0

        lax.fori_loop(lo, hi, one, 0)

    def wait_y_par(late):
        part = YV.at[PAR, :, pl.ds((0, 4)[late] * CHUNK, (4, 2)[late] * CHUNK)]
        remote(part, part, sy_sem, ryp_sem.at[late], pt).wait_recv()

    with jax.named_scope("middle"):
        middle(0, 4)
    with jax.named_scope("second_own"):
        first_in.wait()
        for j in range(6):
            apply(own_tile(jnp.int32(0), j, core), KB[0, STEP_ROWS + j * STRIP : STEP_ROWS + (j + 1) * STRIP, :], YV)
        load_kb(5, 0).start()

        def own_and_middle(i, _):
            load_kb(0, i).wait()
            use(KB, i, lambda h, j: own_tile(2 * i - 1 + h, j, core))
            load_kb(5 + 2 * i, i).start()
            middle(i + 3, i + 4)
            return 0

        lax.fori_loop(1, 3, own_and_middle, 0)
        for h in range(2):
            k_out(state[0] - 1, 0, h).wait()
        load_x(10, 3).start()
        wait_y_par(0)
        load_kb(0, 3).wait()
        use(KB, 3, lambda h, j: own_tile(jnp.int32(N_OWN + h), j, core))
        load_kb(11, 3).start()
    with jax.named_scope("second_cross"):

        def second_cross(t, _):
            with jax.named_scope("wait_y"):
                wait_y(table((0,) + Y_NEED[:-1], t), table(Y_NEED, t))

            def tile(d, h, j):
                q = 4 * t + 2 * d + h
                return pick(q < 10, cross_tile(q, j), last_tile(q - 10, j))

            quad(t, tile)
            return 0

        lax.fori_loop(0, 3, second_cross, 0)

    def second_chunk(k, _):
        done = N_CHUNK - jnp.maximum(k, 1)

        def beside():
            for j in range(2):
                finish(j, done, SB2)

        with jax.named_scope("second_chunk"):
            quad(3 + k, lambda d, h, j: strip_tile(2 * (N_CHUNK - 1 - k) + 1 - d, jnp.int32(h), j), beside)
        send_range(done, done + jnp.minimum(k, 1), SB2, RB2, s2_sem, r2_sem)
        return 0

    lax.fori_loop(0, N_CHUNK, second_chunk, 0)
    finish_range(0, 1, SB2, RB2, s2_sem, r2_sem)

    with jax.named_scope("second_par"):
        wait_y_par(1)
        quad(jnp.int32(9), lambda d, h, j: own_tile(jnp.int32(N_OWN + 2 + 2 * d + h), j, core))
        finish_range(0, N_CHUNK, SB2, RB2, s2_sem, r2_sem, (2,))

    with jax.named_scope("second_end"):
        load_x(0, 2).wait()
        use(X, 2, lambda h, j: own_tile(jnp.int32(5 + h), j, core))

    with jax.named_scope("sent"):
        p_copy.wait_send()
        for j in range(2):
            remote(x_hbm, X.at[1 + j], sx_sem.at[j], rx_sem.at[0], tx).wait_send()
        for buf, sem in ((VT, sv_sem), (NB, sn_sem), (YV, sy_sem)):
            remote(buf.at[1:4], buf.at[1:4], sem, rx_sem.at[0], tx).wait_send()
        remote(SB, RB, s1_sem, rx_sem.at[0], tx).wait_send()

    def final(c, _):
        out_ref[:, cols_of(c)] = YT[OWN, :, cols_of(c)] + jnp.transpose(YR[OWN, sums_of(c), :])
        return 0

    with jax.named_scope("final"):
        lax.fori_loop(0, N_CHUNK, final, 0)
        all_sums = remote(SB2, RB2, s2_sem, r2_sem, pt)
        all_sums.wait_send()
        all_sums.wait_recv()


def solution(mesh):
    def local_program(x_loc, v_loc, length_scale, out_scale):
        dma = pltpu.SemaphoreType.DMA
        hbm = pl.BlockSpec(memory_space=pltpu.HBM)
        vmem = pl.BlockSpec(memory_space=pltpu.VMEM)
        own, parts, _ = pl.pallas_call(
            body,
            out_shape=(
                pltpu.VMEM((32, ROWS), F32),
                pltpu.VMEM((3, 32, ROWS), F32),
                jax.ShapeDtypeStruct((N_PLACE * STEP_ROWS, CHUNK), BF16),
            ),
            in_specs=[hbm, hbm, hbm, hbm],
            out_specs=(vmem, vmem, hbm),
            scratch_shapes=[
                pltpu.VMEM((4, ROWS, 768), BF16),
                pltpu.VMEM((4, 32, ROWS), BF16),
                pltpu.VMEM((4, 32, ROWS), BF16),
                pltpu.VMEM((3, ROWS, 128), F32),
                pltpu.VMEM((4, 1, ROWS), F32),
                pltpu.VMEM((8, CHUNK), F32),
                pltpu.VMEM((3, STRIP + ROWS, 32), F32),
                pltpu.VMEM((5, 32, ROWS), F32),
                pltpu.VMEM((3, 32, ROWS), F32),
                pltpu.VMEM((3, 32, ROWS), F32),
                pltpu.VMEM((3, 32, ROWS), F32),
                pltpu.VMEM((2, HALF_ROWS, CHUNK), BF16),
                pltpu.VMEM((2, HALF_ROWS, CHUNK), BF16),
                pltpu.VMEM((4, 2 * STEP_ROWS, CHUNK), BF16),
                pltpu.SMEM((1,), F32), pltpu.SMEM((1,), F32),
                dma((2,)), dma((N_STRIP,)), dma, dma((2,)), dma, dma((2,)), dma, dma,
                dma((4,)), dma((2, 2)), dma((4,)), dma((4,)),
                dma, dma((N_CHUNK,)), dma, dma((N_CHUNK,)), dma((2,)), dma, dma,
            ],
            compiler_params=pltpu.CompilerParams(collective_id=0, has_side_effects=True, vmem_limit_bytes=56 * 2**20),
            name="products",
        )(x_loc, v_loc.T, length_scale, out_scale)
        return (own + parts[0] + parts[1] + parts[2]).T

    row_spec = P(("task", "row"), None)
    return jax.shard_map(local_program, mesh=mesh, in_specs=(row_spec, row_spec, P("task"), P("task")), out_specs=row_spec, check_vma=False)
```

time: 160 us -> 154 us (0.963)
  Pallas kernels: 157 us -> 152 us
  local copies, waits for them, and re-layouts: 1.77 us -> 0 us
    pallas_call x1, Pallas kernels: 157 us -> 152 us  [local_program(): pl.pallas_call(body, out_shape=(pltpu.VMEM((32, ROWS), F32), pltpu.VMEM((...]
    unnamed x1 -> x0, local copies, waits for them, and re-layouts: 1.77 us -> none
where the time goes in v4:
time: 154 us
  Pallas kernels  152 us (99%)
    pallas_call x1, Pallas kernels, local_program(): pl.pallas_call(body, out_shape=(pltpu.VMEM((32, ROWS), F32), pltpu.VMEM((...  152 us

profile of v4, /device:TPU:0, one launch (start us, length us, event | category | flops | bytes accessed | tf_op | source)
XLA Modules:
  0.0 153.7 jit_solution(4837989387307042820)
XLA Ops:
  1.3 151.6 %products.1 = (f32[32,3072]{1,0:T(8,128)S(1)}, f32[3,32,3072]{2,1,0:T(8,128)S(1)}, bf16[76800,512]{1,0:T(8,128)(2,1)}) custom-call(bf16[3072,768]{1,0:T(8,128)(2,1)} %x_hbm.1, bf16[32,3072]{1,0:T(8,128)(2,1)} %bitcast.15, f32[1]{0:T(128)S(6)} %copy.5.ell_hbm, f32[1]{0:T(128)S(6)} %copy.6.amp_hbm), custom_call_target="tpu_custom_call" | custom-call | tf_op jit(solution)/shard_map/products/pallas_call | solution.py:506
  152.9 0.8 fusion

commit v5 on v4

--- a/solution.py
+++ b/solution.py
@@ -25,9 +25,9 @@
 CROSS_AT = (0, 0, 0, 0, 1, 2, 3, 4, 5, 6, 8, 10)
 CROSS_TILE = (0, 0, 2, 4, 8, 12, 18, 24, 32, 40, 50, 60)
 OWN_PLACE = (1, 2, 3, 4, 5, 48, 49, 6, 7, 44, 45, 46, 47)
-CROSS_PLACE = 8
-STRIP_PLACE = CROSS_PLACE + N_CROSS
-N_PLACE = STRIP_PLACE + 2 * N_STRIP + 6
+STRIP_PLACE = tuple(10 - 2 * n if n < 2 else 46 - 2 * n for n in range(N_STRIP))
+CROSS_PLACE = 12
+N_PLACE = 50
 STEP_ROWS = 6 * STRIP
 HALF_ROWS = UNITS * STRIP
 Y_NEED = (4, 5, 6)
@@ -270,7 +270,7 @@
         return step_of(state, CROSS_PLACE + q, lambda j: cross_tile(q, j))
 
     def strip_step(n, side, state):
-        return step_of(state, STRIP_PLACE + 2 * (N_STRIP - 1 - n) + side, lambda j: strip_tile(n, side, j))
+        return step_of(state, table(STRIP_PLACE, n) + side, lambda j: strip_tile(n, side, j))
 
     with jax.named_scope("pre"):
         state = lax.fori_loop(0, PRE, own_step, i32(0, 0) + none)
@@ -353,7 +353,7 @@
         state = strip_step(last, jnp.int32(0), state)
         finish_range(4, 5, SB, RB, s1_sem, r1_sem)
         state = strip_step(last, jnp.int32(1), state)
-        for i in range(3):
+        for i in range(4):
             load_x(4 + 2 * i, i).start()
         state = flush(state)
         finish_range(5, 6, SB, RB, s1_sem, r1_sem)
@@ -418,12 +418,13 @@
         remote(part, part, sy_sem, ryp_sem.at[late], pt).wait_recv()
 
     with jax.named_scope("middle"):
-        middle(0, 4)
+        middle(0, 3)
     with jax.named_scope("second_own"):
         first_in.wait()
         for j in range(6):
             apply(own_tile(jnp.int32(0), j, core), KB[0, STEP_ROWS + j * STRIP : STEP_ROWS + (j + 1) * STRIP, :], YV)
         load_kb(5, 0).start()
+        middle(3, 4)
 
         def own_and_middle(i, _):
             load_kb(0, i).wait()
@@ -435,45 +436,68 @@
         lax.fori_loop(1, 3, own_and_middle, 0)
         for h in range(2):
             k_out(state[0] - 1, 0, h).wait()
-        load_x(10, 3).start()
         wait_y_par(0)
         load_kb(0, 3).wait()
         use(KB, 3, lambda h, j: own_tile(jnp.int32(N_OWN + h), j, core))
         load_kb(11, 3).start()
+    def strip_quad(c):
+        return lambda d, h, j: strip_tile(2 * c + 1 - d, jnp.int32(h), j)
+
+    with jax.named_scope("second_first"):
+        wait_y(0, 1)
+        quad(jnp.int32(0), strip_quad(jnp.int32(0)))
     with jax.named_scope("second_cross"):
 
         def second_cross(t, _):
             with jax.named_scope("wait_y"):
-                wait_y(table((0,) + Y_NEED[:-1], t), table(Y_NEED, t))
+                wait_y(table((1, 1) + Y_NEED[:-1], t), table((1,) + Y_NEED, t))
 
             def tile(d, h, j):
-                q = 4 * t + 2 * d + h
+                q = 4 * (t - 1) + 2 * d + h
                 return pick(q < 10, cross_tile(q, j), last_tile(q - 10, j))
 
             quad(t, tile)
             return 0
 
-        lax.fori_loop(0, 3, second_cross, 0)
+        lax.fori_loop(1, 4, second_cross, 0)
 
     def second_chunk(k, _):
-        done = N_CHUNK - jnp.maximum(k, 1)
+        done = jnp.where(k == 0, 0, N_CHUNK - k)
 
         def beside():
             for j in range(2):
                 finish(j, done, SB2)
 
         with jax.named_scope("second_chunk"):
-            quad(3 + k, lambda d, h, j: strip_tile(2 * (N_CHUNK - 1 - k) + 1 - d, jnp.int32(h), j), beside)
-        send_range(done, done + jnp.minimum(k, 1), SB2, RB2, s2_sem, r2_sem)
+            quad(4 + k, strip_quad(N_CHUNK - 1 - k), beside)
+        send_range(done, done + 1, SB2, RB2, s2_sem, r2_sem)
         return 0
 
-    lax.fori_loop(0, N_CHUNK, second_chunk, 0)
-    finish_range(0, 1, SB2, RB2, s2_sem, r2_sem)
+    lax.fori_loop(0, N_CHUNK - 2, second_chunk, 0)
+
+    def finish_strip(n):
+        cols = pl.ds(n * STRIP, STRIP)
+        for j in range(2):
+            s = homes[j][0]
+            SB2[j, :, cols] = YT[s, :, cols] + jnp.transpose(YR[s, pl.ds((n + 1) * STRIP, STRIP), :])
+        for j in range(2):
+            remote(SB2.at[j, :, cols], RB2.at[j, :, cols], s2_sem, r2_sem, homes[j][1]).start()
+
+    with jax.named_scope("second_chunk"):
+        load_x(0, 0).wait()
+        load_kb(0, 0).wait()
+        for j in range(2):
+            finish(j, 2, SB2)
+        use(X, 0, lambda h, j: strip_tile(jnp.int32(3), jnp.int32(h), j))
+        send_range(2, 3, SB2, RB2, s2_sem, r2_sem)
+        finish_strip(3)
+        use(KB, 0, lambda h, j: strip_tile(jnp.int32(2), jnp.int32(h), j))
+        finish_strip(2)
 
     with jax.named_scope("second_par"):
         wait_y_par(1)
         quad(jnp.int32(9), lambda d, h, j: own_tile(jnp.int32(N_OWN + 2 + 2 * d + h), j, core))
-        finish_range(0, N_CHUNK, SB2, RB2, s2_sem, r2_sem, (2,))
+        remote(YT.at[PAR], RB2.at[2], s2_sem, r2_sem, pt).start()
 
     with jax.named_scope("second_end"):
         load_x(0, 2).wait()

time: 154 us -> 152 us (0.987)
  Pallas kernels: 152 us -> 150 us
    pallas_call x1, Pallas kernels: 152 us -> 150 us  [local_program(): pl.pallas_call(body, out_shape=(pltpu.VMEM((32, ROWS), F32), pltpu.VMEM((...]
where the time goes in v5:
time: 152 us
  Pallas kernels  150 us (99%)
    pallas_call x1, Pallas kernels, local_program(): pl.pallas_call(body, out_shape=(pltpu.VMEM((32, ROWS), F32), pltpu.VMEM((...  150 us

profile of v5, /device:TPU:0, one launch (start us, length us, event | category | flops | bytes accessed | tf_op | source)
XLA Modules:
  0.0 152.1 jit_solution(5128870119550681421)
XLA Ops:
  1.3 150.0 %products.1 = (f32[32,3072]{1,0:T(8,128)S(1)}, f32[3,32,3072]{2,1,0:T(8,128)S(1)}, bf16[76800,512]{1,0:T(8,128)(2,1)}) custom-call(bf16[3072,768]{1,0:T(8,128)(2,1)} %x_hbm.1, bf16[32,3072]{1,0:T(8,128)(2,1)} %bitcast.15, f32[1]{0:T(128)S(6)} %copy.5.ell_hbm, f32[1]{0:T(128)S(6)} %copy.6.amp_hbm), custom_call_target="tpu_custom_call" | custom-call | tf_op jit(solution)/shard_map/products/pallas_call | solution.py:530
  151.3 0.8 fusion

commit v6 on v5

--- a/solution.py
+++ b/solution.py
@@ -353,8 +353,7 @@
         state = strip_step(last, jnp.int32(0), state)
         finish_range(4, 5, SB, RB, s1_sem, r1_sem)
         state = strip_step(last, jnp.int32(1), state)
-        for i in range(4):
-            load_x(4 + 2 * i, i).start()
+        load_x(4, 0).start()
         state = flush(state)
         finish_range(5, 6, SB, RB, s1_sem, r1_sem)
 
@@ -418,19 +417,20 @@
         remote(part, part, sy_sem, ryp_sem.at[late], pt).wait_recv()
 
     with jax.named_scope("middle"):
-        middle(0, 3)
+        middle(0, 2)
     with jax.named_scope("second_own"):
         first_in.wait()
         for j in range(6):
             apply(own_tile(jnp.int32(0), j, core), KB[0, STEP_ROWS + j * STRIP : STEP_ROWS + (j + 1) * STRIP, :], YV)
         load_kb(5, 0).start()
-        middle(3, 4)
+        middle(2, 4)
 
         def own_and_middle(i, _):
             load_kb(0, i).wait()
             use(KB, i, lambda h, j: own_tile(2 * i - 1 + h, j, core))
+            load_x(4 + 2 * i, i).start()
             load_kb(5 + 2 * i, i).start()
-            middle(i + 3, i + 4)
+            middle(i + 3, 5)
             return 0
 
         lax.fori_loop(1, 3, own_and_middle, 0)
@@ -439,7 +439,9 @@
         wait_y_par(0)
         load_kb(0, 3).wait()
         use(KB, 3, lambda h, j: own_tile(jnp.int32(N_OWN + h), j, core))
+        load_x(10, 3).start()
         load_kb(11, 3).start()
+        middle(5, 6)
     def strip_quad(c):
         return lambda d, h, j: strip_tile(2 * c + 1 - d, jnp.int32(h), j)
 

time: 152 us -> 152 us (level)
  no operation moved by 1% of the time
where the time goes in v6:
time: 152 us; the launch traced here: 151 us
  Pallas kernels  149 us (98%)
    pallas_call x1, Pallas kernels, local_program(): pl.pallas_call(body, out_shape=(pltpu.VMEM((32, ROWS), F32), pltpu.VMEM((...  149 us

profile of v6, /device:TPU:0, one launch (start us, length us, event | category | flops | bytes accessed | tf_op | source)
XLA Modules:
  0.0 151.5 jit_solution(5584000926279553076)
XLA Ops:
  1.3 149.4 %products.1 = (f32[32,3072]{1,0:T(8,128)S(1)}, f32[3,32,3072]{2,1,0:T(8,128)S(1)}, bf16[76800,512]{1,0:T(8,128)(2,1)}) custom-call(bf16[3072,768]{1,0:T(8,128)(2,1)} %x_hbm.1, bf16[32,3072]{1,0:T(8,128)(2,1)} %bitcast.15, f32[1]{0:T(128)S(6)} %copy.5.ell_hbm, f32[1]{0:T(128)S(6)} %copy.6.amp_hbm), custom_call_target="tpu_custom_call" | custom-call | tf_op jit(solution)/shard_map/products/pallas_call | solution.py:532
  150.7 0.8 fusion

commit v7 on v6

--- a/solution.py
+++ b/solution.py
@@ -92,16 +92,20 @@
     return cross
 
 
+def span(start, size, unit):
+    return pl.ds(start if isinstance(start, int) else pl.multiple_of(start, unit), size)
+
+
 def rows_of(a):
-    return pl.ds(pl.multiple_of(a * STRIP, STRIP), STRIP)
+    return span(a * STRIP, STRIP, STRIP)
 
 
 def sums_of(c):
-    return pl.ds(pl.multiple_of(STRIP + c * CHUNK, STRIP), CHUNK)
+    return span(STRIP + c * CHUNK, CHUNK, STRIP)
 
 
 def cols_of(b):
-    return pl.ds(pl.multiple_of(b * CHUNK, CHUNK), CHUNK)
+    return span(b * CHUNK, CHUNK, CHUNK)
 
 
 def body(
@@ -316,8 +320,10 @@
                 finish(j, c, send)
             return 0
 
-        lax.fori_loop(lo, hi, one, 0)
-        send_range(lo, hi, send, recv, ss, rs, js)
+        for c in range(lo, hi):
+            one(c, 0)
+            for j in js:
+                part_copy(j, c, send, recv, ss, rs).start()
 
     def send_range(lo, hi, send, recv, ss, rs, js=(0, 1)):
         def go(c, _):
@@ -346,8 +352,9 @@
     last = jnp.int32(N_STRIP - 1)
     with jax.named_scope("last"):
         state = step_of(state, CROSS_PLACE + 10, lambda j: last_tile(jnp.int32(0), j))
+        finish_range(0, 1, SB, RB, s1_sem, r1_sem)
         state = flush(state)
-        finish_range(0, 3, SB, RB, s1_sem, r1_sem)
+        finish_range(1, 3, SB, RB, s1_sem, r1_sem)
         state = step_of(state, CROSS_PLACE + 11, lambda j: last_tile(jnp.int32(1), j))
         finish_range(3, 4, SB, RB, s1_sem, r1_sem)
         state = strip_step(last, jnp.int32(0), state)
@@ -382,9 +389,12 @@
 
     def use(k, slot, tile):
         for h in range(2):
-            for j in range(6):
-                r = (6 * h + j) * STRIP
-                apply(tile(h, j), k[slot, r : r + STRIP, 0:CHUNK], YV)
+            use_step(k, slot, h, functools.partial(tile, h))
+
+    def use_step(k, slot, h, tile):
+        for j in range(6):
+            r = (6 * h + j) * STRIP
+            apply(tile(j), k[slot, r : r + STRIP, 0:CHUNK], YV)
 
     def quad(t, tile, beside=None):
         slot = t & 3
@@ -423,17 +433,18 @@
         for j in range(6):
             apply(own_tile(jnp.int32(0), j, core), KB[0, STEP_ROWS + j * STRIP : STEP_ROWS + (j + 1) * STRIP, :], YV)
         load_kb(5, 0).start()
-        middle(2, 4)
-
-        def own_and_middle(i, _):
-            load_kb(0, i).wait()
-            use(KB, i, lambda h, j: own_tile(2 * i - 1 + h, j, core))
-            load_x(4 + 2 * i, i).start()
-            load_kb(5 + 2 * i, i).start()
-            middle(i + 3, 5)
-            return 0
-
-        lax.fori_loop(1, 3, own_and_middle, 0)
+        middle(2, 3)
+        load_kb(0, 1).wait()
+        use_step(KB, 1, 0, lambda j: own_tile(jnp.int32(1), j, core))
+        middle(3, 4)
+        use_step(KB, 1, 1, lambda j: own_tile(jnp.int32(2), j, core))
+        load_x(6, 1).start()
+        load_kb(7, 1).start()
+        middle(4, 5)
+        load_kb(0, 2).wait()
+        use(KB, 2, lambda h, j: own_tile(jnp.int32(3 + h), j, core))
+        load_x(8, 2).start()
+        load_kb(9, 2).start()
         for h in range(2):
             k_out(state[0] - 1, 0, h).wait()
         wait_y_par(0)
@@ -518,7 +529,8 @@
         return 0
 
     with jax.named_scope("final"):
-        lax.fori_loop(0, N_CHUNK, final, 0)
+        for c in range(N_CHUNK):
+            final(c, 0)
         all_sums = remote(SB2, RB2, s2_sem, r2_sem, pt)
         all_sums.wait_send()
         all_sums.wait_recv()

time: 152 us -> 151 us (level)
  no operation moved by 1% of the time
where the time goes in v7:
time: 151 us
  Pallas kernels  149 us (99%)
    pallas_call x1, Pallas kernels, local_program(): pl.pallas_call(body, out_shape=(pltpu.VMEM((32, ROWS), F32), pltpu.VMEM((...  149 us

profile of v7, /device:TPU:0, one launch (start us, length us, event | category | flops | bytes accessed | tf_op | source)
XLA Modules:
  0.0 150.9 jit_solution(8833822986200117665)
XLA Ops:
  1.3 148.8 %products.1 = (f32[32,3072]{1,0:T(8,128)S(1)}, f32[3,32,3072]{2,1,0:T(8,128)S(1)}, bf16[76800,512]{1,0:T(8,128)(2,1)}) custom-call(bf16[3072,768]{1,0:T(8,128)(2,1)} %x_hbm.1, bf16[32,3072]{1,0:T(8,128)(2,1)} %bitcast.15, f32[1]{0:T(128)S(6)} %copy.5.ell_hbm, f32[1]{0:T(128)S(6)} %copy.6.amp_hbm), custom_call_target="tpu_custom_call" | custom-call | tf_op jit(solution)/shard_map/products/pallas_call | solution.py:544
  150.1 0.8 fusion

commit v8 on v7

--- a/solution.py
+++ b/solution.py
@@ -19,13 +19,14 @@
 UNITS = 3
 OWN, XNB, YNB, PAR, TRASH = 0, 1, 2, 3, 4
 
-N_OWN, N_PAIR, N_CROSS = 7, 13, 12
-PRE = 5
-OWN_AT = (5, 7, 9, 11, 12, 13, 13, 13, 13, 13, 13, 13)
+N_OWN, N_PAIR = 7, 13
+REMOTE_AT = (0, 0, 7, 7, 13, 13, 18, 18, 21, 21, 23, 23)
+REMOTE_TILE = (0, 44, 80, 108, 128, 140)
 CROSS_AT = (0, 0, 0, 0, 1, 2, 3, 4, 5, 6, 8, 10)
 CROSS_TILE = (0, 0, 2, 4, 8, 12, 18, 24, 32, 40, 50, 60)
-OWN_PLACE = (1, 2, 3, 4, 5, 48, 49, 6, 7, 44, 45, 46, 47)
-STRIP_PLACE = tuple(10 - 2 * n if n < 2 else 46 - 2 * n for n in range(N_STRIP))
+OWN_PLACE = (1, 2, 3, 6, 7, 48, 49, 4, 5, 44, 45, 46, 47)
+REMOTE_ORDER = (20, 21, 22, 23, 16, 17, 18, 19, 10, 13, 14, 15, 4, 5, 6, 7, 8, 9, 11, 12)
+REMOTE_PLACE = tuple(8 + p if p < 4 else 24 + REMOTE_ORDER.index(p) for p in range(24))
 CROSS_PLACE = 12
 N_PLACE = 50
 STEP_ROWS = 6 * STRIP
@@ -70,8 +71,17 @@
     return pick(o < N_OWN, own, par)
 
 
-def strip_tile(n, side, j):
-    return (1 + side, n, jnp.int32(OWN), jnp.int32(j), jnp.int32(OWN))
+def remote_tile(p, j):
+    g = 6 * p + j
+    d, first = jnp.int32(0), jnp.int32(0)
+    for i in range(1, N_CHUNK):
+        d, first = pick(g >= REMOTE_TILE[i], (i, REMOTE_TILE[i]), (d, first))
+    r = g - first
+    rest = r - (22 - 4 * d)
+    k, side, odd = pick(rest >= 0, (rest >> 1, r & 1, 1), (r >> 1, r & 1, 0))
+    k, side, odd = pick(d == 0, (r >> 2, (r >> 1) & 1, r & 1), (k, side, odd))
+    t = jnp.where((k & 1) == (k > 0).astype(jnp.int32), OWN, PAR)
+    return (1 + side, 2 * d + odd, t, d + ((k + 1) >> 1), t)
 
 
 def cross_tile(q, j):
@@ -83,13 +93,11 @@
     return pick(r < 2 * m, t, (jnp.int32(XNB), n - 1 + (r - 2 * m), jnp.int32(YNB), m, jnp.int32(YNB)))
 
 
-def last_tile(i, j):
-    n = jnp.int32(N_STRIP - 1)
-    s, t = (XNB, YNB) if j % 2 else (YNB, XNB)
-    cross = (jnp.int32(s), n, jnp.int32(t), 3 * i + j // 2, jnp.int32(t))
-    if j >= 4:
-        cross = pick(i < 1, cross, (jnp.int32(XNB), jnp.int32(N_STRIP - 2 + j % 2), jnp.int32(YNB), jnp.int32(5), jnp.int32(YNB)))
-    return cross
+def last_tiles():
+    n = N_STRIP - 1
+    tiles = [t for c in range(N_CHUNK - 1) for t in ((YNB, n, XNB, c, XNB), (XNB, n, YNB, c, YNB))]
+    tiles += [(XNB, n - 1, YNB, N_CHUNK - 1, YNB), (XNB, n, YNB, N_CHUNK - 1, YNB)]
+    return [i32(*t) for t in tiles]
 
 
 def span(start, size, unit):
@@ -110,7 +118,7 @@
 
 def body(
     x_hbm, v_hbm, ell_hbm, amp_hbm, out_ref, RB2, k_hbm,
-    X, VT, YV, NA, NB, CR, YR, YT, SB, RB, SB2, kr0, kr1, KB, ell_ref, amp_ref,
+    X, VT, YV, NA, NB, CR, YR, YT, SB, RB, SB2, kr0, kr1, KL, KB, ell_ref, amp_ref,
     sx_sem, rx_sem, sv_sem, rv_sem, sn_sem, rn_sem, sp_sem, rp_sem, loc_sem, ko_sem, kb_sem, kx_sem,
     s1_sem, r1_sem, sy_sem, ry_sem, ryp_sem, s2_sem, r2_sem,
 ):
@@ -239,10 +247,7 @@
     def unflat(xs):
         return [tuple(xs[5 * u : 5 * u + 5]) for u in range(UNITS)]
 
-    def step_of(state, place, tile):
-        seq, before, prev = state[0], state[1], state[2:]
-        d = seq & 1
-
+    def begin(seq, before, place):
         @pl.when(seq >= 2)
         def _():
             for h in range(2):
@@ -253,6 +258,11 @@
             for h in range(2):
                 k_out(seq - 1, before, h).start()
 
+        return seq & 1
+
+    def step_of(state, place, tile):
+        seq, before, prev = state[0], state[1], state[2:]
+        d = begin(seq, before, place)
         first = [tile(u) for u in range(UNITS)]
         second = [tile(UNITS + u) for u in range(UNITS)]
         half_step(unflat(prev), first, kr0, d, kr1, 1 - d)
@@ -261,40 +271,36 @@
 
     none = flat([i32(OWN, -1, OWN, 0, TRASH)] * UNITS)
 
-    def flush(state):
-        for u, t in enumerate(unflat(state[2:])):
-            apply(t, kr1[(state[0] - 1) & 1, u * STRIP : (u + 1) * STRIP, :], VT)
-        return state[:2] + none
-
     def own_step(o, state):
-        place = table(OWN_PLACE, o)
-        return step_of(state, place, lambda j: own_tile(o, j, core))
+        @pl.when(o == N_OWN)
+        def _():
+            p_copy.wait_recv()
+            v_copies[2].wait_recv()
+            n_copies[2].wait_recv()
+
+        return step_of(state, table(OWN_PLACE, o), lambda j: own_tile(o, j, core))
+
+    def remote_step(p, state):
+        return step_of(state, table(REMOTE_PLACE, p), lambda j: remote_tile(p, j))
 
     def cross_step(q, state):
         return step_of(state, CROSS_PLACE + q, lambda j: cross_tile(q, j))
 
-    def strip_step(n, side, state):
-        return step_of(state, table(STRIP_PLACE, n) + side, lambda j: strip_tile(n, side, j))
-
     with jax.named_scope("pre"):
-        state = lax.fori_loop(0, PRE, own_step, i32(0, 0) + none)
+        state = lax.fori_loop(0, N_PAIR, own_step, i32(0, 0) + none)
 
     with jax.named_scope("left_norm"):
         remote(VT.at[1:3], VT.at[1:3], sv_sem, rv_sem.at[0], tx).wait_recv()
         remote(NB.at[1:3], NB.at[1:3], sn_sem, rn_sem.at[0], tx).wait_recv()
         for j in range(2):
             left_norm(1 + j)
-        p_copy.wait_recv()
-        v_copies[2].wait_recv()
-        n_copies[2].wait_recv()
 
     def strip(n, state):
         with jax.named_scope("wait_strip"):
             wait_strip(n)
         with jax.named_scope("strip"):
-            state = lax.fori_loop(0, 2, lambda side, st: strip_step(n, side, st), state)
-            state = lax.fori_loop(table(CROSS_AT, n), table(CROSS_AT, n + 1), cross_step, state)
-            return lax.fori_loop(table(OWN_AT, n), table(OWN_AT, n + 1), own_step, state)
+            state = lax.fori_loop(table(REMOTE_AT, n), table(REMOTE_AT, n + 1), remote_step, state)
+            return lax.fori_loop(table(CROSS_AT, n), table(CROSS_AT, n + 1), cross_step, state)
 
     state = lax.fori_loop(0, N_STRIP - 1, strip, state)
 
@@ -345,31 +351,8 @@
     for i in range(1, 4):
         load_kb(i, i).start()
 
-    finish_range(0, N_CHUNK, SB, RB, s1_sem, r1_sem, (2,))
-    with jax.named_scope("wait_last"):
-        wait_strip(N_STRIP - 1)
-
-    last = jnp.int32(N_STRIP - 1)
-    with jax.named_scope("last"):
-        state = step_of(state, CROSS_PLACE + 10, lambda j: last_tile(jnp.int32(0), j))
-        finish_range(0, 1, SB, RB, s1_sem, r1_sem)
-        state = flush(state)
-        finish_range(1, 3, SB, RB, s1_sem, r1_sem)
-        state = step_of(state, CROSS_PLACE + 11, lambda j: last_tile(jnp.int32(1), j))
-        finish_range(3, 4, SB, RB, s1_sem, r1_sem)
-        state = strip_step(last, jnp.int32(0), state)
-        finish_range(4, 5, SB, RB, s1_sem, r1_sem)
-        state = strip_step(last, jnp.int32(1), state)
-        load_x(4, 0).start()
-        state = flush(state)
-        finish_range(5, 6, SB, RB, s1_sem, r1_sem)
-
-    for h in range(2):
-        k_out(state[0], 0, h).wait()
-        k_out(state[0] - 1, state[1], h).start()
-
     def y_copy(j, c):
-        return remote(YV.at[OWN, :, cols_of(c)], YV.at[1 + j, :, cols_of(c)], sy_sem, ryp_sem.at[c >> 2] if j == 2 else ry_sem.at[c], (tx, ty, pt)[j])
+        return remote(YV.at[OWN, :, cols_of(c)], YV.at[1 + j, :, cols_of(c)], sy_sem, ryp_sem.at[(c >= 3).astype(jnp.int32) + (c >= 4).astype(jnp.int32)] if j == 2 else ry_sem.at[c], (tx, ty, pt)[j])
 
     def middle(lo, hi):
         def one(c, _):
@@ -387,6 +370,62 @@
 
         lax.fori_loop(lo, hi, one, 0)
 
+    last = last_tiles()
+    late = [remote_tile(jnp.int32(23), j) for j in range(6)]
+
+    def rows_in(u, d):
+        if d is None:
+            return KL, (slice(u * STRIP, (u + 1) * STRIP), slice(None))
+        return (kr0, kr1)[u % 6 // UNITS], (d, slice(u % UNITS * STRIP, (u % UNITS + 1) * STRIP), slice(None))
+
+    def grams(tiles, first, d):
+        gs = [gram(t) for t in tiles]
+
+        def put():
+            for u, (t, g) in enumerate(zip(tiles, gs), first):
+                ref, at = rows_in(u, d)
+                ref[at] = kern(t, g)
+
+        return put
+
+    def applies(tiles, first, d):
+        for u, t in enumerate(tiles, first):
+            ref, at = rows_in(u, d)
+            apply(t, ref[at], VT)
+
+    kl_out = pltpu.make_async_copy(KL, k_hbm.at[pl.ds(REMOTE_PLACE[23] * STEP_ROWS, STEP_ROWS)], loc_sem.at[0])
+    seq, before, due = state[0], state[1], unflat(state[2:])
+    d = begin(seq, before, before)
+    put = grams(late[0:2], 0, None)
+    applies(due, UNITS, 1 - d)
+    put()
+    applies(late[0:2], 0, None)
+    finish_range(0, N_CHUNK, SB, RB, s1_sem, r1_sem, (2,))
+    with jax.named_scope("wait_last"):
+        wait_strip(N_STRIP - 1)
+    with jax.named_scope("last"):
+        for c in range(N_CHUNK):
+            if c == 3:
+                d = begin(seq + 1, jnp.int32(CROSS_PLACE + 10), before)
+            put = grams(last[2 * c : 2 * c + 2], 2 * c, d)
+            if c > 0:
+                applies(last[2 * c - 2 : 2 * c], 2 * c - 2, 1 - d if c == 3 else d)
+            put()
+            if c > 0:
+                finish_range(c - 1, c, SB, RB, s1_sem, r1_sem)
+        put = grams(late[2:6], 2, None)
+        applies(last[10:12], 10, d)
+        put()
+        kl_out.start()
+        load_x(4, 0).start()
+        middle(0, 1)
+        applies(late[2:6], 2, None)
+        finish_range(5, 6, SB, RB, s1_sem, r1_sem)
+
+    for h in range(2):
+        k_out(seq, 0, h).wait()
+        k_out(seq + 1, CROSS_PLACE + 11, h).start()
+
     def use(k, slot, tile):
         for h in range(2):
             use_step(k, slot, h, functools.partial(tile, h))
@@ -423,11 +462,11 @@
         lax.fori_loop(lo, hi, one, 0)
 
     def wait_y_par(late):
-        part = YV.at[PAR, :, pl.ds((0, 4)[late] * CHUNK, (4, 2)[late] * CHUNK)]
+        part = YV.at[PAR, :, pl.ds((0, 3, 4)[late] * CHUNK, (3, 1, 2)[late] * CHUNK)]
         remote(part, part, sy_sem, ryp_sem.at[late], pt).wait_recv()
 
     with jax.named_scope("middle"):
-        middle(0, 2)
+        middle(1, 2)
     with jax.named_scope("second_own"):
         first_in.wait()
         for j in range(6):
@@ -436,29 +475,34 @@
         middle(2, 3)
         load_kb(0, 1).wait()
         use_step(KB, 1, 0, lambda j: own_tile(jnp.int32(1), j, core))
+        wait_y_par(0)
+        load_kb(0, 2).wait()
+        use_step(KB, 2, 0, lambda j: own_tile(jnp.int32(N_OWN), j, core))
         middle(3, 4)
         use_step(KB, 1, 1, lambda j: own_tile(jnp.int32(2), j, core))
         load_x(6, 1).start()
         load_kb(7, 1).start()
-        middle(4, 5)
-        load_kb(0, 2).wait()
-        use(KB, 2, lambda h, j: own_tile(jnp.int32(3 + h), j, core))
+        wait_y_par(1)
+        use_step(KB, 2, 1, lambda j: own_tile(jnp.int32(N_OWN + 1), j, core))
         load_x(8, 2).start()
         load_kb(9, 2).start()
+        middle(4, 5)
+        load_kb(0, 3).wait()
+        use(KB, 3, lambda h, j: own_tile(jnp.int32(3 + h), j, core))
+        load_x(10, 3).start()
+        kl_out.wait()
         for h in range(2):
-            k_out(state[0] - 1, 0, h).wait()
-        wait_y_par(0)
-        load_kb(0, 3).wait()
-        use(KB, 3, lambda h, j: own_tile(jnp.int32(N_OWN + h), j, core))
-        load_x(10, 3).start()
+            k_out(seq + 1, 0, h).wait()
         load_kb(11, 3).start()
-        middle(5, 6)
-    def strip_quad(c):
-        return lambda d, h, j: strip_tile(2 * c + 1 - d, jnp.int32(h), j)
+
+    def remote_quad(step):
+        ps = [step(i) for i in range(4)]
+        return lambda d, h, j: remote_tile(ps[2 * d + h], j)
 
     with jax.named_scope("second_first"):
         wait_y(0, 1)
-        quad(jnp.int32(0), strip_quad(jnp.int32(0)))
+        quad(jnp.int32(0), remote_quad(jnp.int32))
+        middle(5, 6)
     with jax.named_scope("second_cross"):
 
         def second_cross(t, _):
@@ -466,27 +510,27 @@
                 wait_y(table((1, 1) + Y_NEED[:-1], t), table((1,) + Y_NEED, t))
 
             def tile(d, h, j):
-                q = 4 * (t - 1) + 2 * d + h
-                return pick(q < 10, cross_tile(q, j), last_tile(q - 10, j))
+                cross = cross_tile(4 * (t - 1) + 2 * d + h, j)
+                return pick(t < 3, cross, last[6 * h + j]) if d else cross
 
             quad(t, tile)
             return 0
 
         lax.fori_loop(1, 4, second_cross, 0)
-
-    def second_chunk(k, _):
-        done = jnp.where(k == 0, 0, N_CHUNK - k)
-
+        wait_y_par(2)
+
+    def second_remote(k, _):
         def beside():
             for j in range(2):
-                finish(j, done, SB2)
+                finish(j, table((4, 4, 3, 2), k), SB2)
+                finish(j, table((5, 5, 3, 2), k), SB2)
 
         with jax.named_scope("second_chunk"):
-            quad(4 + k, strip_quad(N_CHUNK - 1 - k), beside)
-        send_range(done, done + 1, SB2, RB2, s2_sem, r2_sem)
+            quad(4 + k, remote_quad(lambda i: table(REMOTE_ORDER, 4 * k + i)), beside)
+        send_range(table((0, 4, 3, 2), k), table((0, 6, 4, 3), k), SB2, RB2, s2_sem, r2_sem)
         return 0
 
-    lax.fori_loop(0, N_CHUNK - 2, second_chunk, 0)
+    lax.fori_loop(0, 4, second_remote, 0)
 
     def finish_strip(n):
         cols = pl.ds(n * STRIP, STRIP)
@@ -497,18 +541,15 @@
             remote(SB2.at[j, :, cols], RB2.at[j, :, cols], s2_sem, r2_sem, homes[j][1]).start()
 
     with jax.named_scope("second_chunk"):
+        finish_range(0, 1, SB2, RB2, s2_sem, r2_sem)
         load_x(0, 0).wait()
         load_kb(0, 0).wait()
-        for j in range(2):
-            finish(j, 2, SB2)
-        use(X, 0, lambda h, j: strip_tile(jnp.int32(3), jnp.int32(h), j))
-        send_range(2, 3, SB2, RB2, s2_sem, r2_sem)
+        use(X, 0, lambda h, j: remote_tile(jnp.int32(REMOTE_ORDER[16 + h]), j))
+        finish_strip(2)
+        use(KB, 0, lambda h, j: remote_tile(jnp.int32(REMOTE_ORDER[18 + h]), j))
         finish_strip(3)
-        use(KB, 0, lambda h, j: strip_tile(jnp.int32(2), jnp.int32(h), j))
-        finish_strip(2)
 
     with jax.named_scope("second_par"):
-        wait_y_par(1)
         quad(jnp.int32(9), lambda d, h, j: own_tile(jnp.int32(N_OWN + 2 + 2 * d + h), j, core))
         remote(YT.at[PAR], RB2.at[2], s2_sem, r2_sem, pt).start()
 
@@ -564,13 +605,14 @@
                 pltpu.VMEM((3, 32, ROWS), F32),
                 pltpu.VMEM((2, HALF_ROWS, CHUNK), BF16),
                 pltpu.VMEM((2, HALF_ROWS, CHUNK), BF16),
+                pltpu.VMEM((STEP_ROWS, CHUNK), BF16),
                 pltpu.VMEM((4, 2 * STEP_ROWS, CHUNK), BF16),
                 pltpu.SMEM((1,), F32), pltpu.SMEM((1,), F32),
                 dma((2,)), dma((N_STRIP,)), dma, dma((2,)), dma, dma((2,)), dma, dma,
                 dma((4,)), dma((2, 2)), dma((4,)), dma((4,)),
-                dma, dma((N_CHUNK,)), dma, dma((N_CHUNK,)), dma((2,)), dma, dma,
+                dma, dma((N_CHUNK,)), dma, dma((N_CHUNK,)), dma((3,)), dma, dma,
             ],
-            compiler_params=pltpu.CompilerParams(collective_id=0, has_side_effects=True, vmem_limit_bytes=56 * 2**20),
+            compiler_params=pltpu.CompilerParams(collective_id=0, has_side_effects=True, vmem_limit_bytes=58 * 2**20),
             name="products",
         )(x_loc, v_loc.T, length_scale, out_scale)
         return (own + parts[0] + parts[1] + parts[2]).T

time: 151 us -> 150 us (level)
  Pallas kernels: 149 us -> 147 us
where the time goes in v8:
time: 150 us
  Pallas kernels  147 us (98%)
    pallas_call x1, Pallas kernels, local_program(): pl.pallas_call(body, out_shape=(pltpu.VMEM((32, ROWS), F32), pltpu.VMEM((...  147 us

profile of v8, /device:TPU:0, one launch (start us, length us, event | category | flops | bytes accessed | tf_op | source)
XLA Modules:
  0.0 149.5 jit_solution(13475508172796325743)
XLA Ops:
  1.3 147.4 %products.1 = (f32[32,3072]{1,0:T(8,128)S(1)}, f32[3,32,3072]{2,1,0:T(8,128)S(1)}, bf16[76800,512]{1,0:T(8,128)(2,1)}) custom-call(bf16[3072,768]{1,0:T(8,128)(2,1)} %x_hbm.1, bf16[32,3072]{1,0:T(8,128)(2,1)} %bitcast.15, f32[1]{0:T(128)S(6)} %copy.5.ell_hbm, f32[1]{0:T(128)S(6)} %copy.6.amp_hbm), custom_call_target="tpu_custom_call" | custom-call | tf_op jit(solution)/shard_map/products/pallas_call | solution.py:585
  148.7 0.8 fusion

commit v9 on v8

--- a/solution.py
+++ b/solution.py
@@ -439,6 +439,8 @@
         slot = t & 3
         load_x(0, slot).wait()
         load_kb(0, slot).wait()
+
+        t = jnp.int32(t)
 
         @pl.when(jnp.logical_and(t >= 1, t <= 7))
         def _():
@@ -519,18 +521,12 @@
         lax.fori_loop(1, 4, second_cross, 0)
         wait_y_par(2)
 
-    def second_remote(k, _):
-        def beside():
-            for j in range(2):
-                finish(j, table((4, 4, 3, 2), k), SB2)
-                finish(j, table((5, 5, 3, 2), k), SB2)
-
+    for k, done in enumerate(((), (4, 5), (3,), (2,))):
         with jax.named_scope("second_chunk"):
-            quad(4 + k, remote_quad(lambda i: table(REMOTE_ORDER, 4 * k + i)), beside)
-        send_range(table((0, 4, 3, 2), k), table((0, 6, 4, 3), k), SB2, RB2, s2_sem, r2_sem)
-        return 0
-
-    lax.fori_loop(0, 4, second_remote, 0)
+            ps = REMOTE_ORDER[4 * k : 4 * k + 4]
+            quad(4 + k, remote_quad(lambda i: jnp.int32(ps[i])), lambda: [finish(j, c, SB2) for c in done for j in range(2)])
+        for c in done:
+            send_range(c, c + 1, SB2, RB2, s2_sem, r2_sem)
 
     def finish_strip(n):
         cols = pl.ds(n * STRIP, STRIP)

time: 150 us -> 149 us (level)
  no operation moved by 1% of the time
where the time goes in v9:
time: 149 us
  Pallas kernels  147 us (99%)
    pallas_call x1, Pallas kernels, local_program(): pl.pallas_call(body, out_shape=(pltpu.VMEM((32, ROWS), F32), pltpu.VMEM((...  147 us

profile of v9, /device:TPU:0, one launch (start us, length us, event | category | flops | bytes accessed | tf_op | source)
XLA Modules:
  0.0 149.0 jit_solution(12732413866372781193)
XLA Ops:
  1.3 146.9 %products.1 = (f32[32,3072]{1,0:T(8,128)S(1)}, f32[3,32,3072]{2,1,0:T(8,128)S(1)}, bf16[76800,512]{1,0:T(8,128)(2,1)}) custom-call(bf16[3072,768]{1,0:T(8,128)(2,1)} %x_hbm.1, bf16[32,3072]{1,0:T(8,128)(2,1)} %bitcast.15, f32[1]{0:T(128)S(6)} %copy.5.ell_hbm, f32[1]{0:T(128)S(6)} %copy.6.amp_hbm), custom_call_target="tpu_custom_call" | custom-call | tf_op jit(solution)/shard_map/products/pallas_call | solution.py:581
  148.2 0.8 fusion

commit v10 on v9

--- a/solution.py
+++ b/solution.py
@@ -20,14 +20,14 @@
 OWN, XNB, YNB, PAR, TRASH = 0, 1, 2, 3, 4
 
 N_OWN, N_PAIR = 7, 13
-REMOTE_AT = (0, 0, 7, 7, 13, 13, 18, 18, 21, 21, 23, 23)
+REMOTE_AT = (0, 7, 13, 18, 21, 21, 23, 23)
 REMOTE_TILE = (0, 44, 80, 108, 128, 140)
-CROSS_AT = (0, 0, 0, 0, 1, 2, 3, 4, 5, 6, 8, 10)
+CROSS_AT = (0, 0, 1, 3, 5, 6, 8, 10)
 CROSS_TILE = (0, 0, 2, 4, 8, 12, 18, 24, 32, 40, 50, 60)
 OWN_PLACE = (1, 2, 3, 6, 7, 48, 49, 4, 5, 44, 45, 46, 47)
-REMOTE_ORDER = (20, 21, 22, 23, 16, 17, 18, 19, 10, 13, 14, 15, 4, 5, 6, 7, 8, 9, 11, 12)
-REMOTE_PLACE = tuple(8 + p if p < 4 else 24 + REMOTE_ORDER.index(p) for p in range(24))
-CROSS_PLACE = 12
+REMOTE_ORDER = (20, 21, 22, 23, 16, 17, 18, 19, 10, 13, 14, 15, 8, 9, 11, 12)
+REMOTE_PLACE = tuple(8 + p if p < 8 else 28 + REMOTE_ORDER.index(p) for p in range(24))
+CROSS_PLACE = 16
 N_PLACE = 50
 STEP_ROWS = 6 * STRIP
 HALF_ROWS = UNITS * STRIP
@@ -117,8 +117,8 @@
 
 
 def body(
-    x_hbm, v_hbm, ell_hbm, amp_hbm, out_ref, RB2, k_hbm,
-    X, VT, YV, NA, NB, CR, YR, YT, SB, RB, SB2, kr0, kr1, KL, KB, ell_ref, amp_ref,
+    x_hbm, v_hbm, ell_ref, amp_ref, out_ref, RB2, k_hbm,
+    X, VT, YV, NA, NB, CR, YR, YT, SB, RB, SB2, kr0, kr1, KL, KB,
     sx_sem, rx_sem, sv_sem, rv_sem, sn_sem, rn_sem, sp_sem, rp_sem, loc_sem, ko_sem, kb_sem, kx_sem,
     s1_sem, r1_sem, sy_sem, ry_sem, ryp_sem, s2_sem, r2_sem,
 ):
@@ -137,12 +137,15 @@
     def remote(src, dst, ss, rs, to):
         return pltpu.make_async_remote_copy(src_ref=src, dst_ref=dst, send_sem=ss, recv_sem=rs, device_id=to, device_id_type=MESH)
 
-    def x_copy(j, n):
-        return remote(x_hbm.at[rows_of(n)], X.at[1 + j, rows_of(n)], sx_sem.at[j], rx_sem.at[n], (tx, ty)[j])
-
-    def wait_strip(n):
-        two = X.at[1:3, rows_of(n)]
-        remote(two, two, sx_sem.at[0], rx_sem.at[n], tx).wait_recv()
+    def part_rows(i, late):
+        return rows_of(i + 4) if late else cols_of(i)
+
+    def x_copy(j, i, late):
+        return remote(x_hbm.at[part_rows(i, late)], X.at[1 + j, part_rows(i, late)], sx_sem.at[j], rx_sem.at[i], (tx, ty)[j])
+
+    def wait_x(i, late):
+        two = X.at[1:3, part_rows(i, late)]
+        remote(two, two, sx_sem.at[0], rx_sem.at[i], tx).wait_recv()
 
     p_copy = remote(x_hbm, X.at[PAR], sp_sem, rp_sem, pt)
     v_copies = [remote(v_hbm, VT.at[1 + j], sv_sem, rv_sem.at[j // 2], d) for j, d in enumerate((tx, ty, pt))]
@@ -150,8 +153,7 @@
 
     x_loc = pltpu.make_async_copy(x_hbm, X.at[OWN], loc_sem.at[0])
     v_loc = pltpu.make_async_copy(v_hbm, VT.at[OWN], loc_sem.at[1])
-    scalars = [pltpu.make_async_copy(src, dst, loc_sem.at[2 + i]) for i, (src, dst) in enumerate(((ell_hbm, ell_ref), (amp_hbm, amp_ref)))]
-    for c in scalars + [v_loc, x_loc]:
+    for c in (v_loc, x_loc):
         c.start()
 
     barrier = pltpu.get_barrier_semaphore()
@@ -163,17 +165,14 @@
     for c in v_copies:
         c.start()
     for j in range(2):
-        x_copy(j, 0).start()
+        x_copy(j, 0, False).start()
     p_copy.start()
 
-    for c in scalars:
-        c.wait()
     ell = jnp.full((1, CHUNK), ell_ref[0], F32)
     half = LOG2E / (2.0 * ell * ell)
     top = jnp.log2(jnp.full((1, CHUNK), amp_ref[0], F32))
     CR[0:1, :] = 2.0 * half
     CR[1:2, :] = top
-    h1, l1 = half[:, 0:128], top[:, 0:128]
 
     for s in range(3):
         YR[s] = jnp.zeros((STRIP + ROWS, 32), F32)
@@ -189,9 +188,9 @@
     def own_norm(c, _):
         r = pl.ds(pl.multiple_of(c * CHUNK, CHUNK), CHUNK)
         x = X[OWN, r, :].astype(F32)
-        n = jnp.broadcast_to(jnp.sum(x * x, axis=1, keepdims=True), (CHUNK, 128)) * h1
-        NA[OWN, r, :] = l1 - n
-        NB[OWN, :, cols_of(c)] = -jnp.transpose(n)[0:1, :]
+        n = jnp.broadcast_to(0.5 * jnp.sum(x * x, axis=1, keepdims=True), (CHUNK, 128))
+        NA[OWN, r, :] = n
+        NB[OWN, :, cols_of(c)] = jnp.transpose(n)[0:1, :]
         return 0
 
     with jax.named_scope("own_norm"):
@@ -199,17 +198,14 @@
     for c in n_copies:
         c.start()
 
-    def send_strip(n, _):
+    for i in range(1, 8):
         for j in range(2):
-            x_copy(j, n).start()
-        return 0
-
-    lax.fori_loop(1, N_STRIP, send_strip, 0)
+            x_copy(j, i, i >= 4).start()
 
     def left_norm(s):
         def one(c, _):
             r = pl.ds(pl.multiple_of(c * CHUNK, CHUNK), CHUNK)
-            NA[s, r, :] = l1 + jnp.transpose(jnp.broadcast_to(NB[s, :, cols_of(c)], (128, CHUNK)))
+            NA[s, r, :] = jnp.transpose(jnp.broadcast_to(NB[s, :, cols_of(c)], (128, CHUNK)))
             return 0
 
         lax.fori_loop(0, N_CHUNK, one, 0)
@@ -221,8 +217,8 @@
     def kern(tile, g):
         s, a, t, b, _ = tile
         na = NA[s, rows_of(a), :]
-        e = (g * CR[0:1, :] + NB[t, :, cols_of(b)]) + jnp.concatenate([na] * (CHUNK // 128), axis=1)
-        return jnp.exp2(jnp.minimum(e, CR[1:2, :])).astype(BF16)
+        d = (jnp.concatenate([na] * (CHUNK // 128), axis=1) + NB[t, :, cols_of(b)]) - g
+        return jnp.exp2(CR[1:2, :] - jnp.maximum(d, 0.0) * CR[0:1, :]).astype(BF16)
 
     def apply(tile, k, vec):
         s, a, t, b, to = tile
@@ -295,14 +291,22 @@
         for j in range(2):
             left_norm(1 + j)
 
-    def strip(n, state):
+    def landed(i, state):
         with jax.named_scope("wait_strip"):
-            wait_strip(n)
+
+            @pl.when(i < 4)
+            def _():
+                wait_x(i, False)
+
+            @pl.when(i >= 4)
+            def _():
+                wait_x(i, True)
+
         with jax.named_scope("strip"):
-            state = lax.fori_loop(table(REMOTE_AT, n), table(REMOTE_AT, n + 1), remote_step, state)
-            return lax.fori_loop(table(CROSS_AT, n), table(CROSS_AT, n + 1), cross_step, state)
-
-    state = lax.fori_loop(0, N_STRIP - 1, strip, state)
+            state = lax.fori_loop(table(REMOTE_AT, i), table(REMOTE_AT, i + 1), remote_step, state)
+            return lax.fori_loop(table(CROSS_AT, i), table(CROSS_AT, i + 1), cross_step, state)
+
+    state = lax.fori_loop(0, 7, landed, state)
 
     homes = ((XNB, sx), (YNB, sy), (PAR, pt))
 
@@ -321,23 +325,11 @@
                 YR[s, sums_of(c), :] = jnp.zeros((CHUNK, 32), F32)
 
     def finish_range(lo, hi, send, recv, ss, rs, js=(0, 1)):
-        def one(c, _):
+        for c in range(lo, hi):
             for j in js:
                 finish(j, c, send)
-            return 0
-
-        for c in range(lo, hi):
-            one(c, 0)
             for j in js:
                 part_copy(j, c, send, recv, ss, rs).start()
-
-    def send_range(lo, hi, send, recv, ss, rs, js=(0, 1)):
-        def go(c, _):
-            for j in js:
-                part_copy(j, c, send, recv, ss, rs).start()
-            return 0
-
-        lax.fori_loop(lo, hi, go, 0)
 
     def load_kb(d, slot):
         return pltpu.make_async_copy(k_hbm.at[pl.ds(pl.multiple_of(d * 2 * STEP_ROWS, STRIP), 2 * STEP_ROWS)], KB.at[slot], kb_sem.at[slot])
@@ -402,17 +394,19 @@
     applies(late[0:2], 0, None)
     finish_range(0, N_CHUNK, SB, RB, s1_sem, r1_sem, (2,))
     with jax.named_scope("wait_last"):
-        wait_strip(N_STRIP - 1)
+        wait_x(7, True)
     with jax.named_scope("last"):
         for c in range(N_CHUNK):
             if c == 3:
                 d = begin(seq + 1, jnp.int32(CROSS_PLACE + 10), before)
             put = grams(last[2 * c : 2 * c + 2], 2 * c, d)
-            if c > 0:
+            if c > 1:
                 applies(last[2 * c - 2 : 2 * c], 2 * c - 2, 1 - d if c == 3 else d)
             put()
-            if c > 0:
-                finish_range(c - 1, c, SB, RB, s1_sem, r1_sem)
+            if c == 0:
+                applies(last[0:2], 0, d)
+            if c != 1:
+                finish_range(max(c - 1, 0), max(c, 1), SB, RB, s1_sem, r1_sem)
         put = grams(late[2:6], 2, None)
         applies(last[10:12], 10, d)
         put()
@@ -435,11 +429,10 @@
             r = (6 * h + j) * STRIP
             apply(tile(j), k[slot, r : r + STRIP, 0:CHUNK], YV)
 
-    def quad(t, tile, beside=None):
+    def quad(t, tile):
         slot = t & 3
         load_x(0, slot).wait()
         load_kb(0, slot).wait()
-
         t = jnp.int32(t)
 
         @pl.when(jnp.logical_and(t >= 1, t <= 7))
@@ -450,8 +443,6 @@
         def _():
             load_kb(11 + 2 * t, (t - 1) & 3).start()
 
-        if beside is not None:
-            beside()
         use(X, slot, lambda h, j: tile(0, h, j))
         use(KB, slot, lambda h, j: tile(1, h, j))
 
@@ -488,45 +479,48 @@
         use_step(KB, 2, 1, lambda j: own_tile(jnp.int32(N_OWN + 1), j, core))
         load_x(8, 2).start()
         load_kb(9, 2).start()
-        middle(4, 5)
-        load_kb(0, 3).wait()
-        use(KB, 3, lambda h, j: own_tile(jnp.int32(3 + h), j, core))
-        load_x(10, 3).start()
         kl_out.wait()
         for h in range(2):
             k_out(seq + 1, 0, h).wait()
-        load_kb(11, 3).start()
+        load_x(10, 3).start()
+        middle(4, 5)
 
     def remote_quad(step):
         ps = [step(i) for i in range(4)]
         return lambda d, h, j: remote_tile(ps[2 * d + h], j)
 
     with jax.named_scope("second_first"):
+
         wait_y(0, 1)
-        quad(jnp.int32(0), remote_quad(jnp.int32))
+        quad(0, remote_quad(jnp.int32))
         middle(5, 6)
+        load_kb(0, 3).wait()
+        use(KB, 3, lambda h, j: own_tile(jnp.int32(3 + h), j, core))
+        load_kb(11, 3).start()
+        wait_y_par(2)
+        wait_y(1, 2)
+        quad(1, remote_quad(lambda i: jnp.int32(4 + i)))
     with jax.named_scope("second_cross"):
 
         def second_cross(t, _):
             with jax.named_scope("wait_y"):
-                wait_y(table((1, 1) + Y_NEED[:-1], t), table((1,) + Y_NEED, t))
+                wait_y(table((2, 2, 2) + Y_NEED[:-1], t), table((2, 2) + Y_NEED, t))
 
             def tile(d, h, j):
-                cross = cross_tile(4 * (t - 1) + 2 * d + h, j)
-                return pick(t < 3, cross, last[6 * h + j]) if d else cross
+                cross = cross_tile(4 * (t - 2) + 2 * d + h, j)
+                return pick(t < 4, cross, last[6 * h + j]) if d else cross
 
             quad(t, tile)
             return 0
 
-        lax.fori_loop(1, 4, second_cross, 0)
-        wait_y_par(2)
-
-    for k, done in enumerate(((), (4, 5), (3,), (2,))):
+        lax.fori_loop(2, 5, second_cross, 0)
+
+    for k, done in enumerate(((0,), (4, 5), (3,))):
+        for c in done:
+            finish_range(c, c + 1, SB2, RB2, s2_sem, r2_sem)
         with jax.named_scope("second_chunk"):
             ps = REMOTE_ORDER[4 * k : 4 * k + 4]
-            quad(4 + k, remote_quad(lambda i: jnp.int32(ps[i])), lambda: [finish(j, c, SB2) for c in done for j in range(2)])
-        for c in done:
-            send_range(c, c + 1, SB2, RB2, s2_sem, r2_sem)
+            quad(5 + k, remote_quad(lambda i: jnp.int32(ps[i])))
 
     def finish_strip(n):
         cols = pl.ds(n * STRIP, STRIP)
@@ -537,16 +531,16 @@
             remote(SB2.at[j, :, cols], RB2.at[j, :, cols], s2_sem, r2_sem, homes[j][1]).start()
 
     with jax.named_scope("second_chunk"):
-        finish_range(0, 1, SB2, RB2, s2_sem, r2_sem)
+        finish_range(2, 3, SB2, RB2, s2_sem, r2_sem)
         load_x(0, 0).wait()
         load_kb(0, 0).wait()
-        use(X, 0, lambda h, j: remote_tile(jnp.int32(REMOTE_ORDER[16 + h]), j))
+        use(X, 0, lambda h, j: remote_tile(jnp.int32(REMOTE_ORDER[12 + h]), j))
         finish_strip(2)
-        use(KB, 0, lambda h, j: remote_tile(jnp.int32(REMOTE_ORDER[18 + h]), j))
+        use(KB, 0, lambda h, j: remote_tile(jnp.int32(REMOTE_ORDER[14 + h]), j))
         finish_strip(3)
 
     with jax.named_scope("second_par"):
-        quad(jnp.int32(9), lambda d, h, j: own_tile(jnp.int32(N_OWN + 2 + 2 * d + h), j, core))
+        quad(9, lambda d, h, j: own_tile(jnp.int32(N_OWN + 2 + 2 * d + h), j, core))
         remote(YT.at[PAR], RB2.at[2], s2_sem, r2_sem, pt).start()
 
     with jax.named_scope("second_end"):
@@ -561,13 +555,9 @@
             remote(buf.at[1:4], buf.at[1:4], sem, rx_sem.at[0], tx).wait_send()
         remote(SB, RB, s1_sem, rx_sem.at[0], tx).wait_send()
 
-    def final(c, _):
-        out_ref[:, cols_of(c)] = YT[OWN, :, cols_of(c)] + jnp.transpose(YR[OWN, sums_of(c), :])
-        return 0
-
     with jax.named_scope("final"):
         for c in range(N_CHUNK):
-            final(c, 0)
+            out_ref[:, cols_of(c)] = YT[OWN, :, cols_of(c)] + jnp.transpose(YR[OWN, sums_of(c), :])
         all_sums = remote(SB2, RB2, s2_sem, r2_sem, pt)
         all_sums.wait_send()
         all_sums.wait_recv()
@@ -578,6 +568,7 @@
         dma = pltpu.SemaphoreType.DMA
         hbm = pl.BlockSpec(memory_space=pltpu.HBM)
         vmem = pl.BlockSpec(memory_space=pltpu.VMEM)
+        smem = pl.BlockSpec(memory_space=pltpu.SMEM)
         own, parts, _ = pl.pallas_call(
             body,
             out_shape=(
@@ -585,7 +576,7 @@
                 pltpu.VMEM((3, 32, ROWS), F32),
                 jax.ShapeDtypeStruct((N_PLACE * STEP_ROWS, CHUNK), BF16),
             ),
-            in_specs=[hbm, hbm, hbm, hbm],
+            in_specs=[hbm, hbm, smem, smem],
             out_specs=(vmem, vmem, hbm),
             scratch_shapes=[
                 pltpu.VMEM((4, ROWS, 768), BF16),
@@ -603,9 +594,8 @@
                 pltpu.VMEM((2, HALF_ROWS, CHUNK), BF16),
                 pltpu.VMEM((STEP_ROWS, CHUNK), BF16),
                 pltpu.VMEM((4, 2 * STEP_ROWS, CHUNK), BF16),
-                pltpu.SMEM((1,), F32), pltpu.SMEM((1,), F32),
-                dma((2,)), dma((N_STRIP,)), dma, dma((2,)), dma, dma((2,)), dma, dma,
-                dma((4,)), dma((2, 2)), dma((4,)), dma((4,)),
+                dma((2,)), dma((8,)), dma, dma((2,)), dma, dma((2,)), dma, dma,
+                dma((2,)), dma((2, 2)), dma((4,)), dma((4,)),
                 dma, dma((N_CHUNK,)), dma, dma((N_CHUNK,)), dma((3,)), dma, dma,
             ],
             compiler_params=pltpu.CompilerParams(collective_id=0, has_side_effects=True, vmem_limit_bytes=58 * 2**20),

time: 149 us -> 149 us (level)
  no operation moved by 1% of the time
where the time goes in v10:
time: 149 us
  Pallas kernels  147 us (99%)
    pallas_call x1, Pallas kernels, local_program(): pl.pallas_call(body, out_shape=(pltpu.VMEM((32, ROWS), F32), pltpu.VMEM((...  147 us

profile of v10, /device:TPU:0, one launch (start us, length us, event | category | flops | bytes accessed | tf_op | source)
XLA Modules:
  0.0 148.8 jit_solution(231007231255097728)
XLA Ops:
  1.3 146.7 %products.1 = (f32[32,3072]{1,0:T(8,128)S(1)}, f32[3,32,3072]{2,1,0:T(8,128)S(1)}, bf16[76800,512]{1,0:T(8,128)(2,1)}) custom-call(bf16[3072,768]{1,0:T(8,128)(2,1)} %x_hbm.1, bf16[32,3072]{1,0:T(8,128)(2,1)} %bitcast.15, f32[1]{0:T(128)S(6)} %copy.5.ell_ref, f32[1]{0:T(128)S(6)} %copy.6.amp_ref), custom_call_target="tpu_custom_call" | custom-call | tf_op jit(solution)/shard_map/products/pallas_call | solution.py:572
  148.0 0.8 fusion

commit v11 on v10

--- a/solution.py
+++ b/solution.py
@@ -86,8 +86,10 @@
 
 def cross_tile(q, j):
     g = 6 * q + j
-    n = 1 + rank(CROSS_TILE[2:11], g)
-    r = g - table(CROSS_TILE, n)
+    n, first = jnp.int32(1), jnp.int32(0)
+    for i in range(2, N_STRIP - 1):
+        n, first = pick(g >= CROSS_TILE[i], (i, CROSS_TILE[i]), (n, first))
+    r = g - first
     m = n >> 1
     t = pick(r < m, (jnp.int32(XNB), n, jnp.int32(YNB), r, jnp.int32(YNB)), (jnp.int32(YNB), n, jnp.int32(XNB), r - m, jnp.int32(XNB)))
     return pick(r < 2 * m, t, (jnp.int32(XNB), n - 1 + (r - 2 * m), jnp.int32(YNB), m, jnp.int32(YNB)))

time: 149 us -> 149 us (level)
  no operation moved by 1% of the time
where the time goes in v11:
time: 149 us
  Pallas kernels  147 us (99%)
    pallas_call x1, Pallas kernels, local_program(): pl.pallas_call(body, out_shape=(pltpu.VMEM((32, ROWS), F32), pltpu.VMEM((...  147 us

profile of v11, /device:TPU:0, one launch (start us, length us, event | category | flops | bytes accessed | tf_op | source)
XLA Modules:
  0.0 148.8 jit_solution(7507932513276116527)
XLA Ops:
  1.3 146.7 %products.1 = (f32[32,3072]{1,0:T(8,128)S(1)}, f32[3,32,3072]{2,1,0:T(8,128)S(1)}, bf16[76800,512]{1,0:T(8,128)(2,1)}) custom-call(bf16[3072,768]{1,0:T(8,128)(2,1)} %x_hbm.1, bf16[32,3072]{1,0:T(8,128)(2,1)} %bitcast.15, f32[1]{0:T(128)S(6)} %copy.5.ell_ref, f32[1]{0:T(128)S(6)} %copy.6.amp_ref), custom_call_target="tpu_custom_call" | custom-call | tf_op jit(solution)/shard_map/products/pallas_call | solution.py:574
  148.0 0.8 fusion

commit v12 on v11

--- a/solution.py
+++ b/solution.py
@@ -25,7 +25,7 @@
 CROSS_AT = (0, 0, 1, 3, 5, 6, 8, 10)
 CROSS_TILE = (0, 0, 2, 4, 8, 12, 18, 24, 32, 40, 50, 60)
 OWN_PLACE = (1, 2, 3, 6, 7, 48, 49, 4, 5, 44, 45, 46, 47)
-REMOTE_ORDER = (20, 21, 22, 23, 16, 17, 18, 19, 10, 13, 14, 15, 8, 9, 11, 12)
+REMOTE_ORDER = (23, 22, 21, 20, 19, 18, 17, 16, 15, 14, 13, 10, 8, 9, 11, 12)
 REMOTE_PLACE = tuple(8 + p if p < 8 else 28 + REMOTE_ORDER.index(p) for p in range(24))
 CROSS_PLACE = 16
 N_PLACE = 50
@@ -71,6 +71,16 @@
     return pick(o < N_OWN, own, par)
 
 
+def own_ints(o, j):
+    if o < N_OWN:
+        pairs = [(i, c) for c in range(N_CHUNK) for i in range(c + 1)]
+        i, c = pairs[3 * o + j // 2]
+        return (OWN, 2 * i + j % 2, OWN, c, TRASH if i == c else OWN)
+    pairs = [(i, c) for c in range(N_CHUNK) for i in range(c)]
+    i, c = pairs[3 * (o - N_OWN) + j // 2]
+    return (OWN, 2 * i + j % 2, PAR, c, PAR)
+
+
 def remote_tile(p, j):
     g = 6 * p + j
     d, first = jnp.int32(0), jnp.int32(0)
@@ -225,7 +235,10 @@
     def apply(tile, k, vec):
         s, a, t, b, to = tile
         YR[s, rows_of(a + 1), :] += lax.dot_general(k, vec[t, :, cols_of(b)], (((1,), (1,)), ((), ())), preferred_element_type=F32)
-        YT[to, :, cols_of(b)] += jnp.dot(vec[s, :, rows_of(jnp.maximum(a, 0))], k, preferred_element_type=F32)
+        if isinstance(to, int) and to == TRASH:
+            return
+        left = a if isinstance(a, int) else jnp.maximum(a, 0)
+        YT[to, :, cols_of(b)] += jnp.dot(vec[s, :, rows_of(left)], k, preferred_element_type=F32)
 
     def k_out(seq, place, half):
         kr = (kr0, kr1)[half]
@@ -346,23 +359,20 @@
         load_kb(i, i).start()
 
     def y_copy(j, c):
-        return remote(YV.at[OWN, :, cols_of(c)], YV.at[1 + j, :, cols_of(c)], sy_sem, ryp_sem.at[(c >= 3).astype(jnp.int32) + (c >= 4).astype(jnp.int32)] if j == 2 else ry_sem.at[c], (tx, ty, pt)[j])
-
-    def middle(lo, hi):
-        def one(c, _):
-            with jax.named_scope("wait_part"):
-                three = RB.at[:, :, cols_of(c)]
-                remote(three, three, s1_sem, r1_sem.at[c], pt).wait_recv()
-            y = YT[OWN, :, cols_of(c)] + jnp.transpose(YR[OWN, sums_of(c), :])
-            y = y + RB[0, :, cols_of(c)] + RB[1, :, cols_of(c)] + RB[2, :, cols_of(c)]
-            YV[OWN, :, cols_of(c)] = y.astype(BF16)
-            YT[OWN, :, cols_of(c)] = jnp.zeros((32, CHUNK), F32)
-            YR[OWN, sums_of(c), :] = jnp.zeros((CHUNK, 32), F32)
-            for j in range(3):
-                y_copy(j, c).start()
-            return 0
-
-        lax.fori_loop(lo, hi, one, 0)
+        done = ryp_sem.at[(c >= 3) + (c >= 4)] if j == 2 else ry_sem.at[c]
+        return remote(YV.at[OWN, :, cols_of(c)], YV.at[1 + j, :, cols_of(c)], sy_sem, done, (tx, ty, pt)[j])
+
+    def middle(c):
+        with jax.named_scope("wait_part"):
+            three = RB.at[:, :, cols_of(c)]
+            remote(three, three, s1_sem, r1_sem.at[c], pt).wait_recv()
+        y = YT[OWN, :, cols_of(c)] + jnp.transpose(YR[OWN, sums_of(c), :])
+        y = y + RB[0, :, cols_of(c)] + RB[1, :, cols_of(c)] + RB[2, :, cols_of(c)]
+        YV[OWN, :, cols_of(c)] = y.astype(BF16)
+        YT[OWN, :, cols_of(c)] = jnp.zeros((32, CHUNK), F32)
+        YR[OWN, sums_of(c), :] = jnp.zeros((CHUNK, 32), F32)
+        for j in range(3):
+            y_copy(j, c).start()
 
     last = last_tiles()
     late = [remote_tile(jnp.int32(23), j) for j in range(6)]
@@ -414,7 +424,7 @@
         put()
         kl_out.start()
         load_x(4, 0).start()
-        middle(0, 1)
+        middle(0)
         applies(late[2:6], 2, None)
         finish_range(5, 6, SB, RB, s1_sem, r1_sem)
 
@@ -448,10 +458,13 @@
         use(X, slot, lambda h, j: tile(0, h, j))
         use(KB, slot, lambda h, j: tile(1, h, j))
 
+    def wait_y_one(c):
+        two = YV.at[1:3, :, cols_of(c)]
+        remote(two, two, sy_sem, ry_sem.at[c], tx).wait_recv()
+
     def wait_y(lo, hi):
         def one(c, _):
-            two = YV.at[1:3, :, cols_of(c)]
-            remote(two, two, sy_sem, ry_sem.at[c], tx).wait_recv()
+            wait_y_one(c)
             return 0
 
         lax.fori_loop(lo, hi, one, 0)
@@ -461,31 +474,31 @@
         remote(part, part, sy_sem, ryp_sem.at[late], pt).wait_recv()
 
     with jax.named_scope("middle"):
-        middle(1, 2)
+        middle(1)
     with jax.named_scope("second_own"):
         first_in.wait()
         for j in range(6):
-            apply(own_tile(jnp.int32(0), j, core), KB[0, STEP_ROWS + j * STRIP : STEP_ROWS + (j + 1) * STRIP, :], YV)
+            apply(own_ints(0, j), KB[0, STEP_ROWS + j * STRIP : STEP_ROWS + (j + 1) * STRIP, :], YV)
         load_kb(5, 0).start()
-        middle(2, 3)
+        middle(2)
         load_kb(0, 1).wait()
-        use_step(KB, 1, 0, lambda j: own_tile(jnp.int32(1), j, core))
+        use_step(KB, 1, 0, lambda j: own_ints(1, j))
         wait_y_par(0)
         load_kb(0, 2).wait()
-        use_step(KB, 2, 0, lambda j: own_tile(jnp.int32(N_OWN), j, core))
-        middle(3, 4)
-        use_step(KB, 1, 1, lambda j: own_tile(jnp.int32(2), j, core))
+        use_step(KB, 2, 0, lambda j: own_ints(N_OWN, j))
+        middle(3)
+        use_step(KB, 1, 1, lambda j: own_ints(2, j))
         load_x(6, 1).start()
         load_kb(7, 1).start()
         wait_y_par(1)
-        use_step(KB, 2, 1, lambda j: own_tile(jnp.int32(N_OWN + 1), j, core))
+        use_step(KB, 2, 1, lambda j: own_ints(N_OWN + 1, j))
         load_x(8, 2).start()
         load_kb(9, 2).start()
         kl_out.wait()
         for h in range(2):
             k_out(seq + 1, 0, h).wait()
         load_x(10, 3).start()
-        middle(4, 5)
+        middle(4)
 
     def remote_quad(step):
         ps = [step(i) for i in range(4)]
@@ -493,14 +506,14 @@
 
     with jax.named_scope("second_first"):
 
-        wait_y(0, 1)
+        wait_y_one(0)
         quad(0, remote_quad(jnp.int32))
-        middle(5, 6)
+        middle(5)
         load_kb(0, 3).wait()
-        use(KB, 3, lambda h, j: own_tile(jnp.int32(3 + h), j, core))
+        use(KB, 3, lambda h, j: own_ints(3 + h, j))
         load_kb(11, 3).start()
         wait_y_par(2)
-        wait_y(1, 2)
+        wait_y_one(1)
         quad(1, remote_quad(lambda i: jnp.int32(4 + i)))
     with jax.named_scope("second_cross"):
 
@@ -542,12 +555,8 @@
         finish_strip(3)
 
     with jax.named_scope("second_par"):
-        quad(9, lambda d, h, j: own_tile(jnp.int32(N_OWN + 2 + 2 * d + h), j, core))
+        quad(9, lambda d, h, j: own_tile(jnp.int32(N_PAIR - 1), j, core) if d and h else own_ints(N_OWN + 2 + 2 * d + h, j))
         remote(YT.at[PAR], RB2.at[2], s2_sem, r2_sem, pt).start()
-
-    with jax.named_scope("second_end"):
-        load_x(0, 2).wait()
-        use(X, 2, lambda h, j: own_tile(jnp.int32(5 + h), j, core))
 
     with jax.named_scope("sent"):
         p_copy.wait_send()
@@ -556,6 +565,10 @@
         for buf, sem in ((VT, sv_sem), (NB, sn_sem), (YV, sy_sem)):
             remote(buf.at[1:4], buf.at[1:4], sem, rx_sem.at[0], tx).wait_send()
         remote(SB, RB, s1_sem, rx_sem.at[0], tx).wait_send()
+
+    with jax.named_scope("second_end"):
+        load_x(0, 2).wait()
+        use(X, 2, lambda h, j: own_ints(5 + h, j))
 
     with jax.named_scope("final"):
         for c in range(N_CHUNK):

time: 149 us -> 149 us (level)
  no operation moved by 1% of the time
where the time goes in v12:
time: 149 us; the launch traced here: 148 us
  Pallas kernels  146 us (98%)
    pallas_call x1, Pallas kernels, local_program(): pl.pallas_call(body, out_shape=(pltpu.VMEM((32, ROWS), F32), pltpu.VMEM((...  146 us

profile of v12, /device:TPU:0, one launch (start us, length us, event | category | flops | bytes accessed | tf_op | source)
XLA Modules:
  0.0 148.4 jit_solution(14768463942173122225)
XLA Ops:
  1.3 146.3 %products.1 = (f32[32,3072]{1,0:T(8,128)S(1)}, f32[3,32,3072]{2,1,0:T(8,128)S(1)}, bf16[76800,512]{1,0:T(8,128)(2,1)}) custom-call(bf16[3072,768]{1,0:T(8,128)(2,1)} %x_hbm.1, bf16[32,3072]{1,0:T(8,128)(2,1)} %bitcast.15, f32[1]{0:T(128)S(6)} %copy.5.ell_ref, f32[1]{0:T(128)S(6)} %copy.6.amp_ref), custom_call_target="tpu_custom_call" | custom-call | tf_op jit(solution)/shard_map/products/pallas_call | solution.py:587
  147.6 0.8 fusion

commit v13 on v12

--- a/solution.py
+++ b/solution.py
@@ -403,7 +403,10 @@
     put = grams(late[0:2], 0, None)
     applies(due, UNITS, 1 - d)
     put()
+    put = grams(late[2:4], 2, None)
     applies(late[0:2], 0, None)
+    put()
+    applies(late[2:4], 2, None)
     finish_range(0, N_CHUNK, SB, RB, s1_sem, r1_sem, (2,))
     with jax.named_scope("wait_last"):
         wait_x(7, True)
@@ -419,13 +422,13 @@
                 applies(last[0:2], 0, d)
             if c != 1:
                 finish_range(max(c - 1, 0), max(c, 1), SB, RB, s1_sem, r1_sem)
-        put = grams(late[2:6], 2, None)
+        put = grams(late[4:6], 4, None)
         applies(last[10:12], 10, d)
         put()
         kl_out.start()
         load_x(4, 0).start()
         middle(0)
-        applies(late[2:6], 2, None)
+        applies(late[4:6], 4, None)
         finish_range(5, 6, SB, RB, s1_sem, r1_sem)
 
     for h in range(2):

time: 149 us -> 148 us (level)
  no operation moved by 1% of the time
where the time goes in v13:
time: 148 us
  Pallas kernels  146 us (99%)
    pallas_call x1, Pallas kernels, local_program(): pl.pallas_call(body, out_shape=(pltpu.VMEM((32, ROWS), F32), pltpu.VMEM((...  146 us

profile of v13, /device:TPU:0, one launch (start us, length us, event | category | flops | bytes accessed | tf_op | source)
XLA Modules:
  0.0 148.3 jit_solution(9670354199683615513)
XLA Ops:
  1.3 146.2 %products.1 = (f32[32,3072]{1,0:T(8,128)S(1)}, f32[3,32,3072]{2,1,0:T(8,128)S(1)}, bf16[76800,512]{1,0:T(8,128)(2,1)}) custom-call(bf16[3072,768]{1,0:T(8,128)(2,1)} %x_hbm.1, bf16[32,3072]{1,0:T(8,128)(2,1)} %bitcast.15, f32[1]{0:T(128)S(6)} %copy.5.ell_ref, f32[1]{0:T(128)S(6)} %copy.6.amp_ref), custom_call_target="tpu_custom_call" | custom-call | tf_op jit(solution)/shard_map/products/pallas_call | solution.py:590
  147.5 0.8 fusion

commit v14 on v13

--- a/solution.py
+++ b/solution.py
@@ -161,7 +161,9 @@
 
     p_copy = remote(x_hbm, X.at[PAR], sp_sem, rp_sem, pt)
     v_copies = [remote(v_hbm, VT.at[1 + j], sv_sem, rv_sem.at[j // 2], d) for j, d in enumerate((tx, ty, pt))]
-    n_copies = [remote(NB.at[OWN], NB.at[1 + j], sn_sem, rn_sem.at[j // 2], d) for j, d in enumerate((tx, ty, pt))]
+    tail_cols = pl.ds(4 * CHUNK, 2 * CHUNK)
+    n_copies = [remote(NB.at[OWN, :, tail_cols], NB.at[1 + j, :, tail_cols], sn_sem.at[0], rn_sem.at[0], d) for j, d in enumerate((tx, ty))]
+    n_copies.append(remote(NB.at[OWN], NB.at[PAR], sn_sem.at[1], rn_sem.at[1], pt))
 
     x_loc = pltpu.make_async_copy(x_hbm, X.at[OWN], loc_sem.at[0])
     v_loc = pltpu.make_async_copy(v_hbm, VT.at[OWN], loc_sem.at[1])
@@ -197,12 +199,15 @@
     with jax.named_scope("x_local"):
         x_loc.wait()
 
+    def norm_of(s, c):
+        r = pl.ds(pl.multiple_of(c * CHUNK, CHUNK), CHUNK)
+        x = X[s, r, :].astype(F32)
+        n = jnp.broadcast_to(0.5 * jnp.sum(x * x, axis=1, keepdims=True), (CHUNK, 128))
+        NA[s, r, :] = n
+        NB[s, :, cols_of(c)] = jnp.transpose(n)[0:1, :]
+
     def own_norm(c, _):
-        r = pl.ds(pl.multiple_of(c * CHUNK, CHUNK), CHUNK)
-        x = X[OWN, r, :].astype(F32)
-        n = jnp.broadcast_to(0.5 * jnp.sum(x * x, axis=1, keepdims=True), (CHUNK, 128))
-        NA[OWN, r, :] = n
-        NB[OWN, :, cols_of(c)] = jnp.transpose(n)[0:1, :]
+        norm_of(OWN, c)
         return 0
 
     with jax.named_scope("own_norm"):
@@ -220,7 +225,7 @@
             NA[s, r, :] = jnp.transpose(jnp.broadcast_to(NB[s, :, cols_of(c)], (128, CHUNK)))
             return 0
 
-        lax.fori_loop(0, N_CHUNK, one, 0)
+        lax.fori_loop(4, N_CHUNK, one, 0)
 
     def gram(tile):
         s, a, t, b, _ = tile
@@ -302,7 +307,7 @@
 
     with jax.named_scope("left_norm"):
         remote(VT.at[1:3], VT.at[1:3], sv_sem, rv_sem.at[0], tx).wait_recv()
-        remote(NB.at[1:3], NB.at[1:3], sn_sem, rn_sem.at[0], tx).wait_recv()
+        remote(NB.at[1:3, :, tail_cols], NB.at[1:3, :, tail_cols], sn_sem.at[0], rn_sem.at[0], tx).wait_recv()
         for j in range(2):
             left_norm(1 + j)
 
@@ -312,6 +317,8 @@
             @pl.when(i < 4)
             def _():
                 wait_x(i, False)
+                for s in range(1, 3):
+                    norm_of(s, i)
 
             @pl.when(i >= 4)
             def _():
@@ -565,7 +572,9 @@
         p_copy.wait_send()
         for j in range(2):
             remote(x_hbm, X.at[1 + j], sx_sem.at[j], rx_sem.at[0], tx).wait_send()
-        for buf, sem in ((VT, sv_sem), (NB, sn_sem), (YV, sy_sem)):
+        remote(NB.at[1:3, :, tail_cols], NB.at[1:3, :, tail_cols], sn_sem.at[0], rx_sem.at[0], tx).wait_send()
+        n_copies[2].wait_send()
+        for buf, sem in ((VT, sv_sem), (YV, sy_sem)):
             remote(buf.at[1:4], buf.at[1:4], sem, rx_sem.at[0], tx).wait_send()
         remote(SB, RB, s1_sem, rx_sem.at[0], tx).wait_send()
 
@@ -612,7 +621,7 @@
                 pltpu.VMEM((2, HALF_ROWS, CHUNK), BF16),
                 pltpu.VMEM((STEP_ROWS, CHUNK), BF16),
                 pltpu.VMEM((4, 2 * STEP_ROWS, CHUNK), BF16),
-                dma((2,)), dma((8,)), dma, dma((2,)), dma, dma((2,)), dma, dma,
+                dma((2,)), dma((8,)), dma, dma((2,)), dma((2,)), dma((2,)), dma, dma,
                 dma((2,)), dma((2, 2)), dma((4,)), dma((4,)),
                 dma, dma((N_CHUNK,)), dma, dma((N_CHUNK,)), dma((3,)), dma, dma,
             ],

time: 148 us -> 148 us (level)
  no operation moved by 1% of the time
where the time goes in v14:
time: 148 us
  Pallas kernels  146 us (99%)
    pallas_call x1, Pallas kernels, local_program(): pl.pallas_call(body, out_shape=(pltpu.VMEM((32, ROWS), F32), pltpu.VMEM((...  146 us

profile of v14, /device:TPU:0, one launch (start us, length us, event | category | flops | bytes accessed | tf_op | source)
XLA Modules:
  0.0 148.1 jit_solution(14440380831241163881)
XLA Ops:
  1.3 146.0 %products.1 = (f32[32,3072]{1,0:T(8,128)S(1)}, f32[3,32,3072]{2,1,0:T(8,128)S(1)}, bf16[76800,512]{1,0:T(8,128)(2,1)}) custom-call(bf16[3072,768]{1,0:T(8,128)(2,1)} %x_hbm.1, bf16[32,3072]{1,0:T(8,128)(2,1)} %bitcast.15, f32[1]{0:T(128)S(6)} %copy.5.ell_ref, f32[1]{0:T(128)S(6)} %copy.6.amp_ref), custom_call_target="tpu_custom_call" | custom-call | tf_op jit(solution)/shard_map/products/pallas_call | solution.py:599
  147.3 0.8 fusion

commit v15 on v14

--- a/solution.py
+++ b/solution.py
@@ -161,7 +161,7 @@
 
     p_copy = remote(x_hbm, X.at[PAR], sp_sem, rp_sem, pt)
     v_copies = [remote(v_hbm, VT.at[1 + j], sv_sem, rv_sem.at[j // 2], d) for j, d in enumerate((tx, ty, pt))]
-    tail_cols = pl.ds(4 * CHUNK, 2 * CHUNK)
+    tail_cols = pl.ds(5 * CHUNK, CHUNK)
     n_copies = [remote(NB.at[OWN, :, tail_cols], NB.at[1 + j, :, tail_cols], sn_sem.at[0], rn_sem.at[0], d) for j, d in enumerate((tx, ty))]
     n_copies.append(remote(NB.at[OWN], NB.at[PAR], sn_sem.at[1], rn_sem.at[1], pt))
 
@@ -199,12 +199,12 @@
     with jax.named_scope("x_local"):
         x_loc.wait()
 
-    def norm_of(s, c):
-        r = pl.ds(pl.multiple_of(c * CHUNK, CHUNK), CHUNK)
+    def norm_of(s, i, size=CHUNK):
+        r = pl.ds(pl.multiple_of(i * size, size), size)
         x = X[s, r, :].astype(F32)
-        n = jnp.broadcast_to(0.5 * jnp.sum(x * x, axis=1, keepdims=True), (CHUNK, 128))
+        n = jnp.broadcast_to(0.5 * jnp.sum(x * x, axis=1, keepdims=True), (size, 128))
         NA[s, r, :] = n
-        NB[s, :, cols_of(c)] = jnp.transpose(n)[0:1, :]
+        NB[s, :, r] = jnp.transpose(n)[0:1, :]
 
     def own_norm(c, _):
         norm_of(OWN, c)
@@ -225,7 +225,7 @@
             NA[s, r, :] = jnp.transpose(jnp.broadcast_to(NB[s, :, cols_of(c)], (128, CHUNK)))
             return 0
 
-        lax.fori_loop(4, N_CHUNK, one, 0)
+        lax.fori_loop(5, N_CHUNK, one, 0)
 
     def gram(tile):
         s, a, t, b, _ = tile
@@ -323,6 +323,11 @@
             @pl.when(i >= 4)
             def _():
                 wait_x(i, True)
+
+            @pl.when(jnp.logical_or(i == 4, i == 5))
+            def _():
+                for s in range(1, 3):
+                    norm_of(s, i + 4, STRIP)
 
         with jax.named_scope("strip"):
             state = lax.fori_loop(table(REMOTE_AT, i), table(REMOTE_AT, i + 1), remote_step, state)

time: 148 us -> 148 us (level)
  no operation moved by 1% of the time
where the time goes in v15:
time: 148 us
  Pallas kernels  146 us (99%)
    pallas_call x1, Pallas kernels, local_program(): pl.pallas_call(body, out_shape=(pltpu.VMEM((32, ROWS), F32), pltpu.VMEM((...  146 us

profile of v15, /device:TPU:0, one launch (start us, length us, event | category | flops | bytes accessed | tf_op | source)
XLA Modules:
  0.0 148.1 jit_solution(3963531751036709662)
XLA Ops:
  1.3 146.0 %products.1 = (f32[32,3072]{1,0:T(8,128)S(1)}, f32[3,32,3072]{2,1,0:T(8,128)S(1)}, bf16[76800,512]{1,0:T(8,128)(2,1)}) custom-call(bf16[3072,768]{1,0:T(8,128)(2,1)} %x_hbm.1, bf16[32,3072]{1,0:T(8,128)(2,1)} %bitcast.15, f32[1]{0:T(128)S(6)} %copy.5.ell_ref, f32[1]{0:T(128)S(6)} %copy.6.amp_ref), custom_call_target="tpu_custom_call" | custom-call | tf_op jit(solution)/shard_map/products/pallas_call | solution.py:604
  147.3 0.8 fusion
